TPU v7x, 256 devices: a whole 4x4x8 slice. The times are simulated.
256 devices in a mesh: bank: 32 (over y, z), grp: 8 (over x, core).
Axes of the slice: x: 4, y: 4, z: 8, core: 2. Of those that a mesh axis runs over, the one named last changes fastest.
Arguments:
- users: bfloat16 [32768, 256], P(('bank', 'grp')), may hold values from -32 to 32
- bank: bfloat16 [16384, 256], P('bank'), may hold values from -3 to 3
- positives: int32 [32768], P(('bank', 'grp')), may hold values from 0 to 16383
- cohorts: int32 [32768], P(('bank', 'grp')), may hold values from 0 to 15
Outputs:
- loss: float32 [], replicated
- user_grad: float32 [32768, 256], P(('bank', 'grp'))
- bank_grad: float32 [16384, 256], P(('bank', 'grp'))
All inputs are finite; a program needn't handle non-finite values.
Results may differ from a plain program's by a relative error of at most 0.014.
Values may be sent and summed in bfloat16 or wider, within the bound.
No kernel may reach another device: no remote copies, remote signals or barrier semaphores. Data moves between devices by JAX's collectives and lax.ppermute only.
A program may use at most 64 MiB of HBM per device.

v0:
```python
import functools

import jax
import jax.numpy as jnp
from jax import lax
from jax.sharding import Mesh
from jax.sharding import PartitionSpec as P

NCOH = 16
BANK = ("bank_0", "bank_1")
GRP = ("grp_0", "grp_1")
BANK_GRP = ("bank_0", "bank_1", "grp_0", "grp_1")


def over_axes(value, axes):
    return functools.reduce(lax.psum, axes, value)


def copy_for_each(value, axis):
    copies = jnp.broadcast_to(value, (lax.axis_size(axis), *value.shape))
    return lax.all_to_all(copies, axis, split_axis=0, concat_axis=0, tiled=True)


def in_order(pieces, dim):
    pieces = jnp.moveaxis(pieces, 0, dim)
    lengths = pieces.shape
    return pieces.reshape(*lengths[:dim], lengths[dim] * lengths[dim + 1], *lengths[dim + 2 :])


def gather_directly(value, axis, dim):
    pieces = copy_for_each(value, axis)
    return in_order(pieces, dim)


def all_in_one(value, axis):
    leaves = jax.tree.leaves(value)
    turns = sorted(range(len(leaves)), key=lambda k: -leaves[k].size)
    width = (1, *leaves[turns[0]].shape)[-1]
    lines = [
        jnp.pad(leaves[k].reshape(-1), (0, -leaves[k].size % width)).reshape(-1, width)
        for k in turns
    ]
    both, at, found = (copy_for_each(jnp.concatenate(lines), axis), 0, {})
    for k, line in zip(turns, lines):
        section = both[:, at : at + len(line)].reshape(len(both), -1)
        found[k] = section[:, : leaves[k].size].reshape(-1, *leaves[k].shape)
        at += len(line)
    numbers = iter(range(len(leaves)))
    return jax.tree.map(lambda _: found[next(numbers)], value)


def joined_by_halves(pieces, combine):
    while len(jax.tree.leaves(pieces)[0]) > 1:
        pieces = jax.vmap(combine)(
            *(jax.tree.map(lambda part: part[side::2], pieces) for side in (0, 1))
        )
    return jax.tree.map(lambda part: part[0], pieces)


def merged(value, axis, combine):
    pieces = all_in_one(value, axis)
    return joined_by_halves(pieces, combine)


def split_up(value, dim, size):
    before, after = (value.shape[:dim], value.shape[dim + 1 :])
    return jnp.moveaxis(value.reshape(*before, size, -1, *after), dim, 0)


def sent_and_summed(value, axis, dim):
    pieces = split_up(value, dim, lax.axis_size(axis))
    arrived = lax.all_to_all(pieces, axis, split_axis=0, concat_axis=0, tiled=True)
    return arrived.astype(jnp.float32).sum(axis=0)


def combine_stats(first, second):
    top = jnp.maximum(first[0], second[0])
    total = first[1] * jnp.exp(first[0] - top) + second[1] * jnp.exp(second[0] - top)
    return (top, total)


def make_dlogits(upart, local_pos, weight, lse, bank):
    logits = jnp.dot(upart, bank.T, preferred_element_type=jnp.float32)
    item_ids = jnp.arange(bank.shape[0], dtype=jnp.int32)
    hot = (item_ids[None, :] == local_pos[:, None]).astype(jnp.float32)
    prob = jnp.exp(logits - lse[:, None])
    return (weight[:, None] * (prob - hot)).astype(jnp.bfloat16)


def per_device(users, bank, positives, cohorts):
    per_dev = users.shape[0]
    items_here = bank.shape[0]
    bank_size = lax.axis_size(BANK)
    total_users = per_dev * bank_size * lax.axis_size(GRP)
    cohort_ids = jnp.arange(NCOH, dtype=jnp.int32)
    local_counts = jnp.sum((cohorts[:, None] == cohort_ids[None, :]).astype(jnp.float32), axis=0)
    counts = over_axes(local_counts, BANK_GRP)
    gathered, gpos, gcoh = (
        gather_directly(users, BANK, 0),
        gather_directly(positives, BANK, 0),
        gather_directly(cohorts, BANK, 0),
    )
    rows = gathered.shape[0]
    own = jnp.sum(
        jnp.where(gcoh[:, None] == cohort_ids[None, :], counts[None, :], jnp.float32(0.0)), axis=1
    )
    weight = jnp.float32(total_users) / NCOH / own
    local_pos = gpos - lax.axis_index(BANK) * items_here
    block = 512
    count = rows // block
    ublocks = gathered.reshape(count, block, gathered.shape[1])
    pblocks = local_pos.reshape(count, block)
    item_ids = jnp.arange(items_here, dtype=jnp.int32)

    def forward(carry, parts):
        upart, ppart = parts
        logits = jnp.dot(upart, bank.T, preferred_element_type=jnp.float32)
        top = jnp.max(logits, axis=1)
        total = jnp.sum(jnp.exp(logits - top[:, None]), axis=1)
        pos_logit = jnp.sum(
            jnp.where(item_ids[None, :] == ppart[:, None], logits, jnp.float32(0.0)), axis=1
        )
        return (carry, (top, total, pos_logit))

    _, (top_loc, sum_loc, pos_loc) = lax.scan(forward, 0, (ublocks, pblocks))
    top_loc = top_loc.reshape(rows)
    sum_loc = sum_loc.reshape(rows)
    pos_loc = pos_loc.reshape(rows)
    top_all, sum_all = merged((top_loc, sum_loc), BANK, combine_stats)
    lse = top_all + jnp.log(sum_all)
    loss_part = jnp.sum(weight * lse) / jnp.float32(bank_size) - jnp.sum(weight * pos_loc)
    loss = over_axes(loss_part, BANK_GRP) / jnp.float32(total_users)
    wblocks = weight.reshape(count, block)
    lblocks = lse.reshape(count, block)
    empty = jnp.zeros((items_here, gathered.shape[1]), jnp.float32)
    upart = gathered
    ppart = local_pos
    wpart = weight
    lpart = lse
    dlogits = make_dlogits(upart, ppart, wpart, lpart, bank)
    user_grad = sent_and_summed(
        jnp.dot(dlogits, bank, preferred_element_type=jnp.float32).astype(jnp.bfloat16), BANK, 0
    )

    def backward(bacc, parts):
        upart, ppart, wpart, lpart = parts
        dlogits = make_dlogits(upart, ppart, wpart, lpart, bank)
        bacc = bacc + lax.dot_general(
            dlogits, upart, (((0,), (0,)), ((), ())), preferred_element_type=jnp.float32
        )
        return (bacc, 0)

    bank_part, _ = lax.scan(backward, empty, (ublocks, pblocks, wblocks, lblocks))
    bank_grad = sent_and_summed(bank_part.astype(jnp.bfloat16), GRP, 0)
    return (loss, user_grad, bank_grad)


def solution(mesh):
    torus = Mesh(mesh.devices.reshape(4, 8, 4, 2), ("bank_0", "bank_1", "grp_0", "grp_1"))
    return jax.shard_map(
        per_device,
        mesh=torus,
        in_specs=(P(BANK_GRP, None), P(BANK, None), P(BANK_GRP), P(BANK_GRP)),
        out_specs=(P(), P(BANK_GRP, None), P(BANK_GRP, None)),
        check_vma=False,
    )
```

profile of v0, /device:TPU:2, one launch (start us, length us, event | category | flops | bytes accessed | tf_op | source)
XLA Modules:
  0.0 271.2 jit_solution(16516447025549730609)
XLA Ops:
  1.3 21.1 %all_to_all.32 = s32[32,1,128]{2,1,0:T(1,128)S(1)} all-to-all(s32[32,1,128]{2,1,0:T(1,128)S(1)} %broadcast_in_dim.60), channel_id=1, replica_groups=mesh['bank_0'=4,'bank_1'=8,'grp_0'=4,'grp_1'=2] {'bank_0','bank_1'}, dimensions={0} | all-to-all | bytes 32768 | tf_op jit(solution)/shard_map/all_to_all | solution.py:21
  22.4 2.4 broadcast_in_dim.59
  24.8 4.1 %all-to-all-start.1 = ((bf16[32,128,256]{2,1,0:T(8,128)(2,1)}), bf16[32,128,256]{2,1,0:T(8,128)(2,1)S(1)}, u32[]{:S(2)}, u32[]{:S(2)}) async-start(bf16[32,128,256]{2,1,0:T(8,128)(2,1)} %broadcast_in_dim.59), calls=%async_computation.1 | async-start | bytes 4194304 | tf_op jit(solution)/shard_map/all_to_all | solution.py:21
  30.8 47.3 %all-to-all-done.1 = bf16[32,128,256]{2,1,0:T(8,128)(2,1)S(1)} async-done(((bf16[32,128,256]{2,1,0:T(8,128)(2,1)}), bf16[32,128,256]{2,1,0:T(8,128)(2,1)S(1)}, u32[]{:S(2)}, u32[]{:S(2)}) %all-to-all-start.1) | async-done | bytes 2097184 | tf_op jit(solution)/shard_map/all_to_all | solution.py:21
  78.7 5.9 %all-to-all-start = ((s32[32,1,128]{2,1,0:T(1,128)}), s32[32,1,128]{2,1,0:T(1,128)S(1)}, u32[]{:S(2)}, u32[]{:S(2)}) async-start(s32[32,1,128]{2,1,0:T(1,128)} %broadcast_in_dim.56), calls=%async_computation | async-start | bytes 32768 | tf_op jit(solution)/shard_map/all_to_all | solution.py:21
  84.6 16.9 %while.26 = (s32[]{:T(128)}, f32[8,512]{1,0:T(8,128)S(1)}, f32[8,512]{1,0:T(8,128)S(1)}, f32[8,512]{1,0:T(8,128)}, bf16[8,512,256]{2,1,0:T(8,128)(2,1)S(1)}, /*i...) while((s32[]{:T(128)}, f32[8,512]{1,0:T(8,128)S(1)}, ...), condition=%wide.region_10.11_spmd.clone, body=%wide.region_6.10_spmd.clone.sunk | while | flops 135789056 | bytes 2648177 | solution.py:125
  89.5 1.3 dynamic_update_slice.18
  91.6 1.3 dynamic_update_slice.18
  101.7 1.5 broadcast_in_dim.61
  103.1 9.8 %all-to-all-start.3 = ((f32[32,2,4096]{2,1,0:T(2,128)}), f32[32,2,4096]{2,1,0:T(2,128)S(1)}, u32[]{:S(2)}, u32[]{:S(2)}) async-start(f32[32,2,4096]{2,1,0:T(2,128)} %broadcast_in_dim.61), calls=%async_computation.3 | async-start | bytes 2097152 | tf_op jit(solution)/shard_map/all_to_all | solution.py:21
  113.0 11.4 %psum.56 = f32[16]{0:T(128)S(1)} all-reduce(f32[16]{0:T(128)S(1)} %convert_reduce_fusion.2), channel_id=1, replica_groups=mesh['bank_0'=4,'bank_1'=8,'grp_0'=4,'grp_1'=2] {'bank_0'}, use_global_device_ids=true, to_apply=%region_1.0 | all-reduce | flops 16 | bytes 128 | tf_op jit(solution)/shard_map/psum | solution.py:16
  124.5 22.2 %psum.57 = f32[16]{0:T(128)S(1)} all-reduce(f32[16]{0:T(128)S(1)} %psum.56), channel_id=1, replica_groups=mesh['bank_0'=4,'bank_1'=8,'grp_0'=4,'grp_1'=2] {'bank_1'}, use_global_device_ids=true, to_apply=%region_2.0 | all-reduce | flops 16 | bytes 128 | tf_op jit(solution)/shard_map/psum | solution.py:16
  146.6 8.6 %psum.58 = f32[16]{0:T(128)S(1)} all-reduce(f32[16]{0:T(128)S(1)} %psum.57), channel_id=1, replica_groups=mesh['bank_0'=4,'bank_1'=8,'grp_0'=4,'grp_1'=2] {'grp_0'}, use_global_device_ids=true, to_apply=%region_3.0 | all-reduce | flops 16 | bytes 128 | tf_op jit(solution)/shard_map/psum | solution.py:16
  155.2 2.5 psum.59
  167.5 1.3 broadcast_divide_fusion
  168.8 7.3 %while.27 = (s32[]{:T(128)}, f32[512,256]{1,0:T(8,128)S(1)}, f32[8,512]{1,0:T(8,128)S(1)}, bf16[8,512,256]{2,1,0:T(8,128)(2,1)S(1)}, bf16[512,256]{1,0:T(8,128)(...) while((s32[]{:T(128)}, f32[512,256]{1,0:T(8,128)S(1)}, ...), condition=%wide.region_19.20_spmd.clone, body=%wide.region_18.19_spmd.clone.sunk | while | flops 270270464 | bytes 1854575 | solution.py:153
  177.0 5.8 %all-to-all-start.5 = ((bf16[8,64,256]{2,1,0:T(8,128)(2,1)}), bf16[8,64,256]{2,1,0:T(8,128)(2,1)S(1)}, u32[]{:S(2)}, u32[]{:S(2)}) async-start(bf16[8,64,256]{2,1,0:T(8,128)(2,1)} %bitcast.7), calls=%async_computation.5 | async-start | bytes 524288 | tf_op jit(solution)/shard_map/all_to_all | solution.py:72
  182.7 4.5 %convolution_convert_fusion = bf16[4096,256]{1,0:T(8,128)(2,1)} fusion(bf16[512,256]{1,0:T(8,128)(2,1)S(1)} %get-tuple-element.334, bf16[4096,256]{1,0:T(8,128)(2,1)S(1)} %bitcast.63, s32[4096]{0:T(1024)S(1)} %bitcast.77, f32[4096]{0:T(1024)S(1)} %bitcast.71, f32[4096]{0:T(1024)S(1)} %get-tuple-element.176), kind=kOutput, calls=%fused_computation.29 | convolution fusion | flops 2161115136 | bytes 4505600 | tf_op jit(solution)/shard_map/dot_general | solution.py:142
  187.2 1.6 all-to-all-done.5
  188.8 8.5 %all-to-all-start.4 = ((bf16[32,128,256]{2,1,0:T(8,128)(2,1)}), bf16[32,128,256]{2,1,0:T(8,128)(2,1)S(1)}, u32[]{:S(2)}, u32[]{:S(2)}) async-start(bf16[32,128,256]{2,1,0:T(8,128)(2,1)} %bitcast.64), calls=%async_computation.4 | async-start | bytes 4194304 | tf_op jit(solution)/shard_map/all_to_all | solution.py:72
  199.3 11.3 %psum.60 = f32[]{:T(128)} all-reduce(f32[]{:T(128)S(6)} %sub.95), channel_id=1, replica_groups=mesh['bank_0'=4,'bank_1'=8,'grp_0'=4,'grp_1'=2] {'bank_0'}, use_global_device_ids=true, to_apply=%region_13.14 | all-reduce | flops 1 | bytes 8 | tf_op jit(solution)/shard_map/psum | solution.py:16
  210.6 44.4 %psum.61 = f32[]{:T(128)} all-reduce(f32[]{:T(128)} %psum.60), channel_id=1, replica_groups=mesh['bank_0'=4,'bank_1'=8,'grp_0'=4,'grp_1'=2] {'bank_1'}, use_global_device_ids=true, to_apply=%region_14.15 | all-reduce | flops 1 | bytes 8 | tf_op jit(solution)/shard_map/psum | solution.py:16
  255.0 9.8 %psum.62 = f32[]{:T(128)} all-reduce(f32[]{:T(128)} %psum.61), channel_id=1, replica_groups=mesh['bank_0'=4,'bank_1'=8,'grp_0'=4,'grp_1'=2] {'grp_0'}, use_global_device_ids=true, to_apply=%region_15.16 | all-reduce | flops 1 | bytes 8 | tf_op jit(solution)/shard_map/psum | solution.py:16
  264.8 3.1 %psum.63 = f32[]{:T(128)} all-reduce(f32[]{:T(128)} %psum.62), channel_id=1, replica_groups=mesh['bank_0'=4,'bank_1'=8,'grp_0'=4,'grp_1'=2] {'grp_1'}, use_global_device_ids=true, to_apply=%region_16.17 | all-reduce | flops 1 | bytes 8 | tf_op jit(solution)/shard_map/psum | solution.py:16
  (127 shorter events, 36.8 us)
Async XLA Ops:
  24.8 53.3 %copy-start.4 = (s32[128]{0:T(128)S(1)}, s32[128]{0:T(128)}, u32[]{:S(2)}) copy-start(s32[128]{0:T(128)} %param.11) | copy-start | bytes 1540
  24.8 59.8 %copy-start = (bf16[512,256]{1,0:T(8,128)(2,1)S(1)}, bf16[512,256]{1,0:T(8,128)(2,1)}, u32[]{:S(2)}) copy-start(bf16[512,256]{1,0:T(8,128)(2,1)} %param.9) | copy-start | bytes 786436
  24.8 53.3 %all-to-all-start.1 = ((bf16[32,128,256]{2,1,0:T(8,128)(2,1)}), bf16[32,128,256]{2,1,0:T(8,128)(2,1)S(1)}, u32[]{:S(2)}, u32[]{:S(2)}) async-start(bf16[32,128,256]{2,1,0:T(8,128)(2,1)} %broadcast_in_dim.59), calls=%async_computation.1 | async-start | bytes 4194304 | tf_op jit(solution)/shard_map/all_to_all | solution.py:21
  78.7 22.9 %all-to-all-start = ((s32[32,1,128]{2,1,0:T(1,128)}), s32[32,1,128]{2,1,0:T(1,128)S(1)}, u32[]{:S(2)}, u32[]{:S(2)}) async-start(s32[32,1,128]{2,1,0:T(1,128)} %broadcast_in_dim.56), calls=%async_computation | async-start | bytes 32768 | tf_op jit(solution)/shard_map/all_to_all | solution.py:21
  103.1 55.3 %all-to-all-start.3 = ((f32[32,2,4096]{2,1,0:T(2,128)}), f32[32,2,4096]{2,1,0:T(2,128)S(1)}, u32[]{:S(2)}, u32[]{:S(2)}) async-start(f32[32,2,4096]{2,1,0:T(2,128)} %broadcast_in_dim.61), calls=%async_computation.3 | async-start | bytes 2097152 | tf_op jit(solution)/shard_map/all_to_all | solution.py:21
  163.2 5.7 %copy-start.1 = (f32[512,256]{1,0:T(8,128)S(1)}, f32[512,256]{1,0:T(8,128)}, u32[]{:S(2)}) copy-start(f32[512,256]{1,0:T(8,128)} %custom-call) | copy-start | bytes 1572868
  168.8 13.9 %copy-start.2 = (s32[32,1,128]{2,1,0:T(1,128)S(1)}, s32[32,1,128]{2,1,0:T(1,128)}, u32[]{:S(2)}) copy-start(s32[32,1,128]{2,1,0:T(1,128)} %get-tuple-element.169) | copy-start | bytes 49156
  177.0 11.9 %all-to-all-start.5 = ((bf16[8,64,256]{2,1,0:T(8,128)(2,1)}), bf16[8,64,256]{2,1,0:T(8,128)(2,1)S(1)}, u32[]{:S(2)}, u32[]{:S(2)}) async-start(bf16[8,64,256]{2,1,0:T(8,128)(2,1)} %bitcast.7), calls=%async_computation.5 | async-start | bytes 524288 | tf_op jit(solution)/shard_map/all_to_all | solution.py:72
  188.8 9.2 %copy-start.3 = (f32[8,512]{1,0:T(8,128)S(1)}, f32[8,512]{1,0:T(8,128)}, u32[]{:S(2)}) copy-start(f32[8,512]{1,0:T(8,128)} %get-tuple-element.86) | copy-start | bytes 49156
  188.8 80.3 %all-to-all-start.4 = ((bf16[32,128,256]{2,1,0:T(8,128)(2,1)}), bf16[32,128,256]{2,1,0:T(8,128)(2,1)S(1)}, u32[]{:S(2)}, u32[]{:S(2)}) async-start(bf16[32,128,256]{2,1,0:T(8,128)(2,1)} %bitcast.64), calls=%async_computation.4 | async-start | bytes 4194304 | tf_op jit(solution)/shard_map/all_to_all | solution.py:72
where the time goes:
time: 274 us; the launch traced here: 271 us
  blocking collectives  134 us (49%)
  waiting for transfers between devices  48.9 us (18%)
  starting transfers between devices  34.2 us (12%)
  local copies, waits for them, and re-layouts  23.4 us (9%)
  matrix products  14.1 us (5%)
  other arithmetic  11.7 us (4%)
  between operations  4.03 us (1%)
    psum x8, blocking collectives, over_axes(): return functools.reduce(lax.psum, axes, value)  113 us
    all_to_all x3, waiting for transfers between devices, copy_for_each(): return lax.all_to_all(copies, axis, split_axis=0, concat_axis=0, tiled=True)  47.3 us
    all_to_all x1, blocking collectives, copy_for_each(): return lax.all_to_all(copies, axis, split_axis=0, concat_axis=0, tiled=True)  21.1 us
    all_to_all x3, starting transfers between devices, copy_for_each(): return lax.all_to_all(copies, axis, split_axis=0, concat_axis=0, tiled=True)  19.8 us
    all_to_all x2, starting transfers between devices, sent_and_summed(): lax.all_to_all(pieces, axis, split_axis=0, concat_axis=0, tiled=True)  14.3 us
    dynamic_update_slice x24, local copies, waits for them, and re-layouts, per_device(): _, (top_loc, sum_loc, pos_loc) = lax.scan(forward, 0, (ublocks, pblocks))  11.4 us
    dot_general x8, matrix products, backward(): lax.dot_general(dlogits, upart, (((0,), (0,)), ((), ())), preferred_eleme...  6.85 us
  transfers between devices with their start and end apart: 5, of which 2 were waited for; matrix products, arithmetic and copies ran while one was open for 9% of the time, Pallas kernels for 0%

commit v1 on v0

v1 whole, which is shorter than its diff:
```python
import functools

import jax
import jax.numpy as jnp
from jax import lax
from jax.experimental import pallas as pl
from jax.experimental.pallas import tpu as pltpu
from jax.sharding import Mesh
from jax.sharding import PartitionSpec as P

NCOH = 16
PLANE = ("y", "x")
GROUP = ("c", "y", "x")
COLUMN = ("z", "x", "c")
ALL = ("y", "z", "x", "c")
SHIFT = (0, 4, 1, 5, 7, 3, 2, 6)
F32 = jnp.float32
BF16 = jnp.bfloat16
SHARDS = 4


def exchange(value, axis):
    return lax.all_to_all(value, axis, split_axis=0, concat_axis=0, tiled=True)


def copies(value, n):
    return jnp.broadcast_to(value[None], (n, *value.shape))


def scores(bank, users):
    return lax.dot_general(bank, users, (((1,), (1,)), ((), ())), preferred_element_type=F32)


def lanes(ref, row):
    return jnp.concatenate([ref[s, row : row + 1, :] for s in range(SHARDS)], axis=1)


def forward_kernel(half, users, bank, pos, count, stats_in, stats):
    del half, stats_in
    users = users[...].reshape(SHARDS * users.shape[1], users.shape[2])
    logits = scores(bank[...], users)
    top = jnp.max(logits, axis=0, keepdims=True)
    total = jnp.sum(jnp.exp(logits - top), axis=0, keepdims=True)
    items = lax.broadcasted_iota(jnp.int32, logits.shape, 0)
    own = jnp.sum(jnp.where(items == lanes(pos, 0), logits, F32(0)), axis=0, keepdims=True)
    for s in range(SHARDS):
        cut = slice(s * 128, (s + 1) * 128)
        stats[s, 0:1, :] = top[:, cut]
        stats[s, 1:2, :] = total[:, cut]
        stats[s, 2:3, :] = own[:, cut]
        stats[s, 3:4, :] = count[...]
        stats[s, 4:8, :] = jnp.zeros((4, 128), F32)


def forward(half, users, bank, pos, count, stats):
    shards, rows, width = users.shape
    steps = shards // SHARDS
    at_half = lambda i, h: (h[0] * steps + i, 0, 0)
    whole = lambda i, h: (0, 0)
    return pl.pallas_call(
        forward_kernel,
        grid_spec=pltpu.PrefetchScalarGridSpec(
            num_scalar_prefetch=1,
            grid=(steps,),
            in_specs=[
                pl.BlockSpec((SHARDS, rows, width), lambda i, h: (i, 0, 0)),
                pl.BlockSpec(bank.shape, whole),
                pl.BlockSpec((SHARDS, 1, rows), at_half),
                pl.BlockSpec(count.shape, whole),
                pl.BlockSpec(memory_space=pl.ANY),
            ],
            out_specs=pl.BlockSpec((SHARDS, 8, rows), at_half),
        ),
        out_shape=jax.ShapeDtypeStruct(stats.shape, stats.dtype),
        input_output_aliases={5: 0},
        name="forward",
    )(half, users, bank, pos, count, stats)


def combine_kernel(scale, stats, cohorts, out):
    top = jnp.max(stats[:, 0, :], axis=0, keepdims=True)
    total = jnp.sum(stats[:, 1, :] * jnp.exp(stats[:, 0, :] - top), axis=0, keepdims=True)
    own = jnp.sum(stats[:, 2, :], axis=0, keepdims=True)
    counts = jnp.sum(stats[:, 3, :], axis=0, keepdims=True)
    shape = (NCOH, counts.shape[1])
    row = lax.broadcasted_iota(jnp.int32, shape, 0)
    lane = lax.broadcasted_iota(jnp.int32, shape, 1)
    column = jnp.sum(jnp.where(row == lane, counts, F32(0)), axis=1, keepdims=True)
    mine = jnp.sum(jnp.where(row == cohorts[...], column, F32(0)), axis=0, keepdims=True)
    weight = scale / mine
    lse = top + jnp.log(total)
    loss = jnp.sum(weight * (lse - own), axis=1, keepdims=True)
    rows = lax.broadcasted_iota(jnp.int32, (8, lse.shape[1]), 0)
    tile = jnp.where(rows == 0, lse, jnp.where(rows == 1, weight, jnp.where(rows == 2, loss, F32(0))))
    out[...] = jnp.broadcast_to(tile[None], out.shape)


def backward_kernel(half, users, bank, bank_t, pos, sent, grad_in, user_part, bank_part, acc):
    del half
    step = pl.program_id(0)

    @pl.when(step == 0)
    def _():
        acc[...] = grad_in[...]

    users = users[...].reshape(SHARDS * users.shape[1], users.shape[2])
    logits = scores(bank[...], users)
    items = lax.broadcasted_iota(jnp.int32, logits.shape, 0)
    hot = jnp.where(items == lanes(pos, 0), F32(1), F32(0))
    prob = jnp.exp(logits - lanes(sent, 0))
    dlogits = (lanes(sent, 1) * (prob - hot)).astype(BF16)
    part = jnp.dot(bank_t[...], dlogits, preferred_element_type=F32).astype(BF16)
    for s in range(SHARDS):
        user_part[s] = part[:, s * 128 : (s + 1) * 128]
    acc[...] += jnp.dot(dlogits, users, preferred_element_type=F32)

    @pl.when(step == pl.num_programs(0) - 1)
    def _():
        bank_part[...] = acc[...].astype(bank_part.dtype)


def backward(half, users, bank, bank_t, pos, sent, grad_in, dtype):
    shards, rows, width = users.shape
    steps = shards // SHARDS
    at_half = lambda i, h: (h[0] * steps + i, 0, 0)
    whole = lambda i, h: (0, 0)
    return pl.pallas_call(
        backward_kernel,
        grid_spec=pltpu.PrefetchScalarGridSpec(
            num_scalar_prefetch=1,
            grid=(steps,),
            in_specs=[
                pl.BlockSpec((SHARDS, rows, width), lambda i, h: (i, 0, 0)),
                pl.BlockSpec(bank.shape, whole),
                pl.BlockSpec(bank_t.shape, whole),
                pl.BlockSpec((SHARDS, 1, rows), at_half),
                pl.BlockSpec((SHARDS, 8, rows), at_half),
                pl.BlockSpec(grad_in.shape, whole),
            ],
            out_specs=[
                pl.BlockSpec((SHARDS, width, rows), lambda i, h: (i, 0, 0)),
                pl.BlockSpec(bank.shape, whole),
            ],
            scratch_shapes=[pltpu.VMEM(bank.shape, F32)],
        ),
        out_shape=[
            jax.ShapeDtypeStruct((shards, width, rows), BF16),
            jax.ShapeDtypeStruct(bank.shape, dtype),
        ],
        name="backward",
    )(half, users, bank, bank_t, pos, sent, grad_in)


def finish_kernel(parts, out):
    total = parts[0].astype(F32)
    for k in range(1, parts.shape[0]):
        total = total + parts[k].astype(F32)
    out[...] = total.T


def per_device(users, bank, positives, cohorts):
    rows, width = users.shape
    items_here = bank.shape[0]
    ny, nz, nx, nc = (lax.axis_size(a) for a in ALL)
    plane, group = ny * nx, ny * nx * nc
    total_users = rows * ny * nz * nx * nc
    core = lax.axis_index("c")
    cross = [(k, 1 - k) for k in range(nc)]

    pairs = []
    for z in range(nz):
        for k in range(nx * nc):
            pairs.append((((z + SHIFT[k]) % nz) * nx * nc + k, z * nx * nc + k))
    back = [(b, a) for a, b in pairs]
    column = lax.axis_index("x") * nc + core
    shift = jnp.asarray(SHIFT, jnp.int32)[column]
    block = lax.axis_index("y") * nz + (lax.axis_index("z") + shift) % nz

    near = exchange(copies(users, plane), PLANE)
    pos = exchange(copies(positives[None], group), GROUP)
    item_block = lax.ppermute(bank, COLUMN, pairs)
    ids = jnp.arange(128, dtype=jnp.int32)
    count = jnp.sum((cohorts[:, None] == ids[None, :]).astype(F32), axis=0)
    count = jnp.sum(exchange(copies(count[None], nz), "z"), axis=0)
    pos = pos - block * items_here
    far = lax.ppermute(near, "c", cross)

    here = jnp.reshape(core, (1,)).astype(jnp.int32)
    there = 1 - here
    stats = jnp.zeros((group, 8, rows), F32)
    stats = forward(here, near, item_block, pos, count, stats)
    stats = forward(there, far, item_block, pos, count, stats)
    stats = exchange(stats, GROUP)
    sent = pl.pallas_call(
        functools.partial(combine_kernel, total_users / NCOH),
        out_shape=jax.ShapeDtypeStruct(stats.shape, F32),
        name="combine",
    )(stats, cohorts[None])
    sent = exchange(sent, GROUP)
    loss = jnp.sum(sent[:, 2, :1], axis=0, keepdims=True)
    loss = exchange(jnp.broadcast_to(loss[None], (nz, 1, 128)), "z")
    loss = jnp.sum(loss[:, 0, 0]) / F32(total_users)

    bank_t = item_block.T
    none = jnp.zeros(bank.shape, F32)
    far_part, bank_part = backward(there, far, item_block, bank_t, pos, sent, none, F32)
    far_part = lax.ppermute(far_part, "c", cross)
    near_part, bank_part = backward(here, near, item_block, bank_t, pos, sent, bank_part, BF16)
    user_part = (near_part.astype(F32) + far_part.astype(F32)).astype(BF16)
    user_part = exchange(user_part, PLANE)
    bank_part = lax.ppermute(bank_part, COLUMN, back)
    bank_part = exchange(bank_part.reshape(nx * nc, -1, width), ("x", "c"))
    bank_grad = jnp.sum(bank_part.astype(F32), axis=0)
    user_grad = pl.pallas_call(
        finish_kernel,
        out_shape=jax.ShapeDtypeStruct(users.shape, F32),
        name="finish",
    )(user_part)
    return loss, user_grad, bank_grad


def solution(mesh):
    torus = Mesh(mesh.devices.reshape(4, 8, 4, 2), ALL)
    return jax.shard_map(
        per_device,
        mesh=torus,
        in_specs=(P(ALL, None), P(("y", "z"), None), P(ALL), P(ALL)),
        out_specs=(P(), P(ALL, None), P(ALL, None)),
        check_vma=False,
    )
```

time: 274 us -> 161 us (0.59)
  blocking collectives: 134 us -> 72.1 us
  waiting for transfers between devices: 48.9 us -> 21.7 us
  Pallas kernels: 0 us -> 24 us
  local copies, waits for them, and re-layouts: 23.4 us -> 7.25 us
  matrix products: 14.1 us -> 0 us
  starting transfers between devices: 34.2 us -> 25.1 us
  other arithmetic: 11.7 us -> 6.59 us
    psum x8 -> x0, blocking collectives: 113 us -> none  [over_axes(): return functools.reduce(lax.psum, axes, value)]
    all_to_all x1 -> x5, blocking collectives: 21.1 us -> 72.1 us  [exchange(): return lax.all_to_all(value, axis, split_axis=0, concat_axis=0, tiled=True)]
    all_to_all x5 -> x3, waiting for transfers between devices: 48.9 us -> 21.7 us  [exchange(): return lax.all_to_all(value, axis, split_axis=0, concat_axis=0, tiled=True)]
    pallas_call x0 -> x6, Pallas kernels: none -> 24 us  [the longest x2 11.6 us: backward(): pl.pallas_call(backward_kernel, grid_spec=pltpu.PrefetchScalarGridSpec(nu...]
    all_to_all x5 -> x3, starting transfers between devices: 34.2 us -> 14.5 us  [exchange(): return lax.all_to_all(value, axis, split_axis=0, concat_axis=0, tiled=True)]
    dot_general x17 -> x0, matrix products: 14.1 us -> none  [the longest x8 6.85 us: backward(): lax.dot_general(dlogits, upart, (((0,), (0,)), ((), ())), preferred_eleme...]
    dynamic_update_slice x24 -> x0, local copies, waits for them, and re-layouts: 11.4 us -> none  [per_device(): _, (top_loc, sum_loc, pos_loc) = lax.scan(forward, 0, (ublocks, pblocks))]
    ppermute x0 -> x4, starting transfers between devices: none -> 10.6 us  [the longest x1 7.76 us: per_device(): item_block = lax.ppermute(bank, COLUMN, pairs)]
  transfers between devices with their start and end apart: 5 -> 7, of which waited for: 2 -> 3; matrix products, arithmetic and copies ran while one was open for 9% -> 6% of each run, Pallas kernels for 0% -> 6%
where the time goes in v1:
time: 161 us; the launch traced here: 160 us
  blocking collectives  72.1 us (45%)
  starting transfers between devices  25.1 us (16%)
  Pallas kernels  24 us (15%)
  waiting for transfers between devices  21.7 us (13%)
  local copies, waits for them, and re-layouts  7.25 us (5%)
  other arithmetic  6.59 us (4%)
  between operations  3.23 us (2%)
    all_to_all x5, blocking collectives, exchange(): return lax.all_to_all(value, axis, split_axis=0, concat_axis=0, tiled=True)  72.1 us
    all_to_all x3, waiting for transfers between devices, exchange(): return lax.all_to_all(value, axis, split_axis=0, concat_axis=0, tiled=True)  21.7 us
    all_to_all x3, starting transfers between devices, exchange(): return lax.all_to_all(value, axis, split_axis=0, concat_axis=0, tiled=True)  14.5 us
    pallas_call x2, Pallas kernels, backward(): pl.pallas_call(backward_kernel, grid_spec=pltpu.PrefetchScalarGridSpec(nu...  11.6 us
    pallas_call x2, Pallas kernels, forward(): pl.pallas_call(forward_kernel, grid_spec=pltpu.PrefetchScalarGridSpec(num...  8.6 us
    ppermute x1, starting transfers between devices, per_device(): item_block = lax.ppermute(bank, COLUMN, pairs)  7.76 us
  transfers between devices with their start and end apart: 7, of which 3 were waited for; matrix products, arithmetic and copies ran while one was open for 6% of the time, Pallas kernels for 6%

profile of v1, /device:TPU:2, one launch (start us, length us, event | category | flops | bytes accessed | tf_op | source)
XLA Modules:
  0.0 160.0 jit_solution(13937720929414374477)
XLA Ops:
  0.6 0.9 broadcast_in_dim.14
  1.6 23.2 %all_to_all.40.users = bf16[16,128,256]{2,1,0:T(8,128)(2,1)S(1)} all-to-all(bf16[16,128,256]{2,1,0:T(8,128)(2,1)S(1)} %broadcast_in_dim.14), channel_id=1, replica_groups=mesh['y'=4,'z'=8,'x'=4,'c'=2] {'y','x'}, dimensions={0} | all-to-all | bytes 2097152 | tf_op jit(solution)/shard_map/all_to_all | solution.py:23
  25.0 7.8 %collective-permute-start.1 = (bf16[512,256]{0,1:T(8,128)(2,1)S(1)}, bf16[512,256]{0,1:T(8,128)(2,1)S(1)}, u32[]{:S(2)}, u32[]{:S(2)}) collective-permute-start(bf16[512,256]{0,1:T(8,128)(2,1)S(1)} %copy.20), channel_id=1, source_target_pairs={{0,0},{33,1},{10,2},{43,3},{60,4},{29,5},{22,6},{55,7},{8,8},{41,9... | collective-permute-start | bytes 786440 | tf_op jit(solution)/shard_map/ppermute | solution.py:181
  32.9 11.2 %all_to_all.41 = f32[8,1,128]{2,1,0:T(1,128)S(1)} all-to-all(f32[8,1,128]{2,1,0:T(1,128)S(1)} %broadcast_in_dim.16), channel_id=1, replica_groups=mesh['y'=4,'z'=8,'x'=4,'c'=2] {'z'}, dimensions={0} | all-to-all | bytes 8192 | tf_op jit(solution)/shard_map/all_to_all | solution.py:23
  44.7 4.6 %all-to-all-start.1 = ((s32[32,1,128]{2,1,0:T(1,128)}), s32[32,1,128]{2,1,0:T(1,128)S(1)}, u32[]{:S(2)}, u32[]{:S(2)}) async-start(s32[32,1,128]{2,1,0:T(1,128)} %broadcast_in_dim.15), calls=%async_computation.1 | async-start | bytes 32768 | tf_op jit(solution)/shard_map/all_to_all | solution.py:23
  51.1 4.2 %all-to-all-done.1 = s32[32,1,128]{2,1,0:T(1,128)S(1)} async-done(((s32[32,1,128]{2,1,0:T(1,128)}), s32[32,1,128]{2,1,0:T(1,128)S(1)}, u32[]{:S(2)}, u32[]{:S(2)}) %all-to-all-start.1) | async-done | bytes 16416 | tf_op jit(solution)/shard_map/all_to_all | solution.py:23
  57.5 4.3 %forward.2.stats_in = f32[32,8,128]{2,1,0:T(8,128)} custom-call(s32[1]{0:T(128)} %bitcast.half, bf16[16,128,256]{2,1,0:T(8,128)(2,1)} %copy-done, bf16[512,256]{1,0:T(8,128)(2,1)} %copy.23.bank, s32[32,1,128]{2,1,0:T(1,128)} %bitcast.11, f32[1,128]{1,0:T(1,128)} %bitcast.17, f32[32,8,128]{2,1,0:T(8,128)} %broadcast_in_dim.17.stats_in), custom_call_target="tpu_custom_call", output_to_operand_aliasing={{}: (5, {})} | custom-call | tf_op jit(solution)/shard_map/forward/pallas_call | solution.py:60
  61.8 1.0 copy-done.1
  62.8 4.3 %forward.3 = f32[32,8,128]{2,1,0:T(8,128)} custom-call(s32[1]{0:T(128)S(6)} %sub.9.half, bf16[16,128,256]{2,1,0:T(8,128)(2,1)} %copy-done.1, bf16[512,256]{1,0:T(8,128)(2,1)} %copy.23.bank, s32[32,1,128]{2,1,0:T(1,128)} %bitcast.12, f32[1,128]{1,0:T(1,128)} %bitcast.18, f32[32,8,128]{2,1,0:T(8,128)} %forward.2.stats_in), custom_call_target="tpu_custom_call", output_to_operand_aliasing={{}: (5, {})} | custom-call | tf_op jit(solution)/shard_map/forward/pallas_call | solution.py:60
  67.1 12.4 %all_to_all.42.stats = f32[32,8,128]{2,1,0:T(8,128)} all-to-all(f32[32,8,128]{2,1,0:T(8,128)} %forward.3), channel_id=1, replica_groups=mesh['y'=4,'z'=8,'x'=4,'c'=2] {'c','y','x'}, dimensions={0} | all-to-all | bytes 262144 | tf_op jit(solution)/shard_map/all_to_all | solution.py:23
  79.4 1.8 %combine.1 = f32[32,8,128]{2,1,0:T(8,128)} custom-call(f32[32,8,128]{2,1,0:T(8,128)} %all_to_all.42.stats, s32[1,128]{1,0:T(1,128)} %bitcast.19), custom_call_target="tpu_custom_call" | custom-call | tf_op jit(solution)/shard_map/combine/pallas_call | solution.py:194
  81.2 12.4 %all_to_all.43.sent = f32[32,8,128]{2,1,0:T(8,128)} all-to-all(f32[32,8,128]{2,1,0:T(8,128)} %combine.1), channel_id=1, replica_groups=mesh['y'=4,'z'=8,'x'=4,'c'=2] {'c','y','x'}, dimensions={0} | all-to-all | bytes 262144 | tf_op jit(solution)/shard_map/all_to_all | solution.py:23
  94.4 5.8 %backward.2 = (bf16[16,256,128]{2,1,0:T(8,128)(2,1)}, f32[512,256]{1,0:T(8,128)}) custom-call(s32[1]{0:T(128)S(6)} %sub.9.half, bf16[16,128,256]{2,1,0:T(8,128)(2,1)} %copy-done.1, bf16[512,256]{1,0:T(8,128)(2,1)} %copy.23.bank, bf16[256,512]{1,0:T(8,128)(2,1)} %bitcast.9, s32[32,1,128]{2,1,0:T(1,128)} %bitcast.13, f32[32,8,128]{2,1,0:T(8,128)} %all_to_all.43.sent, ...), custom_call_target="tpu_custom_call" | custom-call | tf_op jit(solution)/shard_map/backward/pallas_call | solution.py:127
  100.2 5.8 %backward.3 = (bf16[16,256,128]{2,1,0:T(8,128)(2,1)}, bf16[512,256]{1,0:T(8,128)(2,1)}) custom-call(s32[1]{0:T(128)} %bitcast.half, bf16[16,128,256]{2,1,0:T(8,128)(2,1)} %copy-done, bf16[512,256]{1,0:T(8,128)(2,1)} %copy.23.bank, bf16[256,512]{1,0:T(8,128)(2,1)} %bitcast.10, s32[32,1,128]{2,1,0:T(1,128)} %bitcast.14, f32[32,8,128]{2,1,0:T(8,128)} %all_to_all.43.sent, ...), custom_call_target="tpu_custom_call" | custom-call | tf_op jit(solution)/shard_map/backward/pallas_call | solution.py:127
  106.0 2.9 %collective-permute-start.3 = (bf16[512,256]{1,0:T(8,128)(2,1)}, bf16[512,256]{1,0:T(8,128)(2,1)}, u32[]{:S(2)}, u32[]{:S(2)}) collective-permute-start(bf16[512,256]{1,0:T(8,128)(2,1)} %get-tuple-element.10), channel_id=1, source_target_pairs={{0,0},{1,33},{2,10},{3,43},{4,60},{5,29},{6,22},{7,55},{8,8},{9,41... | collective-permute-start | bytes 786440 | tf_op jit(solution)/shard_map/ppermute | solution.py:211
  108.9 1.5 slice_reduce_fusion
  111.1 13.0 %all_to_all.44 = f32[8,1,128]{2,1,0:T(1,128)S(1)} all-to-all(f32[8,1,128]{2,1,0:T(1,128)S(1)} %broadcast_in_dim.37), channel_id=1, replica_groups=mesh['y'=4,'z'=8,'x'=4,'c'=2] {'z'}, dimensions={0} | all-to-all | bytes 8192 | tf_op jit(solution)/shard_map/all_to_all | solution.py:23
  124.1 5.0 %all-to-all-start.7 = ((bf16[8,64,256]{2,1,0:T(8,128)(2,1)}), bf16[8,64,256]{2,1,0:T(8,128)(2,1)S(1)}, u32[]{:S(2)}, u32[]{:S(2)}) async-start(bf16[8,64,256]{2,1,0:T(8,128)(2,1)} %bitcast.6), calls=%async_computation.7 | async-start | bytes 524288 | tf_op jit(solution)/shard_map/all_to_all | solution.py:23
  129.1 2.5 %add_convert_fusion = bf16[16,256,128]{2,1,0:T(8,128)(2,1)} fusion(bf16[16,256,128]{2,1,0:T(8,128)(2,1)S(1)} %collective-permute-done.2, bf16[16,256,128]{2,1,0:T(8,128)(2,1)} %get-tuple-element.8), kind=kLoop, calls=%fused_computation | loop fusion | flops 2097152 | bytes 3145728 | tf_op jit(solution)/shard_map/convert_element_type | solution.py:209
  131.5 3.6 %all-to-all-done.7 = bf16[8,64,256]{2,1,0:T(8,128)(2,1)S(1)} async-done(((bf16[8,64,256]{2,1,0:T(8,128)(2,1)}), bf16[8,64,256]{2,1,0:T(8,128)(2,1)S(1)}, u32[]{:S(2)}, u32[]{:S(2)}) %all-to-all-start.7) | async-done | bytes 262176 | tf_op jit(solution)/shard_map/all_to_all | solution.py:23
  135.1 4.9 %all-to-all-start.6 = ((bf16[16,256,128]{2,1,0:T(8,128)(2,1)}), bf16[16,256,128]{2,1,0:T(8,128)(2,1)S(1)}, u32[]{:S(2)}, u32[]{:S(2)}) async-start(bf16[16,256,128]{2,1,0:T(8,128)(2,1)} %add_convert_fusion), calls=%async_computation.6 | async-start | bytes 2097152 | tf_op jit(solution)/shard_map/all_to_all | solution.py:23
  142.0 13.9 %all-to-all-done.6.parts = bf16[16,256,128]{2,1,0:T(8,128)(2,1)S(1)} async-done(((bf16[16,256,128]{2,1,0:T(8,128)(2,1)}), bf16[16,256,128]{2,1,0:T(8,128)(2,1)S(1)}, u32[]{:S(2)}, u32[]{:S(2)}) %all-to-all-start.6) | async-done | bytes 1048608 | tf_op jit(solution)/shard_map/all_to_all | solution.py:23
  155.8 1.0 copy-done.2
  156.8 2.1 %finish.1 = f32[128,256]{1,0:T(8,128)} custom-call(bf16[16,256,128]{2,1,0:T(8,128)(2,1)} %copy-done.2), custom_call_target="tpu_custom_call" | custom-call | tf_op jit(solution)/shard_map/finish/pallas_call | solution.py:214
  (33 shorter events, 6.9 us)
Async XLA Ops:
  1.6 23.2 %copy-start.4 = (bf16[512,256]{1,0:T(8,128)(2,1)S(1)}, bf16[512,256]{1,0:T(8,128)(2,1)}, u32[]{:S(2)}) copy-start(bf16[512,256]{1,0:T(8,128)(2,1)} %param.6) | copy-start | bytes 786436
  1.6 31.2 %copy-start.5 = (s32[128]{0:T(128)S(1)}, s32[128]{0:T(128)}, u32[]{:S(2)}) copy-start(s32[128]{0:T(128)} %param.8) | copy-start | bytes 1540
  1.6 42.5 %copy-start.6 = (s32[128]{0:T(128)S(1)}, s32[128]{0:T(128)}, u32[]{:S(2)}) copy-start(s32[128]{0:T(128)} %param.7) | copy-start | bytes 1540
  1.6 47.7 %copy-start.7 = (s32[8]{0:T(128)S(1)}, s32[8]{0:T(128)}, u32[]{:S(2)}) copy-start(s32[8]{0:T(128)} %constant.45.clone) | copy-start | bytes 100
  24.8 32.7 %copy-start = (bf16[16,128,256]{2,1,0:T(8,128)(2,1)}, bf16[16,128,256]{2,1,0:T(8,128)(2,1)S(1)}, u32[]{:S(2)}) copy-start(bf16[16,128,256]{2,1,0:T(8,128)(2,1)S(1)} %all_to_all.40.users) | copy-start | bytes 3145732
  24.8 37.0 %collective-permute-start = (bf16[16,128,256]{2,1,0:T(8,128)(2,1)S(1)}, bf16[16,128,256]{2,1,0:T(8,128)(2,1)S(1)}, u32[]{:S(2)}, u32[]{:S(2)}) collective-permute-start(bf16[16,128,256]{2,1,0:T(8,128)(2,1)S(1)} %all_to_all.40.users), channel_id=1, source_target_pairs={{0,1},{1,0},{2,3},{3,2},{4,5},{5,4},{6,7},{7,6},{8,9},{9,8},{10,11... | collective-permute-start | bytes 3145736 | tf_op jit(solution)/shard_map/ppermute | solution.py:186
  25.0 31.0 %collective-permute-start.1 = (bf16[512,256]{0,1:T(8,128)(2,1)S(1)}, bf16[512,256]{0,1:T(8,128)(2,1)S(1)}, u32[]{:S(2)}, u32[]{:S(2)}) collective-permute-start(bf16[512,256]{0,1:T(8,128)(2,1)S(1)} %copy.20), channel_id=1, source_target_pairs={{0,0},{33,1},{10,2},{43,3},{60,4},{29,5},{22,6},{55,7},{8,8},{41,9... | collective-permute-start | bytes 786440 | tf_op jit(solution)/shard_map/ppermute | solution.py:181
  44.7 10.7 %all-to-all-start.1 = ((s32[32,1,128]{2,1,0:T(1,128)}), s32[32,1,128]{2,1,0:T(1,128)S(1)}, u32[]{:S(2)}, u32[]{:S(2)}) async-start(s32[32,1,128]{2,1,0:T(1,128)} %broadcast_in_dim.15), calls=%async_computation.1 | async-start | bytes 32768 | tf_op jit(solution)/shard_map/all_to_all | solution.py:23
  56.0 5.8 %copy-start.3 = (bf16[512,256]{0,1:T(8,128)(2,1)}, bf16[512,256]{0,1:T(8,128)(2,1)S(1)}, u32[]{:S(2)}) copy-start(bf16[512,256]{0,1:T(8,128)(2,1)S(1)} %collective-permute-done.1) | copy-start | bytes 786436
  61.8 1.0 copy-start.1
  100.2 28.9 %collective-permute-start.2 = (bf16[16,256,128]{2,1,0:T(8,128)(2,1)}, bf16[16,256,128]{2,1,0:T(8,128)(2,1)S(1)}, u32[]{:S(2)}, u32[]{:S(2)}) collective-permute-start(bf16[16,256,128]{2,1,0:T(8,128)(2,1)} %get-tuple-element.9), channel_id=1, source_target_pairs={{0,1},{1,0},{2,3},{3,2},{4,5},{5,4},{6,7},{7,6},{8,9},{9,8},{10,11... | collective-permute-start | bytes 3145736 | tf_op jit(solution)/shard_map/ppermute | solution.py:207
  106.0 18.1 %collective-permute-start.3 = (bf16[512,256]{1,0:T(8,128)(2,1)}, bf16[512,256]{1,0:T(8,128)(2,1)}, u32[]{:S(2)}, u32[]{:S(2)}) collective-permute-start(bf16[512,256]{1,0:T(8,128)(2,1)} %get-tuple-element.10), channel_id=1, source_target_pairs={{0,0},{1,33},{2,10},{3,43},{4,60},{5,29},{6,22},{7,55},{8,8},{9,41... | collective-permute-start | bytes 786440 | tf_op jit(solution)/shard_map/ppermute | solution.py:211
  124.1 11.1 %all-to-all-start.7 = ((bf16[8,64,256]{2,1,0:T(8,128)(2,1)}), bf16[8,64,256]{2,1,0:T(8,128)(2,1)S(1)}, u32[]{:S(2)}, u32[]{:S(2)}) async-start(bf16[8,64,256]{2,1,0:T(8,128)(2,1)} %bitcast.6), calls=%async_computation.7 | async-start | bytes 524288 | tf_op jit(solution)/shard_map/all_to_all | solution.py:23
  135.1 20.7 %all-to-all-start.6 = ((bf16[16,256,128]{2,1,0:T(8,128)(2,1)}), bf16[16,256,128]{2,1,0:T(8,128)(2,1)S(1)}, u32[]{:S(2)}, u32[]{:S(2)}) async-start(bf16[16,256,128]{2,1,0:T(8,128)(2,1)} %add_convert_fusion), calls=%async_computation.6 | async-start | bytes 2097152 | tf_op jit(solution)/shard_map/all_to_all | solution.py:23
  155.8 1.0 copy-start.2

commit v2 on v1

v2 whole, which is shorter than its diff:
```python
import functools

import jax
import jax.numpy as jnp
from jax import lax
from jax.experimental import pallas as pl
from jax.experimental.pallas import tpu as pltpu
from jax.sharding import Mesh
from jax.sharding import PartitionSpec as P

NCOH = 16
PLANE = ("y", "x")
COLUMN = ("z", "x", "c")
ALL = ("y", "z", "x", "c")
SHIFT = (0, 4, 1, 5, 7, 3, 2, 6)
F32 = jnp.float32
BF16 = jnp.bfloat16
LANES = 128
RADIX = 128
STEP = 4
VMEM = pl.BlockSpec(memory_space=pltpu.VMEM)
SMEM = pl.BlockSpec(memory_space=pltpu.SMEM)


def exchange(value, axis):
    return lax.all_to_all(value, axis, split_axis=0, concat_axis=0, tiled=True)


def copies(value, n):
    return jnp.broadcast_to(value[None], (n, *value.shape))


def summed_along(value, axis):
    n = lax.axis_size(axis)
    total = value
    for by in range(1, n):
        total = total + lax.ppermute(value, axis, [(k, (k + by) % n) for k in range(n)])
    return total


def scores(bank, users):
    return lax.dot_general(bank, users, (((1,), (1,)), ((), ())), preferred_element_type=F32)


def iota(shape, dim):
    return lax.broadcasted_iota(jnp.int32, shape, dim)


def shard_users(packed, at, rows):
    return jnp.concatenate([packed[at + s, :rows, :] for s in range(STEP)], axis=0)


def shard_row(packed, at, row, half):
    cut = slice(half * LANES, (half + 1) * LANES)
    tiles = [packed[at + s, row : row + 8, cut].astype(F32)[0:1] for s in range(STEP)]
    return jnp.concatenate(tiles, axis=1)


def cohort_row(packed, at, rows, half):
    cut = slice(half * LANES, (half + 1) * LANES)
    tiles = [packed[at + s, rows : rows + 8, cut].astype(F32)[1:2] for s in range(STEP)]
    return jnp.concatenate(tiles, axis=1)


def local_positives(packed, at, rows, first):
    high = shard_row(packed, at, rows, 0)
    low = shard_row(packed, at, rows, 1)
    return (high * RADIX + low).astype(jnp.int32) - first


def column_to_row(column):
    shape = (NCOH, LANES)
    spread = jnp.where(iota(shape, 0) == iota(shape, 1), column, F32(0))
    return jnp.sum(spread, axis=0, keepdims=True)


def row_to_column(row):
    shape = (NCOH, LANES)
    spread = jnp.where(iota(shape, 0) == iota(shape, 1), row, F32(0))
    return jnp.sum(spread, axis=1, keepdims=True)


def forward_kernel(rows, first, packed, bank, stats, coh):
    shards = packed.shape[0]
    positive = jnp.zeros((NCOH, 1), F32)
    for at in range(0, shards, STEP):
        logits = scores(bank[...], shard_users(packed, at, rows))
        top = jnp.max(logits, axis=0, keepdims=True)
        total = jnp.sum(jnp.exp(logits - top), axis=0, keepdims=True)
        pos = local_positives(packed, at, rows, first[0])
        own = jnp.sum(jnp.where(iota(logits.shape, 0) == pos, logits, F32(0)), axis=0, keepdims=True)
        lse = top + jnp.log(total)
        mine = cohort_row(packed, at, rows, 0)
        ids = iota((NCOH, mine.shape[1]), 0).astype(F32)
        positive += jnp.sum(jnp.where(ids == mine, own, F32(0)), axis=1, keepdims=True)
        for s in range(STEP):
            cut = slice(s * LANES, (s + 1) * LANES)
            stats[at + s : at + s + 1, :] = lse[:, cut]
            coh[at + s : at + s + 1, :] = mine[:, cut]
    stats[shards : shards + 8, :] = jnp.broadcast_to(column_to_row(positive), (8, LANES))


def forward(packed, bank, first, rows):
    shards = packed.shape[0]
    return pl.pallas_call(
        functools.partial(forward_kernel, rows),
        in_specs=[SMEM, VMEM, VMEM],
        out_specs=[VMEM, VMEM],
        out_shape=[
            jax.ShapeDtypeStruct((shards + 8, LANES), F32),
            jax.ShapeDtypeStruct((shards, LANES), F32),
        ],
        name="forward",
    )(first, packed, bank)


def join_kernel(near, far, other_near, other_far, count, other_count, out):
    shards = near.shape[0] - 8

    def join(a, b):
        top = jnp.maximum(a, b)
        return top + jnp.log(jnp.exp(a - top) + jnp.exp(b - top))

    first = join(near[:shards], other_far[:shards])
    second = join(far[:shards], other_near[:shards])
    positive = near[shards:] + far[shards:] + other_near[shards:] + other_far[shards:]
    counts = count[...] + other_count[...]
    for k in range(out.shape[0]):
        out[k, :shards] = first
        out[k, shards : 2 * shards] = second
        out[k, 2 * shards : 2 * shards + 8] = positive
        out[k, 2 * shards + 8 :] = counts


def settle_kernel(scale, stats, coh_near, coh_far, lse_out, weight_out, loss_out):
    shards = coh_near.shape[0]
    both = 2 * shards
    top = stats[0, :both]
    for k in range(1, stats.shape[0]):
        top = jnp.maximum(top, stats[k, :both])
    total = jnp.exp(stats[0, :both] - top)
    rest = stats[0, both:]
    for k in range(1, stats.shape[0]):
        total += jnp.exp(stats[k, :both] - top)
        rest += stats[k, both:]
    lse = top + jnp.log(total)
    lse_out[...] = lse
    per_cohort = scale / row_to_column(rest[8:9])
    weight_out[...] = jnp.broadcast_to(per_cohort, weight_out.shape)
    weights = jnp.zeros((both, LANES), F32)
    cohorts = jnp.concatenate([coh_near[...], coh_far[...]], axis=0)
    for c in range(NCOH):
        weights = jnp.where(cohorts == F32(c), per_cohort[c : c + 1, :], weights)
    loss = jnp.sum(weights * lse, keepdims=True)
    loss -= jnp.sum(per_cohort * row_to_column(rest[0:1]), keepdims=True)
    loss_out[...] = jnp.broadcast_to(loss, loss_out.shape)


def backward_kernel(rows, half, first, packed, bank, lse, weight, grad_in, user_part, bank_part):
    shards = packed.shape[0]
    total = grad_in[...]
    bank_t = bank[...].T
    for at in range(0, shards, STEP):
        users = shard_users(packed, at, rows)
        logits = scores(bank[...], users)
        pos = local_positives(packed, at, rows, first[0])
        mine = cohort_row(packed, at, rows, 0)
        ids = iota((NCOH, mine.shape[1]), 0).astype(F32)
        weights = jnp.sum(jnp.where(ids == mine, weight[:, 0:1], F32(0)), axis=0, keepdims=True)
        line = half * shards + at
        level = jnp.concatenate([lse[line + s : line + s + 1, :] for s in range(STEP)], axis=1)
        hot = jnp.where(iota(logits.shape, 0) == pos, F32(1), F32(0))
        dlogits = (weights * (jnp.exp(logits - level) - hot)).astype(BF16)
        part = jnp.dot(bank_t, dlogits, preferred_element_type=F32).astype(BF16)
        for s in range(STEP):
            user_part[at + s] = part[:, s * LANES : (s + 1) * LANES]
        total = total + jnp.dot(dlogits, users, preferred_element_type=F32)
    bank_part[...] = total.astype(bank_part.dtype)


def backward(half, packed, bank, first, lse, weight, grad_in, rows, dtype):
    shards, _, width = packed.shape
    return pl.pallas_call(
        functools.partial(backward_kernel, rows, half),
        in_specs=[SMEM] + [VMEM] * 5,
        out_specs=[VMEM, VMEM],
        out_shape=[
            jax.ShapeDtypeStruct((shards, width, rows), BF16),
            jax.ShapeDtypeStruct(bank.shape, dtype),
        ],
        name="backward",
    )(first, packed, bank, lse, weight, grad_in)


def finish_kernel(parts, out):
    total = parts[0].astype(F32)
    for k in range(1, parts.shape[0]):
        total = total + parts[k].astype(F32)
    out[...] = total.T


def per_device(users, bank, positives, cohorts):
    rows, width = users.shape
    ny, nz, nx, nc = (lax.axis_size(a) for a in ALL)
    plane = ny * nx
    total_users = rows * plane * nz * nc
    cross = [(k, 1 - k) for k in range(nc)]

    pairs = []
    for z in range(nz):
        for k in range(nx * nc):
            pairs.append((((z + SHIFT[k]) % nz) * nx * nc + k, z * nx * nc + k))
    back = [(b, a) for a, b in pairs]
    column = lax.axis_index("x") * nc + lax.axis_index("c")
    shift = sum(jnp.where(column == k, SHIFT[k], 0) for k in range(nx * nc))
    block = lax.axis_index("y") * nz + (lax.axis_index("z") + shift) % nz
    first = jnp.reshape(block * bank.shape[0], (1,)).astype(jnp.int32)

    digits = jnp.concatenate([positives // RADIX, positives % RADIX])[None]
    labels = jnp.concatenate([cohorts, jnp.zeros_like(cohorts)])[None]
    extra = jnp.concatenate([digits, labels, jnp.zeros((14, width), jnp.int32)]).astype(BF16)
    packed = jnp.concatenate([users, extra])
    near = exchange(copies(packed, plane), PLANE)
    item_block = lax.ppermute(bank, COLUMN, pairs)
    ids = jnp.arange(LANES, dtype=jnp.int32)
    count = jnp.sum((cohorts[:, None] == ids[None, :]).astype(F32), axis=0)
    count = summed_along(jnp.broadcast_to(count[None], (8, LANES)), "z")
    other_count = lax.ppermute(count, "c", cross)
    far = lax.ppermute(near, "c", cross)

    near_stats, near_coh = forward(near, item_block, first, rows)
    other_near = lax.ppermute(near_stats, "c", cross)
    far_stats, far_coh = forward(far, item_block, first, rows)
    other_far = lax.ppermute(far_stats, "c", cross)
    stats = pl.pallas_call(
        join_kernel,
        in_specs=[VMEM] * 6,
        out_specs=VMEM,
        out_shape=jax.ShapeDtypeStruct((plane, 2 * plane + 16, LANES), F32),
        name="join",
    )(near_stats, far_stats, other_near, other_far, count, other_count)
    stats = exchange(stats, PLANE)
    lse, weight, loss = pl.pallas_call(
        functools.partial(settle_kernel, total_users / NCOH),
        in_specs=[VMEM] * 3,
        out_specs=[VMEM] * 3,
        out_shape=[
            jax.ShapeDtypeStruct((2 * plane, LANES), F32),
            jax.ShapeDtypeStruct((NCOH, LANES), F32),
            jax.ShapeDtypeStruct((8, LANES), F32),
        ],
        name="settle",
    )(stats, near_coh, far_coh)
    loss = summed_along(loss, "z")[0, 0] / F32(total_users)

    none = jnp.zeros(bank.shape, F32)
    far_part, bank_part = backward(1, far, item_block, first, lse, weight, none, rows, F32)
    far_part = lax.ppermute(far_part, "c", cross)
    near_part, bank_part = backward(0, near, item_block, first, lse, weight, bank_part, rows, BF16)
    user_part = (near_part.astype(F32) + far_part.astype(F32)).astype(BF16)
    user_part = exchange(user_part, PLANE)
    bank_part = lax.ppermute(bank_part, COLUMN, back)
    bank_part = exchange(bank_part.reshape(nx * nc, -1, width), ("x", "c"))
    bank_grad = jnp.sum(bank_part.astype(F32), axis=0)
    user_grad = pl.pallas_call(
        finish_kernel,
        in_specs=[VMEM],
        out_specs=VMEM,
        out_shape=jax.ShapeDtypeStruct(users.shape, F32),
        name="finish",
    )(user_part)
    return loss, user_grad, bank_grad


def solution(mesh):
    torus = Mesh(mesh.devices.reshape(4, 8, 4, 2), ALL)
    return jax.shard_map(
        per_device,
        mesh=torus,
        in_specs=(P(ALL, None), P(("y", "z"), None), P(ALL), P(ALL)),
        out_specs=(P(), P(ALL, None), P(ALL, None)),
        check_vma=False,
    )
```

time: 161 us -> 145 us (0.901)
  blocking collectives: 72.1 us -> 43.3 us
  starting transfers between devices: 25.1 us -> 50.3 us
  waiting for transfers between devices: 21.7 us -> 16.5 us
  local copies, waits for them, and re-layouts: 7.25 us -> 3.75 us
    all_to_all x5 -> x2, blocking collectives: 72.1 us -> 43.3 us  [exchange(): return lax.all_to_all(value, axis, split_axis=0, concat_axis=0, tiled=True)]
    ppermute x0 -> x17, starting transfers between devices: none -> 26.5 us  [the longest x14 24.8 us: summed_along(): lax.ppermute(value, axis, [(k, (k + by) % n) for k in range(n)])]
    all_to_all x3 -> x2, waiting for transfers between devices: 21.7 us -> 3.57 us  [exchange(): return lax.all_to_all(value, axis, split_axis=0, concat_axis=0, tiled=True)]
    ppermute x1, waiting for transfers between devices: 0.01 us -> 7.5 us  [per_device(): bank_part = lax.ppermute(bank_part, COLUMN, back)]
    ppermute x0 -> x17, waiting for transfers between devices: none -> 5.46 us  [the longest x14 4.63 us: summed_along(): lax.ppermute(value, axis, [(k, (k + by) % n) for k in range(n)])]
    reduce_sum x3 -> x0, other arithmetic: 2.74 us -> none  [the longest x1 1.54 us: per_device(): loss = jnp.sum(sent[:, 2, :1], axis=0, keepdims=True)]
    pallas_call x6 -> x7, Pallas kernels: 24 us -> 22.4 us  [the longest x2 9.59 us: backward(): pl.pallas_call(functools.partial(backward_kernel, rows, half), in_specs=[...]
    all_to_all x3 -> x2, starting transfers between devices: 14.5 us -> 13.8 us  [exchange(): return lax.all_to_all(value, axis, split_axis=0, concat_axis=0, tiled=True)]
  transfers between devices with their start and end apart: 7 -> 23, of which waited for: 3 -> 6; matrix products, arithmetic and copies ran while one was open for 6% -> 3% of each run, Pallas kernels for 6% -> 8%
where the time goes in v2:
time: 145 us; the launch traced here: 144 us
  starting transfers between devices  50.3 us (35%)
  blocking collectives  43.3 us (30%)
  Pallas kernels  22.4 us (15%)
  waiting for transfers between devices  16.5 us (11%)
  other arithmetic  5.52 us (4%)
  local copies, waits for them, and re-layouts  3.75 us (3%)
  between operations  2.58 us (2%)
    all_to_all x2, blocking collectives, exchange(): return lax.all_to_all(value, axis, split_axis=0, concat_axis=0, tiled=True)  43.3 us
    ppermute x14, starting transfers between devices, summed_along(): lax.ppermute(value, axis, [(k, (k + by) % n) for k in range(n)])  24.8 us
    all_to_all x2, starting transfers between devices, exchange(): return lax.all_to_all(value, axis, split_axis=0, concat_axis=0, tiled=True)  13.8 us
    pallas_call x2, Pallas kernels, backward(): pl.pallas_call(functools.partial(backward_kernel, rows, half), in_specs=[...  9.59 us
    ppermute x1, starting transfers between devices, per_device(): item_block = lax.ppermute(bank, COLUMN, pairs)  7.76 us
    ppermute x1, waiting for transfers between devices, per_device(): bank_part = lax.ppermute(bank_part, COLUMN, back)  7.5 us
    pallas_call x2, Pallas kernels, forward(): pl.pallas_call(functools.partial(forward_kernel, rows), in_specs=[SMEM, V...  7.33 us
    ppermute x14, waiting for transfers between devices, summed_along(): lax.ppermute(value, axis, [(k, (k + by) % n) for k in range(n)])  4.63 us
  transfers between devices with their start and end apart: 23, of which 6 were waited for; matrix products, arithmetic and copies ran while one was open for 3% of the time, Pallas kernels for 8%

profile of v2, /device:TPU:2, one launch (start us, length us, event | category | flops | bytes accessed | tf_op | source)
XLA Modules:
  0.0 144.4 jit_solution(16797067348693225197)
XLA Ops:
  3.1 24.6 %all_to_all.20.packed = bf16[16,144,256]{2,1,0:T(8,128)(2,1)S(1)} all-to-all(bf16[16,144,256]{2,1,0:T(8,128)(2,1)S(1)} %broadcast_in_dim.32), channel_id=1, replica_groups=mesh['y'=4,'z'=8,'x'=4,'c'=2] {'y','x'}, dimensions={0} | all-to-all | bytes 2359296 | tf_op jit(solution)/shard_map/all_to_all | solution.py:26
  27.7 7.8 %collective-permute-start = (bf16[512,256]{1,0:T(8,128)(2,1)S(1)}, bf16[512,256]{1,0:T(8,128)(2,1)S(1)}, u32[]{:S(2)}, u32[]{:S(2)}) collective-permute-start(bf16[512,256]{1,0:T(8,128)(2,1)S(1)} %copy-done.10), channel_id=1, source_target_pairs={{0,0},{33,1},{10,2},{43,3},{60,4},{29,5},{22,6},{55,7},{8,8},{41,9... | collective-permute-start | bytes 786440 | tf_op jit(solution)/shard_map/ppermute | solution.py:224
  39.5 4.1 %collective-permute-start.7 = (f32[8,128]{1,0:T(8,128)S(1)}, f32[8,128]{1,0:T(8,128)S(1)}, u32[]{:S(2)}, u32[]{:S(2)}) collective-permute-start(f32[8,128]{1,0:T(8,128)S(1)} %broadcast_in_dim.33), channel_id=1, source_target_pairs={{0,32},{8,40},{16,48},{24,56},{32,0},{40,8},{48,16},{56,24},{1,33}... | collective-permute-start | bytes 12296 | tf_op jit(solution)/shard_map/ppermute | solution.py:37
  43.7 2.8 %collective-permute-start.6 = (f32[8,128]{1,0:T(8,128)S(1)}, f32[8,128]{1,0:T(8,128)S(1)}, u32[]{:S(2)}, u32[]{:S(2)}) collective-permute-start(f32[8,128]{1,0:T(8,128)S(1)} %broadcast_in_dim.33), channel_id=1, source_target_pairs={{0,24},{8,32},{16,40},{24,48},{32,56},{40,0},{48,8},{56,16},{1,25}... | collective-permute-start | bytes 12296 | tf_op jit(solution)/shard_map/ppermute | solution.py:37
  47.2 3.7 %forward.2 = (f32[24,128]{1,0:T(8,128)}, f32[16,128]{1,0:T(8,128)}) custom-call(s32[1]{0:T(128)} %bitcast.first, bf16[16,144,256]{2,1,0:T(8,128)(2,1)} %copy-done, bf16[512,256]{1,0:T(8,128)(2,1)} %copy-done.3), custom_call_target="tpu_custom_call" | custom-call | tf_op jit(solution)/shard_map/forward/pallas_call | solution.py:105
  50.8 3.7 %forward.3 = (f32[24,128]{1,0:T(8,128)}, f32[16,128]{1,0:T(8,128)}) custom-call(s32[1]{0:T(128)} %bitcast.first, bf16[16,144,256]{2,1,0:T(8,128)(2,1)} %copy-done.1, bf16[512,256]{1,0:T(8,128)(2,1)} %copy-done.3), custom_call_target="tpu_custom_call" | custom-call | tf_op jit(solution)/shard_map/forward/pallas_call | solution.py:105
  58.2 1.6 %join.1 = f32[16,48,128]{2,1,0:T(8,128)} custom-call(f32[24,128]{1,0:T(8,128)} %get-tuple-element.14.near, f32[24,128]{1,0:T(8,128)} %get-tuple-element.15.far, f32[24,128]{1,0:T(8,128)} %copy-done.6, f32[24,128]{1,0:T(8,128)} %copy-done.7, f32[8,128]{1,0:T(8,128)} %copy-done.4, f32[8,128]{1,0:T(8,128)} %copy-done.8), custom_call_target="tpu_custom_call" | custom-call | tf_op jit(solution)/shard_map/join/pallas_call | solution.py:235
  59.8 18.7 %all_to_all.21.stats = f32[16,48,128]{2,1,0:T(8,128)} all-to-all(f32[16,48,128]{2,1,0:T(8,128)} %join.1), channel_id=1, replica_groups=mesh['y'=4,'z'=8,'x'=4,'c'=2] {'y','x'}, dimensions={0} | all-to-all | bytes 786432 | tf_op jit(solution)/shard_map/all_to_all | solution.py:26
  78.5 1.8 %settle.1 = (f32[32,128]{1,0:T(8,128)}, f32[16,128]{1,0:T(8,128)}, f32[8,128]{1,0:T(8,128)}) custom-call(f32[16,48,128]{2,1,0:T(8,128)} %all_to_all.21.stats, f32[16,128]{1,0:T(8,128)} %get-tuple-element.16.coh_near, f32[16,128]{1,0:T(8,128)} %get-tuple-element.17.coh_far), custom_call_target="tpu_custom_call" | custom-call | tf_op jit(solution)/shard_map/settle/pallas_call | solution.py:243
  81.1 4.8 %backward.2 = (bf16[16,256,128]{2,1,0:T(8,128)(2,1)}, f32[512,256]{1,0:T(8,128)}) custom-call(s32[1]{0:T(128)} %bitcast.first, bf16[16,144,256]{2,1,0:T(8,128)(2,1)} %copy-done.1, bf16[512,256]{1,0:T(8,128)(2,1)} %copy-done.3, f32[32,128]{1,0:T(8,128)} %get-tuple-element.19.lse, f32[16,128]{1,0:T(8,128)} %get-tuple-element.20.weight, ...), custom_call_target="tpu_custom_call" | custom-call | tf_op jit(solution)/shard_map/backward/pallas_call | solution.py:183
  86.0 4.8 %backward.3 = (bf16[16,256,128]{2,1,0:T(8,128)(2,1)}, bf16[512,256]{1,0:T(8,128)(2,1)}) custom-call(s32[1]{0:T(128)} %bitcast.first, bf16[16,144,256]{2,1,0:T(8,128)(2,1)} %copy-done, bf16[512,256]{1,0:T(8,128)(2,1)} %copy-done.3, f32[32,128]{1,0:T(8,128)} %get-tuple-element.19.lse, f32[16,128]{1,0:T(8,128)} %get-tuple-element.20.weight, ...), custom_call_target="tpu_custom_call" | custom-call | tf_op jit(solution)/shard_map/backward/pallas_call | solution.py:183
  90.7 2.3 %collective-permute-start.20 = (bf16[512,256]{1,0:T(8,128)(2,1)}, bf16[512,256]{1,0:T(8,128)(2,1)}, u32[]{:S(2)}, u32[]{:S(2)}) collective-permute-start(bf16[512,256]{1,0:T(8,128)(2,1)} %get-tuple-element.24), channel_id=1, source_target_pairs={{0,0},{1,33},{2,10},{3,43},{4,60},{5,29},{6,22},{7,55},{8,8},{9,41... | collective-permute-start | bytes 786440 | tf_op jit(solution)/shard_map/ppermute | solution.py:262
  93.0 7.5 %collective-permute-done.20 = bf16[512,256]{1,0:T(8,128)(2,1)} collective-permute-done((bf16[512,256]{1,0:T(8,128)(2,1)}, bf16[512,256]{1,0:T(8,128)(2,1)}, u32[]{:S(2)}, u32[]{:S(2)}) %collective-permute-start.20) | collective-permute-done | bytes 262176 | tf_op jit(solution)/shard_map/ppermute | solution.py:262
  100.5 8.9 %all-to-all-start.3 = ((bf16[8,64,256]{2,1,0:T(8,128)(2,1)}), bf16[8,64,256]{2,1,0:T(8,128)(2,1)S(1)}, u32[]{:S(2)}, u32[]{:S(2)}) async-start(bf16[8,64,256]{2,1,0:T(8,128)(2,1)} %bitcast.2), calls=%async_computation.3 | async-start | bytes 524288 | tf_op jit(solution)/shard_map/all_to_all | solution.py:26
  109.4 2.5 %add_convert_fusion = bf16[16,256,128]{2,1,0:T(8,128)(2,1)} fusion(bf16[16,256,128]{2,1,0:T(8,128)(2,1)S(1)} %collective-permute-done.19, bf16[16,256,128]{2,1,0:T(8,128)(2,1)} %get-tuple-element.22), kind=kLoop, calls=%fused_computation | loop fusion | flops 2097152 | bytes 3145728 | tf_op jit(solution)/shard_map/convert_element_type | solution.py:260
  111.9 3.6 %all-to-all-done.3 = bf16[8,64,256]{2,1,0:T(8,128)(2,1)S(1)} async-done(((bf16[8,64,256]{2,1,0:T(8,128)(2,1)}), bf16[8,64,256]{2,1,0:T(8,128)(2,1)S(1)}, u32[]{:S(2)}, u32[]{:S(2)}) %all-to-all-start.3) | async-done | bytes 262176 | tf_op jit(solution)/shard_map/all_to_all | solution.py:26
  115.5 4.9 %all-to-all-start.2 = ((bf16[16,256,128]{2,1,0:T(8,128)(2,1)}), bf16[16,256,128]{2,1,0:T(8,128)(2,1)S(1)}, u32[]{:S(2)}, u32[]{:S(2)}) async-start(bf16[16,256,128]{2,1,0:T(8,128)(2,1)} %add_convert_fusion), calls=%async_computation.2 | async-start | bytes 2097152 | tf_op jit(solution)/shard_map/all_to_all | solution.py:26
  120.4 2.5 %collective-permute-start.18 = (f32[8,128]{1,0:T(8,128)S(1)}, f32[8,128]{1,0:T(8,128)S(1)}, u32[]{:S(2)}, u32[]{:S(2)}) collective-permute-start(f32[8,128]{1,0:T(8,128)S(1)} %copy-done.9), channel_id=1, source_target_pairs={{0,56},{8,0},{16,8},{24,16},{32,24},{40,32},{48,40},{56,48},{1,57}... | collective-permute-start | bytes 12296 | tf_op jit(solution)/shard_map/ppermute | solution.py:37
  122.9 3.2 %collective-permute-start.17 = (f32[8,128]{1,0:T(8,128)S(1)}, f32[8,128]{1,0:T(8,128)S(1)}, u32[]{:S(2)}, u32[]{:S(2)}) collective-permute-start(f32[8,128]{1,0:T(8,128)S(1)} %copy-done.9), channel_id=1, source_target_pairs={{0,48},{8,56},{16,0},{24,8},{32,16},{40,24},{48,32},{56,40},{1,49}... | collective-permute-start | bytes 12296 | tf_op jit(solution)/shard_map/ppermute | solution.py:37
  126.2 4.2 %collective-permute-start.15 = (f32[8,128]{1,0:T(8,128)S(1)}, f32[8,128]{1,0:T(8,128)S(1)}, u32[]{:S(2)}, u32[]{:S(2)}) collective-permute-start(f32[8,128]{1,0:T(8,128)S(1)} %copy-done.9), channel_id=1, source_target_pairs={{0,32},{8,40},{16,48},{24,56},{32,0},{40,8},{48,16},{56,24},{1,33}... | collective-permute-start | bytes 12296 | tf_op jit(solution)/shard_map/ppermute | solution.py:37
  130.9 2.6 %collective-permute-start.13 = (f32[8,128]{1,0:T(8,128)S(1)}, f32[8,128]{1,0:T(8,128)S(1)}, u32[]{:S(2)}, u32[]{:S(2)}) collective-permute-start(f32[8,128]{1,0:T(8,128)S(1)} %copy-done.9), channel_id=1, source_target_pairs={{0,16},{8,24},{16,32},{24,40},{32,48},{40,56},{48,0},{56,8},{1,17}... | collective-permute-start | bytes 12296 | tf_op jit(solution)/shard_map/ppermute | solution.py:37
  133.5 1.6 %collective-permute-start.12 = (f32[8,128]{1,0:T(8,128)S(1)}, f32[8,128]{1,0:T(8,128)S(1)}, u32[]{:S(2)}, u32[]{:S(2)}) collective-permute-start(f32[8,128]{1,0:T(8,128)S(1)} %copy-done.9), channel_id=1, source_target_pairs={{0,8},{8,16},{16,24},{24,32},{32,40},{40,48},{48,56},{56,0},{1,9},... | collective-permute-start | bytes 12296 | tf_op jit(solution)/shard_map/ppermute | solution.py:37
  135.1 2.0 %collective-permute-done.14 = f32[8,128]{1,0:T(8,128)S(1)} collective-permute-done((f32[8,128]{1,0:T(8,128)S(1)}, f32[8,128]{1,0:T(8,128)S(1)}, u32[]{:S(2)}, u32[]{:S(2)}) %collective-permute-start.14) | collective-permute-done | bytes 4128 | tf_op jit(solution)/shard_map/ppermute | solution.py:37
  141.2 2.1 %finish.1 = f32[128,256]{1,0:T(8,128)} custom-call(bf16[16,256,128]{2,1,0:T(8,128)(2,1)} %copy-done.2), custom_call_target="tpu_custom_call" | custom-call | tf_op jit(solution)/shard_map/finish/pallas_call | solution.py:265
  (73 shorter events, 15.6 us)
Async XLA Ops:
  3.1 32.4 %copy-start.11 = (s32[128]{0:T(128)S(1)}, s32[128]{0:T(128)}, u32[]{:S(2)}) copy-start(s32[128]{0:T(128)} %param.7) | copy-start | bytes 1540
  27.7 18.8 %collective-permute-start.1 = (bf16[16,144,256]{2,1,0:T(8,128)(2,1)S(1)}, bf16[16,144,256]{2,1,0:T(8,128)(2,1)S(1)}, u32[]{:S(2)}, u32[]{:S(2)}) collective-permute-start(bf16[16,144,256]{2,1,0:T(8,128)(2,1)S(1)} %all_to_all.20.packed), channel_id=1, source_target_pairs={{0,1},{1,0},{2,3},{3,2},{4,5},{5,4},{6,7},{7,6},{8,9},{9,8},{10,11... | collective-permute-start | bytes 3538952 | tf_op jit(solution)/shard_map/ppermute | solution.py:229
  27.7 18.7 %collective-permute-start = (bf16[512,256]{1,0:T(8,128)(2,1)S(1)}, bf16[512,256]{1,0:T(8,128)(2,1)S(1)}, u32[]{:S(2)}, u32[]{:S(2)}) collective-permute-start(bf16[512,256]{1,0:T(8,128)(2,1)S(1)} %copy-done.10), channel_id=1, source_target_pairs={{0,0},{33,1},{10,2},{43,3},{60,4},{29,5},{22,6},{55,7},{8,8},{41,9... | collective-permute-start | bytes 786440 | tf_op jit(solution)/shard_map/ppermute | solution.py:224
  35.6 3.9 %collective-permute-start.10 = (f32[8,128]{1,0:T(8,128)S(1)}, f32[8,128]{1,0:T(8,128)S(1)}, u32[]{:S(2)}, u32[]{:S(2)}) collective-permute-start(f32[8,128]{1,0:T(8,128)S(1)} %broadcast_in_dim.33), channel_id=1, source_target_pairs={{0,56},{8,0},{16,8},{24,16},{32,24},{40,32},{48,40},{56,48},{1,57}... | collective-permute-start | bytes 12296 | tf_op jit(solution)/shard_map/ppermute | solution.py:37
  36.7 6.9 %collective-permute-start.9 = (f32[8,128]{1,0:T(8,128)S(1)}, f32[8,128]{1,0:T(8,128)S(1)}, u32[]{:S(2)}, u32[]{:S(2)}) collective-permute-start(f32[8,128]{1,0:T(8,128)S(1)} %broadcast_in_dim.33), channel_id=1, source_target_pairs={{0,48},{8,56},{16,0},{24,8},{32,16},{40,24},{48,32},{56,40},{1,49}... | collective-permute-start | bytes 12296 | tf_op jit(solution)/shard_map/ppermute | solution.py:37
  38.2 16.4 %collective-permute-start.8 = (f32[8,128]{1,0:T(8,128)S(1)}, f32[8,128]{1,0:T(8,128)S(1)}, u32[]{:S(2)}, u32[]{:S(2)}) collective-permute-start(f32[8,128]{1,0:T(8,128)S(1)} %broadcast_in_dim.33), channel_id=1, source_target_pairs={{0,40},{8,48},{16,56},{24,0},{32,8},{40,16},{48,24},{56,32},{1,41}... | collective-permute-start | bytes 12296 | tf_op jit(solution)/shard_map/ppermute | solution.py:37
  39.5 16.1 %collective-permute-start.7 = (f32[8,128]{1,0:T(8,128)S(1)}, f32[8,128]{1,0:T(8,128)S(1)}, u32[]{:S(2)}, u32[]{:S(2)}) collective-permute-start(f32[8,128]{1,0:T(8,128)S(1)} %broadcast_in_dim.33), channel_id=1, source_target_pairs={{0,32},{8,40},{16,48},{24,56},{32,0},{40,8},{48,16},{56,24},{1,33}... | collective-permute-start | bytes 12296 | tf_op jit(solution)/shard_map/ppermute | solution.py:37
  43.7 12.0 %collective-permute-start.6 = (f32[8,128]{1,0:T(8,128)S(1)}, f32[8,128]{1,0:T(8,128)S(1)}, u32[]{:S(2)}, u32[]{:S(2)}) collective-permute-start(f32[8,128]{1,0:T(8,128)S(1)} %broadcast_in_dim.33), channel_id=1, source_target_pairs={{0,24},{8,32},{16,40},{24,48},{32,56},{40,0},{48,8},{56,16},{1,25}... | collective-permute-start | bytes 12296 | tf_op jit(solution)/shard_map/ppermute | solution.py:37
  46.5 9.2 %collective-permute-start.5 = (f32[8,128]{1,0:T(8,128)S(1)}, f32[8,128]{1,0:T(8,128)S(1)}, u32[]{:S(2)}, u32[]{:S(2)}) collective-permute-start(f32[8,128]{1,0:T(8,128)S(1)} %broadcast_in_dim.33), channel_id=1, source_target_pairs={{0,16},{8,24},{16,32},{24,40},{32,48},{40,56},{48,0},{56,8},{1,17}... | collective-permute-start | bytes 12296 | tf_op jit(solution)/shard_map/ppermute | solution.py:37
  46.5 9.2 %collective-permute-start.4 = (f32[8,128]{1,0:T(8,128)S(1)}, f32[8,128]{1,0:T(8,128)S(1)}, u32[]{:S(2)}, u32[]{:S(2)}) collective-permute-start(f32[8,128]{1,0:T(8,128)S(1)} %broadcast_in_dim.33), channel_id=1, source_target_pairs={{0,8},{8,16},{16,24},{24,32},{32,40},{40,48},{48,56},{56,0},{1,9},... | collective-permute-start | bytes 12296 | tf_op jit(solution)/shard_map/ppermute | solution.py:37
  54.5 2.5 %collective-permute-start.2 = (f32[24,128]{1,0:T(8,128)S(1)}, f32[24,128]{1,0:T(8,128)S(1)}, u32[]{:S(2)}, u32[]{:S(2)}) collective-permute-start(f32[24,128]{1,0:T(8,128)S(1)} %copy-done.5), channel_id=1, source_target_pairs={{0,1},{1,0},{2,3},{3,2},{4,5},{5,4},{6,7},{7,6},{8,9},{9,8},{10,11... | collective-permute-start | bytes 36872 | tf_op jit(solution)/shard_map/ppermute | solution.py:232
  55.6 1.5 %collective-permute-start.3 = (f32[24,128]{1,0:T(8,128)}, f32[24,128]{1,0:T(8,128)S(1)}, u32[]{:S(2)}, u32[]{:S(2)}) collective-permute-start(f32[24,128]{1,0:T(8,128)} %get-tuple-element.15.far), channel_id=1, source_target_pairs={{0,1},{1,0},{2,3},{3,2},{4,5},{5,4},{6,7},{7,6},{8,9},{9,8},{10,11... | collective-permute-start | bytes 36872 | tf_op jit(solution)/shard_map/ppermute | solution.py:234
  55.7 1.3 collective-permute-start.11
  86.0 23.5 %collective-permute-start.19 = (bf16[16,256,128]{2,1,0:T(8,128)(2,1)}, bf16[16,256,128]{2,1,0:T(8,128)(2,1)S(1)}, u32[]{:S(2)}, u32[]{:S(2)}) collective-permute-start(bf16[16,256,128]{2,1,0:T(8,128)(2,1)} %get-tuple-element.23), channel_id=1, source_target_pairs={{0,1},{1,0},{2,3},{3,2},{4,5},{5,4},{6,7},{7,6},{8,9},{9,8},{10,11... | collective-permute-start | bytes 3145736 | tf_op jit(solution)/shard_map/ppermute | solution.py:258
  90.7 9.8 %collective-permute-start.20 = (bf16[512,256]{1,0:T(8,128)(2,1)}, bf16[512,256]{1,0:T(8,128)(2,1)}, u32[]{:S(2)}, u32[]{:S(2)}) collective-permute-start(bf16[512,256]{1,0:T(8,128)(2,1)} %get-tuple-element.24), channel_id=1, source_target_pairs={{0,0},{1,33},{2,10},{3,43},{4,60},{5,29},{6,22},{7,55},{8,8},{9,41... | collective-permute-start | bytes 786440 | tf_op jit(solution)/shard_map/ppermute | solution.py:262
  100.5 15.0 %all-to-all-start.3 = ((bf16[8,64,256]{2,1,0:T(8,128)(2,1)}), bf16[8,64,256]{2,1,0:T(8,128)(2,1)S(1)}, u32[]{:S(2)}, u32[]{:S(2)}) async-start(bf16[8,64,256]{2,1,0:T(8,128)(2,1)} %bitcast.2), calls=%async_computation.3 | async-start | bytes 524288 | tf_op jit(solution)/shard_map/all_to_all | solution.py:26
  115.5 24.7 %all-to-all-start.2 = ((bf16[16,256,128]{2,1,0:T(8,128)(2,1)}), bf16[16,256,128]{2,1,0:T(8,128)(2,1)S(1)}, u32[]{:S(2)}, u32[]{:S(2)}) async-start(bf16[16,256,128]{2,1,0:T(8,128)(2,1)} %add_convert_fusion), calls=%async_computation.2 | async-start | bytes 2097152 | tf_op jit(solution)/shard_map/all_to_all | solution.py:26
  120.4 10.5 %collective-permute-start.18 = (f32[8,128]{1,0:T(8,128)S(1)}, f32[8,128]{1,0:T(8,128)S(1)}, u32[]{:S(2)}, u32[]{:S(2)}) collective-permute-start(f32[8,128]{1,0:T(8,128)S(1)} %copy-done.9), channel_id=1, source_target_pairs={{0,56},{8,0},{16,8},{24,16},{32,24},{40,32},{48,40},{56,48},{1,57}... | collective-permute-start | bytes 12296 | tf_op jit(solution)/shard_map/ppermute | solution.py:37
  122.9 10.6 %collective-permute-start.17 = (f32[8,128]{1,0:T(8,128)S(1)}, f32[8,128]{1,0:T(8,128)S(1)}, u32[]{:S(2)}, u32[]{:S(2)}) collective-permute-start(f32[8,128]{1,0:T(8,128)S(1)} %copy-done.9), channel_id=1, source_target_pairs={{0,48},{8,56},{16,0},{24,8},{32,16},{40,24},{48,32},{56,40},{1,49}... | collective-permute-start | bytes 12296 | tf_op jit(solution)/shard_map/ppermute | solution.py:37
  126.1 9.0 %collective-permute-start.16 = (f32[8,128]{1,0:T(8,128)S(1)}, f32[8,128]{1,0:T(8,128)S(1)}, u32[]{:S(2)}, u32[]{:S(2)}) collective-permute-start(f32[8,128]{1,0:T(8,128)S(1)} %copy-done.9), channel_id=1, source_target_pairs={{0,40},{8,48},{16,56},{24,0},{32,8},{40,16},{48,24},{56,32},{1,41}... | collective-permute-start | bytes 12296 | tf_op jit(solution)/shard_map/ppermute | solution.py:37
  126.2 8.8 %collective-permute-start.15 = (f32[8,128]{1,0:T(8,128)S(1)}, f32[8,128]{1,0:T(8,128)S(1)}, u32[]{:S(2)}, u32[]{:S(2)}) collective-permute-start(f32[8,128]{1,0:T(8,128)S(1)} %copy-done.9), channel_id=1, source_target_pairs={{0,32},{8,40},{16,48},{24,56},{32,0},{40,8},{48,16},{56,24},{1,33}... | collective-permute-start | bytes 12296 | tf_op jit(solution)/shard_map/ppermute | solution.py:37
  130.5 6.6 %collective-permute-start.14 = (f32[8,128]{1,0:T(8,128)S(1)}, f32[8,128]{1,0:T(8,128)S(1)}, u32[]{:S(2)}, u32[]{:S(2)}) collective-permute-start(f32[8,128]{1,0:T(8,128)S(1)} %copy-done.9), channel_id=1, source_target_pairs={{0,24},{8,32},{16,40},{24,48},{32,56},{40,0},{48,8},{56,16},{1,25}... | collective-permute-start | bytes 12296 | tf_op jit(solution)/shard_map/ppermute | solution.py:37
  130.9 6.2 %collective-permute-start.13 = (f32[8,128]{1,0:T(8,128)S(1)}, f32[8,128]{1,0:T(8,128)S(1)}, u32[]{:S(2)}, u32[]{:S(2)}) collective-permute-start(f32[8,128]{1,0:T(8,128)S(1)} %copy-done.9), channel_id=1, source_target_pairs={{0,16},{8,24},{16,32},{24,40},{32,48},{40,56},{48,0},{56,8},{1,17}... | collective-permute-start | bytes 12296 | tf_op jit(solution)/shard_map/ppermute | solution.py:37
  133.5 4.8 %collective-permute-start.12 = (f32[8,128]{1,0:T(8,128)S(1)}, f32[8,128]{1,0:T(8,128)S(1)}, u32[]{:S(2)}, u32[]{:S(2)}) collective-permute-start(f32[8,128]{1,0:T(8,128)S(1)} %copy-done.9), channel_id=1, source_target_pairs={{0,8},{8,16},{16,24},{24,32},{32,40},{40,48},{48,56},{56,0},{1,9},... | collective-permute-start | bytes 12296 | tf_op jit(solution)/shard_map/ppermute | solution.py:37
  (11 other events, 65.4 us)

commit v3 on v2

--- a/solution.py
+++ b/solution.py
@@ -7,6 +7,7 @@
 from jax.experimental.pallas import tpu as pltpu
 from jax.sharding import Mesh
 from jax.sharding import PartitionSpec as P
+
 
 NCOH = 16
 PLANE = ("y", "x")
@@ -30,14 +31,6 @@
     return jnp.broadcast_to(value[None], (n, *value.shape))
 
 
-def summed_along(value, axis):
-    n = lax.axis_size(axis)
-    total = value
-    for by in range(1, n):
-        total = total + lax.ppermute(value, axis, [(k, (k + by) % n) for k in range(n)])
-    return total
-
-
 def scores(bank, users):
     return lax.dot_general(bank, users, (((1,), (1,)), ((), ())), preferred_element_type=F32)
 
@@ -83,6 +76,7 @@
 def forward_kernel(rows, first, packed, bank, stats, coh):
     shards = packed.shape[0]
     positive = jnp.zeros((NCOH, 1), F32)
+    count = jnp.zeros((NCOH, 1), F32)
     for at in range(0, shards, STEP):
         logits = scores(bank[...], shard_users(packed, at, rows))
         top = jnp.max(logits, axis=0, keepdims=True)
@@ -93,11 +87,13 @@
         mine = cohort_row(packed, at, rows, 0)
         ids = iota((NCOH, mine.shape[1]), 0).astype(F32)
         positive += jnp.sum(jnp.where(ids == mine, own, F32(0)), axis=1, keepdims=True)
+        count += jnp.sum(jnp.where(ids == mine, F32(1), F32(0)), axis=1, keepdims=True)
         for s in range(STEP):
             cut = slice(s * LANES, (s + 1) * LANES)
             stats[at + s : at + s + 1, :] = lse[:, cut]
             coh[at + s : at + s + 1, :] = mine[:, cut]
-    stats[shards : shards + 8, :] = jnp.broadcast_to(column_to_row(positive), (8, LANES))
+    extra = jnp.where(iota((8, LANES), 0) == 0, column_to_row(positive), column_to_row(count))
+    stats[shards : shards + 8, :] = extra
 
 
 def forward(packed, bank, first, rows):
@@ -114,7 +110,7 @@
     )(first, packed, bank)
 
 
-def join_kernel(near, far, other_near, other_far, count, other_count, out):
+def join_kernel(near, far, other_near, other_far, count, out):
     shards = near.shape[0] - 8
 
     def join(a, b):
@@ -124,15 +120,14 @@
     first = join(near[:shards], other_far[:shards])
     second = join(far[:shards], other_near[:shards])
     positive = near[shards:] + far[shards:] + other_near[shards:] + other_far[shards:]
-    counts = count[...] + other_count[...]
+    extra = jnp.where(iota(positive.shape, 0) == 0, positive, count[...])
     for k in range(out.shape[0]):
         out[k, :shards] = first
         out[k, shards : 2 * shards] = second
-        out[k, 2 * shards : 2 * shards + 8] = positive
-        out[k, 2 * shards + 8 :] = counts
-
-
-def settle_kernel(scale, stats, coh_near, coh_far, lse_out, weight_out, loss_out):
+        out[k, 2 * shards :] = extra
+
+
+def settle_kernel(scale, repeats, stats, coh_near, coh_far, lse_out, weight_out, loss_out):
     shards = coh_near.shape[0]
     both = 2 * shards
     top = stats[0, :both]
@@ -145,7 +140,7 @@
         rest += stats[k, both:]
     lse = top + jnp.log(total)
     lse_out[...] = lse
-    per_cohort = scale / row_to_column(rest[8:9])
+    per_cohort = scale * repeats / row_to_column(rest[1:2])
     weight_out[...] = jnp.broadcast_to(per_cohort, weight_out.shape)
     weights = jnp.zeros((both, LANES), F32)
     cohorts = jnp.concatenate([coh_near[...], coh_far[...]], axis=0)
@@ -156,9 +151,8 @@
     loss_out[...] = jnp.broadcast_to(loss, loss_out.shape)
 
 
-def backward_kernel(rows, half, first, packed, bank, lse, weight, grad_in, user_part, bank_part):
+def backward_core(rows, half, first, packed, bank, lse, weight, user_part, total):
     shards = packed.shape[0]
-    total = grad_in[...]
     bank_t = bank[...].T
     for at in range(0, shards, STEP):
         users = shard_users(packed, at, rows)
@@ -174,22 +168,64 @@
         part = jnp.dot(bank_t, dlogits, preferred_element_type=F32).astype(BF16)
         for s in range(STEP):
             user_part[at + s] = part[:, s * LANES : (s + 1) * LANES]
-        total = total + jnp.dot(dlogits, users, preferred_element_type=F32)
-    bank_part[...] = total.astype(bank_part.dtype)
-
-
-def backward(half, packed, bank, first, lse, weight, grad_in, rows, dtype):
+        grad = jnp.dot(dlogits, users, preferred_element_type=F32)
+        total = grad if total is None else total + grad
+    return total
+
+
+def backward_far_kernel(rows, first, packed, bank, lse, weight, user_part, bank_part):
+    bank_part[...] = backward_core(rows, 1, first, packed, bank, lse, weight, user_part, None)
+
+
+def digits_of(value):
+    high = value.astype(BF16)
+    rest = value - high.astype(F32)
+    mid = rest.astype(BF16)
+    low = (rest - mid.astype(F32)).astype(BF16)
+    row = iota(value.shape, 0)
+    zero = F32(0)
+    tile = jnp.where(row == 0, high.astype(F32), zero)
+    tile = jnp.where(row == 1, mid.astype(F32), tile)
+    return jnp.where(row == 2, low.astype(F32), tile).astype(BF16)
+
+
+def backward_near_kernel(rows, first, packed, bank, lse, weight, far_part, loss, user_part, *rest):
+    pieces, acc = rest[:-1], rest[-1]
+    acc[...] = backward_core(rows, 0, first, packed, bank, lse, weight, user_part, far_part[...])
+    height = acc.shape[0] // len(pieces)
+    tile = digits_of(loss[...])
+    for k, piece in enumerate(pieces):
+        at = pl.multiple_of(((first[1] + k) % len(pieces)) * height, height)
+        piece[:height, :] = acc[pl.ds(at, height), :].astype(BF16)
+        piece[height:, :LANES] = tile
+        piece[height:, LANES:] = tile
+
+
+def backward_far(packed, bank, first, lse, weight, rows):
     shards, _, width = packed.shape
     return pl.pallas_call(
-        functools.partial(backward_kernel, rows, half),
-        in_specs=[SMEM] + [VMEM] * 5,
+        functools.partial(backward_far_kernel, rows),
+        in_specs=[SMEM] + [VMEM] * 4,
         out_specs=[VMEM, VMEM],
         out_shape=[
             jax.ShapeDtypeStruct((shards, width, rows), BF16),
-            jax.ShapeDtypeStruct(bank.shape, dtype),
+            jax.ShapeDtypeStruct(bank.shape, F32),
         ],
-        name="backward",
-    )(first, packed, bank, lse, weight, grad_in)
+        name="backward_far",
+    )(first, packed, bank, lse, weight)
+
+
+def backward_near(packed, bank, first, lse, weight, far_part, loss, rows, pieces):
+    shards, _, width = packed.shape
+    piece = jax.ShapeDtypeStruct((bank.shape[0] // pieces + 8, width), BF16)
+    return pl.pallas_call(
+        functools.partial(backward_near_kernel, rows),
+        in_specs=[SMEM] + [VMEM] * 6,
+        out_specs=[VMEM] * (1 + pieces),
+        out_shape=[jax.ShapeDtypeStruct((shards, width, rows), BF16)] + [piece] * pieces,
+        scratch_shapes=[pltpu.VMEM(bank.shape, F32)],
+        name="backward_near",
+    )(first, packed, bank, lse, weight, far_part, loss)
 
 
 def finish_kernel(parts, out):
@@ -199,49 +235,66 @@
     out[...] = total.T
 
 
-def per_device(users, bank, positives, cohorts):
+def gather_kernel(share, *refs):
+    pieces, (grad, loss) = refs[:-2], refs[-2:]
+    height = grad.shape[0]
+    total = pieces[0][...].astype(F32)
+    for piece in pieces[1:]:
+        total = total + piece[...].astype(F32)
+    grad[...] = total[:height]
+    tail = total[height:]
+    loss[...] = (jnp.sum(tail, axis=0, keepdims=True) * share)[:, :LANES]
+
+
+def step(users, bank, positives, cohorts):
     rows, width = users.shape
     ny, nz, nx, nc = (lax.axis_size(a) for a in ALL)
     plane = ny * nx
     total_users = rows * plane * nz * nc
     cross = [(k, 1 - k) for k in range(nc)]
 
-    pairs = []
-    for z in range(nz):
-        for k in range(nx * nc):
-            pairs.append((((z + SHIFT[k]) % nz) * nx * nc + k, z * nx * nc + k))
-    back = [(b, a) for a, b in pairs]
+    cols = nx * nc
+    fetch = [
+        (((z + SHIFT[k]) % nz) * cols + k, z * cols + k) for z in range(nz) for k in range(cols)
+    ]
     column = lax.axis_index("x") * nc + lax.axis_index("c")
-    shift = sum(jnp.where(column == k, SHIFT[k], 0) for k in range(nx * nc))
+    shift = sum(jnp.where(column == k, SHIFT[k], 0) for k in range(cols))
     block = lax.axis_index("y") * nz + (lax.axis_index("z") + shift) % nz
-    first = jnp.reshape(block * bank.shape[0], (1,)).astype(jnp.int32)
-
+    first = jnp.stack([block * bank.shape[0], column]).astype(jnp.int32)
+
+    turn = lambda y, x: (y * nx + x) % nz
+    counts_from = [
+        ((y * nz + (z + turn(y, x)) % nz) * nx + x, (y * nz + z) * nx + x)
+        for y in range(ny)
+        for z in range(nz)
+        for x in range(nx)
+    ]
+    repeats = plane // nz
+
+    item_block = lax.ppermute(bank, COLUMN, fetch)
     digits = jnp.concatenate([positives // RADIX, positives % RADIX])[None]
     labels = jnp.concatenate([cohorts, jnp.zeros_like(cohorts)])[None]
     extra = jnp.concatenate([digits, labels, jnp.zeros((14, width), jnp.int32)]).astype(BF16)
     packed = jnp.concatenate([users, extra])
     near = exchange(copies(packed, plane), PLANE)
-    item_block = lax.ppermute(bank, COLUMN, pairs)
-    ids = jnp.arange(LANES, dtype=jnp.int32)
-    count = jnp.sum((cohorts[:, None] == ids[None, :]).astype(F32), axis=0)
-    count = summed_along(jnp.broadcast_to(count[None], (8, LANES)), "z")
-    other_count = lax.ppermute(count, "c", cross)
     far = lax.ppermute(near, "c", cross)
 
     near_stats, near_coh = forward(near, item_block, first, rows)
+    count = lax.ppermute(near_stats[plane:], ("y", "z", "x"), counts_from)
     other_near = lax.ppermute(near_stats, "c", cross)
     far_stats, far_coh = forward(far, item_block, first, rows)
     other_far = lax.ppermute(far_stats, "c", cross)
+    count = count + lax.ppermute(count, "c", cross)
     stats = pl.pallas_call(
         join_kernel,
-        in_specs=[VMEM] * 6,
+        in_specs=[VMEM] * 5,
         out_specs=VMEM,
-        out_shape=jax.ShapeDtypeStruct((plane, 2 * plane + 16, LANES), F32),
+        out_shape=jax.ShapeDtypeStruct((plane, 2 * plane + 8, LANES), F32),
         name="join",
-    )(near_stats, far_stats, other_near, other_far, count, other_count)
+    )(near_stats, far_stats, other_near, other_far, count)
     stats = exchange(stats, PLANE)
     lse, weight, loss = pl.pallas_call(
-        functools.partial(settle_kernel, total_users / NCOH),
+        functools.partial(settle_kernel, total_users / NCOH, repeats),
         in_specs=[VMEM] * 3,
         out_specs=[VMEM] * 3,
         out_shape=[
@@ -251,17 +304,30 @@
         ],
         name="settle",
     )(stats, near_coh, far_coh)
-    loss = summed_along(loss, "z")[0, 0] / F32(total_users)
-
-    none = jnp.zeros(bank.shape, F32)
-    far_part, bank_part = backward(1, far, item_block, first, lse, weight, none, rows, F32)
+
+    far_part, bank_part = backward_far(far, item_block, first, lse, weight, rows)
     far_part = lax.ppermute(far_part, "c", cross)
-    near_part, bank_part = backward(0, near, item_block, first, lse, weight, bank_part, rows, BF16)
+    near_part, *pieces = backward_near(near, item_block, first, lse, weight, bank_part, loss, rows, cols)
     user_part = (near_part.astype(F32) + far_part.astype(F32)).astype(BF16)
     user_part = exchange(user_part, PLANE)
-    bank_part = lax.ppermute(bank_part, COLUMN, back)
-    bank_part = exchange(bank_part.reshape(nx * nc, -1, width), ("x", "c"))
-    bank_grad = jnp.sum(bank_part.astype(F32), axis=0)
+    arrived = []
+    for turned, piece in enumerate(pieces):
+        ways = [
+            (z * cols + k, ((z + SHIFT[k]) % nz) * cols + (k + turned) % cols)
+            for z in range(nz)
+            for k in range(cols)
+        ]
+        arrived.append(lax.ppermute(piece, COLUMN, ways))
+    bank_grad, loss = pl.pallas_call(
+        functools.partial(gather_kernel, 1.0 / total_users),
+        in_specs=[VMEM] * cols,
+        out_specs=[VMEM] * 2,
+        out_shape=[
+            jax.ShapeDtypeStruct((bank.shape[0] // cols, width), F32),
+            jax.ShapeDtypeStruct((1, LANES), F32),
+        ],
+        name="gather",
+    )(*arrived)
     user_grad = pl.pallas_call(
         finish_kernel,
         in_specs=[VMEM],
@@ -269,13 +335,13 @@
         out_shape=jax.ShapeDtypeStruct(users.shape, F32),
         name="finish",
     )(user_part)
-    return loss, user_grad, bank_grad
+    return loss[0, 0], user_grad, bank_grad
 
 
 def solution(mesh):
     torus = Mesh(mesh.devices.reshape(4, 8, 4, 2), ALL)
     return jax.shard_map(
-        per_device,
+        step,
         mesh=torus,
         in_specs=(P(ALL, None), P(("y", "z"), None), P(ALL), P(ALL)),
         out_specs=(P(), P(ALL, None), P(ALL, None)),

time: 145 us -> 134 us (0.924)
  the two profiles are of different devices: /device:TPU:2 before, /device:TPU:1 now
where the time goes in v3:
time: 134 us; the launch traced here: 133 us
  blocking collectives  48 us (36%)
  starting transfers between devices  39.9 us (30%)
  Pallas kernels  23.7 us (18%)
  waiting for transfers between devices  9.02 us (7%)
  other arithmetic  6 us (4%)
  local copies, waits for them, and re-layouts  5.47 us (4%)
    all_to_all x2, blocking collectives, exchange(): return lax.all_to_all(value, axis, split_axis=0, concat_axis=0, tiled=True)  48 us
    ppermute x8, starting transfers between devices, step(): arrived.append(lax.ppermute(piece, COLUMN, ways))  22.4 us
    ppermute x1, starting transfers between devices, step(): item_block = lax.ppermute(bank, COLUMN, fetch)  8.81 us
    pallas_call x2, Pallas kernels, forward(): pl.pallas_call(functools.partial(forward_kernel, rows), in_specs=[SMEM, V...  7.37 us
    pallas_call x1, Pallas kernels, backward_near(): pl.pallas_call(functools.partial(backward_near_kernel, rows), in_specs=[S...  4.73 us
    ppermute x8, waiting for transfers between devices, step(): arrived.append(lax.ppermute(piece, COLUMN, ways))  4.68 us
    pallas_call x1, Pallas kernels, backward_far(): pl.pallas_call(functools.partial(backward_far_kernel, rows), in_specs=[SM...  4.6 us
    unnamed x46, local copies, waits for them, and re-layouts  4.6 us
  transfers between devices with their start and end apart: 16, of which 5 were waited for; matrix products, arithmetic and copies ran while one was open for 1% of the time, Pallas kernels for 10%

profile of v3, /device:TPU:1, one launch (start us, length us, event | category | flops | bytes accessed | tf_op | source)
XLA Modules:
  0.0 133.0 jit_solution(12578685530761243095)
XLA Ops:
  3.1 25.0 %all_to_all.15.packed = bf16[16,144,256]{2,1,0:T(8,128)(2,1)S(1)} all-to-all(bf16[16,144,256]{2,1,0:T(8,128)(2,1)S(1)} %broadcast_in_dim.21), channel_id=1, replica_groups=mesh['y'=4,'z'=8,'x'=4,'c'=2] {'y','x'}, dimensions={0} | all-to-all | bytes 2359296 | tf_op jit(solution)/shard_map/all_to_all | solution.py:27
  28.1 2.0 %collective-permute-start.1 = (bf16[16,144,256]{2,1,0:T(8,128)(2,1)S(1)}, bf16[16,144,256]{2,1,0:T(8,128)(2,1)S(1)}, u32[]{:S(2)}, u32[]{:S(2)}) collective-permute-start(bf16[16,144,256]{2,1,0:T(8,128)(2,1)S(1)} %all_to_all.15.packed), channel_id=1, source_target_pairs={{0,1},{1,0},{2,3},{3,2},{4,5},{5,4},{6,7},{7,6},{8,9},{9,8},{10,11... | collective-permute-start | bytes 3538952 | tf_op jit(solution)/shard_map/ppermute | solution.py:280
  30.1 8.8 %collective-permute-start = (bf16[512,256]{1,0:T(8,128)(2,1)S(1)}, bf16[512,256]{1,0:T(8,128)(2,1)S(1)}, u32[]{:S(2)}, u32[]{:S(2)}) collective-permute-start(bf16[512,256]{1,0:T(8,128)(2,1)S(1)} %copy-done.14), channel_id=1, source_target_pairs={{0,0},{33,1},{10,2},{43,3},{60,4},{29,5},{22,6},{55,7},{8,8},{41,9... | collective-permute-start | bytes 786440 | tf_op jit(solution)/shard_map/ppermute | solution.py:274
  39.6 3.2 %collective-permute-done.bank = bf16[512,256]{1,0:T(8,128)(2,1)S(1)} collective-permute-done((bf16[512,256]{1,0:T(8,128)(2,1)S(1)}, bf16[512,256]{1,0:T(8,128)(2,1)S(1)}, u32[]{:S(2)}, u32[]{:S(2)}) %collective-permute-start) | collective-permute-done | bytes 262176 | tf_op jit(solution)/shard_map/ppermute | solution.py:274
  43.5 3.7 %forward.2 = (f32[24,128]{1,0:T(8,128)}, f32[16,128]{1,0:T(8,128)}) custom-call(s32[2]{0:T(128)} %pad_add_fusion.first, bf16[16,144,256]{2,1,0:T(8,128)(2,1)} %copy-done, bf16[512,256]{1,0:T(8,128)(2,1)} %copy-done.3), custom_call_target="tpu_custom_call" | custom-call | tf_op jit(solution)/shard_map/forward/pallas_call | solution.py:101
  48.2 3.7 %forward.3 = (f32[24,128]{1,0:T(8,128)}, f32[16,128]{1,0:T(8,128)}) custom-call(s32[2]{0:T(128)} %pad_add_fusion.first, bf16[16,144,256]{2,1,0:T(8,128)(2,1)} %copy-done.1, bf16[512,256]{1,0:T(8,128)(2,1)} %copy-done.3), custom_call_target="tpu_custom_call" | custom-call | tf_op jit(solution)/shard_map/forward/pallas_call | solution.py:101
  56.8 1.5 %join.1 = f32[16,40,128]{2,1,0:T(8,128)} custom-call(f32[24,128]{1,0:T(8,128)} %get-tuple-element.23.near, f32[24,128]{1,0:T(8,128)} %get-tuple-element.24.far, f32[24,128]{1,0:T(8,128)} %copy-done.12, f32[24,128]{1,0:T(8,128)} %copy-done.13, f32[8,128]{1,0:T(8,128)} %add.58.count), custom_call_target="tpu_custom_call" | custom-call | tf_op jit(solution)/shard_map/join/pallas_call | solution.py:288
  58.3 23.0 %all_to_all.16.stats = f32[16,40,128]{2,1,0:T(8,128)} all-to-all(f32[16,40,128]{2,1,0:T(8,128)} %join.1), channel_id=1, replica_groups=mesh['y'=4,'z'=8,'x'=4,'c'=2] {'y','x'}, dimensions={0} | all-to-all | bytes 655360 | tf_op jit(solution)/shard_map/all_to_all | solution.py:27
  81.3 1.8 %settle.1 = (f32[32,128]{1,0:T(8,128)}, f32[16,128]{1,0:T(8,128)}, f32[8,128]{1,0:T(8,128)}) custom-call(f32[16,40,128]{2,1,0:T(8,128)} %all_to_all.16.stats, f32[16,128]{1,0:T(8,128)} %get-tuple-element.25.coh_near, f32[16,128]{1,0:T(8,128)} %get-tuple-element.26.coh_far), custom_call_target="tpu_custom_call" | custom-call | tf_op jit(solution)/shard_map/settle/pallas_call | solution.py:296
  83.2 4.6 %backward_far.1 = (bf16[16,256,128]{2,1,0:T(8,128)(2,1)}, f32[512,256]{1,0:T(8,128)}) custom-call(s32[2]{0:T(128)} %pad_add_fusion.first, bf16[16,144,256]{2,1,0:T(8,128)(2,1)} %copy-done.1, bf16[512,256]{1,0:T(8,128)(2,1)} %copy-done.3, f32[32,128]{1,0:T(8,128)} %get-tuple-element.27.lse, f32[16,128]{1,0:T(8,128)} %get-tuple-element.28.weight), custom_call_target="tpu_custom_call" | custom-call | tf_op jit(solution)/shard_map/backward_far/pallas_call | solution.py:206
  87.8 1.5 %collective-permute-start.14 = (bf16[16,256,128]{2,1,0:T(8,128)(2,1)}, bf16[16,256,128]{2,1,0:T(8,128)(2,1)S(1)}, u32[]{:S(2)}, u32[]{:S(2)}) collective-permute-start(bf16[16,256,128]{2,1,0:T(8,128)(2,1)} %get-tuple-element.41), channel_id=1, source_target_pairs={{0,1},{1,0},{2,3},{3,2},{4,5},{5,4},{6,7},{7,6},{8,9},{9,8},{10,11... | collective-permute-start | bytes 3145736 | tf_op jit(solution)/shard_map/ppermute | solution.py:309
  89.3 4.7 %backward_near.1 = (bf16[16,256,128]{2,1,0:T(8,128)(2,1)}, bf16[72,256]{1,0:T(8,128)(2,1)}, bf16[72,256]{1,0:T(8,128)(2,1)}, bf16[72,256]{1,0:T(8,128)(2,1)}, bf...) custom-call(s32[2]{0:T(128)} %pad_add_fusion.first, ...), custom_call_target="tpu_custom_call" | custom-call | tf_op jit(solution)/shard_map/backward_near/pallas_call | solution.py:221
  94.0 2.5 %add_convert_fusion = bf16[16,256,128]{2,1,0:T(8,128)(2,1)} fusion(bf16[16,256,128]{2,1,0:T(8,128)(2,1)S(1)} %collective-permute-done.14, bf16[16,256,128]{2,1,0:T(8,128)(2,1)} %get-tuple-element.40), kind=kLoop, calls=%fused_computation | loop fusion | flops 2097152 | bytes 3145728 | tf_op jit(solution)/shard_map/convert_element_type | solution.py:311
  96.6 4.0 %all-to-all-start.2 = ((bf16[16,256,128]{2,1,0:T(8,128)(2,1)}), bf16[16,256,128]{2,1,0:T(8,128)(2,1)S(1)}, u32[]{:S(2)}, u32[]{:S(2)}) async-start(bf16[16,256,128]{2,1,0:T(8,128)(2,1)} %add_convert_fusion), calls=%async_computation.2 | async-start | bytes 2097152 | tf_op jit(solution)/shard_map/all_to_all | solution.py:27
  100.6 5.9 %collective-permute-start.6 = (bf16[72,256]{1,0:T(8,128)(2,1)S(1)}, bf16[72,256]{1,0:T(8,128)(2,1)S(1)}, u32[]{:S(2)}, u32[]{:S(2)}) collective-permute-start(bf16[72,256]{1,0:T(8,128)(2,1)S(1)} %copy-done.22), channel_id=1, source_target_pairs={{0,0},{1,33},{2,10},{3,43},{4,60},{5,29},{6,22},{7,55},{8,8},{9,41... | collective-permute-start | bytes 110600 | tf_op jit(solution)/shard_map/ppermute | solution.py:320
  106.4 3.6 %collective-permute-start.7 = (bf16[72,256]{1,0:T(8,128)(2,1)S(1)}, bf16[72,256]{1,0:T(8,128)(2,1)S(1)}, u32[]{:S(2)}, u32[]{:S(2)}) collective-permute-start(bf16[72,256]{1,0:T(8,128)(2,1)S(1)} %copy-done.21), channel_id=1, source_target_pairs={{0,1},{1,34},{2,11},{3,44},{4,61},{5,30},{6,23},{7,48},{8,9},{9,42... | collective-permute-start | bytes 110600 | tf_op jit(solution)/shard_map/ppermute | solution.py:320
  110.5 4.4 %collective-permute-start.9 = (bf16[72,256]{1,0:T(8,128)(2,1)S(1)}, bf16[72,256]{1,0:T(8,128)(2,1)S(1)}, u32[]{:S(2)}, u32[]{:S(2)}) collective-permute-start(bf16[72,256]{1,0:T(8,128)(2,1)S(1)} %copy-done.19), channel_id=1, source_target_pairs={{0,3},{1,36},{2,13},{3,46},{4,63},{5,24},{6,17},{7,50},{8,11},{9,4... | collective-permute-start | bytes 110600 | tf_op jit(solution)/shard_map/ppermute | solution.py:320
  114.9 2.4 %collective-permute-start.10 = (bf16[72,256]{1,0:T(8,128)(2,1)S(1)}, bf16[72,256]{1,0:T(8,128)(2,1)S(1)}, u32[]{:S(2)}, u32[]{:S(2)}) collective-permute-start(bf16[72,256]{1,0:T(8,128)(2,1)S(1)} %copy-done.18), channel_id=1, source_target_pairs={{0,4},{1,37},{2,14},{3,47},{4,56},{5,25},{6,18},{7,51},{8,12},{9,4... | collective-permute-start | bytes 110600 | tf_op jit(solution)/shard_map/ppermute | solution.py:320
  117.3 2.2 %collective-permute-start.11 = (bf16[72,256]{1,0:T(8,128)(2,1)S(1)}, bf16[72,256]{1,0:T(8,128)(2,1)S(1)}, u32[]{:S(2)}, u32[]{:S(2)}) collective-permute-start(bf16[72,256]{1,0:T(8,128)(2,1)S(1)} %copy-done.17), channel_id=1, source_target_pairs={{0,5},{1,38},{2,15},{3,40},{4,57},{5,26},{6,19},{7,52},{8,13},{9,4... | collective-permute-start | bytes 110600 | tf_op jit(solution)/shard_map/ppermute | solution.py:320
  119.5 2.3 %collective-permute-start.12 = (bf16[72,256]{1,0:T(8,128)(2,1)S(1)}, bf16[72,256]{1,0:T(8,128)(2,1)S(1)}, u32[]{:S(2)}, u32[]{:S(2)}) collective-permute-start(bf16[72,256]{1,0:T(8,128)(2,1)S(1)} %copy-done.16), channel_id=1, source_target_pairs={{0,6},{1,39},{2,8},{3,41},{4,58},{5,27},{6,20},{7,53},{8,14},{9,47... | collective-permute-start | bytes 110600 | tf_op jit(solution)/shard_map/ppermute | solution.py:320
  123.6 1.6 %collective-permute-done.12.refs_6_ = bf16[72,256]{1,0:T(8,128)(2,1)S(1)} collective-permute-done((bf16[72,256]{1,0:T(8,128)(2,1)S(1)}, bf16[72,256]{1,0:T(8,128)(2,1)S(1)}, u32[]{:S(2)}, u32[]{:S(2)}) %collective-permute-start.12) | collective-permute-done | bytes 36896 | tf_op jit(solution)/shard_map/ppermute | solution.py:320
  125.2 2.5 %collective-permute-done.13.refs_7_ = bf16[72,256]{1,0:T(8,128)(2,1)S(1)} collective-permute-done((bf16[72,256]{1,0:T(8,128)(2,1)S(1)}, bf16[72,256]{1,0:T(8,128)(2,1)S(1)}, u32[]{:S(2)}, u32[]{:S(2)}) %collective-permute-start.13) | collective-permute-done | bytes 36896 | tf_op jit(solution)/shard_map/ppermute | solution.py:320
  128.3 1.6 %gather.1 = (f32[64,256]{1,0:T(8,128)}, f32[1,128]{1,0:T(1,128)}) custom-call(bf16[72,256]{1,0:T(8,128)(2,1)} %copy-done.4, bf16[72,256]{1,0:T(8,128)(2,1)} %copy-done.5, bf16[72,256]{1,0:T(8,128)(2,1)} %copy-done.6, bf16[72,256]{1,0:T(8,128)(2,1)} %copy-done.7, bf16[72,256]{1,0:T(8,128)(2,1)} %copy-done.8, bf16[72,256]{1,0:T(8,128)(2,1)} %copy-done.9, ...), custom_call_target="tpu_custom_call" | custom-call | tf_op jit(solution)/shard_map/gather/pallas_call | solution.py:321
  130.9 2.1 %finish.1 = f32[128,256]{1,0:T(8,128)} custom-call(bf16[16,256,128]{2,1,0:T(8,128)(2,1)} %copy-done.2), custom_call_target="tpu_custom_call" | custom-call | tf_op jit(solution)/shard_map/finish/pallas_call | solution.py:331
  (78 shorter events, 13.6 us)
Async XLA Ops:
  3.1 27.0 %copy-start.14 = (bf16[512,256]{1,0:T(8,128)(2,1)S(1)}, bf16[512,256]{1,0:T(8,128)(2,1)}, u32[]{:S(2)}) copy-start(bf16[512,256]{1,0:T(8,128)(2,1)} %param.5) | copy-start | bytes 786436
  28.1 14.7 %copy-start = (bf16[16,144,256]{2,1,0:T(8,128)(2,1)}, bf16[16,144,256]{2,1,0:T(8,128)(2,1)S(1)}, u32[]{:S(2)}) copy-start(bf16[16,144,256]{2,1,0:T(8,128)(2,1)S(1)} %all_to_all.15.packed) | copy-start | bytes 3538948
  28.1 19.1 %collective-permute-start.1 = (bf16[16,144,256]{2,1,0:T(8,128)(2,1)S(1)}, bf16[16,144,256]{2,1,0:T(8,128)(2,1)S(1)}, u32[]{:S(2)}, u32[]{:S(2)}) collective-permute-start(bf16[16,144,256]{2,1,0:T(8,128)(2,1)S(1)} %all_to_all.15.packed), channel_id=1, source_target_pairs={{0,1},{1,0},{2,3},{3,2},{4,5},{5,4},{6,7},{7,6},{8,9},{9,8},{10,11... | collective-permute-start | bytes 3538952 | tf_op jit(solution)/shard_map/ppermute | solution.py:280
  30.1 12.7 %collective-permute-start = (bf16[512,256]{1,0:T(8,128)(2,1)S(1)}, bf16[512,256]{1,0:T(8,128)(2,1)S(1)}, u32[]{:S(2)}, u32[]{:S(2)}) collective-permute-start(bf16[512,256]{1,0:T(8,128)(2,1)S(1)} %copy-done.14), channel_id=1, source_target_pairs={{0,0},{33,1},{10,2},{43,3},{60,4},{29,5},{22,6},{55,7},{8,8},{41,9... | collective-permute-start | bytes 786440 | tf_op jit(solution)/shard_map/ppermute | solution.py:274
  47.2 8.4 %collective-permute-start.2 = (f32[24,128]{1,0:T(8,128)}, f32[24,128]{1,0:T(8,128)S(1)}, u32[]{:S(2)}, u32[]{:S(2)}) collective-permute-start(f32[24,128]{1,0:T(8,128)} %get-tuple-element.23.near), channel_id=1, source_target_pairs={{0,1},{1,0},{2,3},{3,2},{4,5},{5,4},{6,7},{7,6},{8,9},{9,8},{10,11... | collective-permute-start | bytes 36872 | tf_op jit(solution)/shard_map/ppermute | solution.py:284
  51.9 3.7 %collective-permute-start.3 = (f32[24,128]{1,0:T(8,128)}, f32[24,128]{1,0:T(8,128)S(1)}, u32[]{:S(2)}, u32[]{:S(2)}) collective-permute-start(f32[24,128]{1,0:T(8,128)} %get-tuple-element.24.far), channel_id=1, source_target_pairs={{0,1},{1,0},{2,3},{3,2},{4,5},{5,4},{6,7},{7,6},{8,9},{9,8},{10,11... | collective-permute-start | bytes 36872 | tf_op jit(solution)/shard_map/ppermute | solution.py:286
  53.1 0.7 collective-permute-start.4
  53.8 1.3 collective-permute-start.5
  87.8 6.2 %collective-permute-start.14 = (bf16[16,256,128]{2,1,0:T(8,128)(2,1)}, bf16[16,256,128]{2,1,0:T(8,128)(2,1)S(1)}, u32[]{:S(2)}, u32[]{:S(2)}) collective-permute-start(bf16[16,256,128]{2,1,0:T(8,128)(2,1)} %get-tuple-element.41), channel_id=1, source_target_pairs={{0,1},{1,0},{2,3},{3,2},{4,5},{5,4},{6,7},{7,6},{8,9},{9,8},{10,11... | collective-permute-start | bytes 3145736 | tf_op jit(solution)/shard_map/ppermute | solution.py:309
  96.5 13.5 %copy-start.20 = (bf16[72,256]{1,0:T(8,128)(2,1)S(1)}, bf16[72,256]{1,0:T(8,128)(2,1)}, u32[]{:S(2)}) copy-start(bf16[72,256]{1,0:T(8,128)(2,1)} %get-tuple-element.33) | copy-start | bytes 110596
  96.5 14.0 %copy-start.19 = (bf16[72,256]{1,0:T(8,128)(2,1)S(1)}, bf16[72,256]{1,0:T(8,128)(2,1)}, u32[]{:S(2)}) copy-start(bf16[72,256]{1,0:T(8,128)(2,1)} %get-tuple-element.34) | copy-start | bytes 110596
  96.5 18.4 %copy-start.18 = (bf16[72,256]{1,0:T(8,128)(2,1)S(1)}, bf16[72,256]{1,0:T(8,128)(2,1)}, u32[]{:S(2)}) copy-start(bf16[72,256]{1,0:T(8,128)(2,1)} %get-tuple-element.35) | copy-start | bytes 110596
  96.5 20.8 %copy-start.17 = (bf16[72,256]{1,0:T(8,128)(2,1)S(1)}, bf16[72,256]{1,0:T(8,128)(2,1)}, u32[]{:S(2)}) copy-start(bf16[72,256]{1,0:T(8,128)(2,1)} %get-tuple-element.36) | copy-start | bytes 110596
  96.5 23.0 %copy-start.16 = (bf16[72,256]{1,0:T(8,128)(2,1)S(1)}, bf16[72,256]{1,0:T(8,128)(2,1)}, u32[]{:S(2)}) copy-start(bf16[72,256]{1,0:T(8,128)(2,1)} %get-tuple-element.37) | copy-start | bytes 110596
  96.5 25.3 %copy-start.15 = (bf16[72,256]{1,0:T(8,128)(2,1)S(1)}, bf16[72,256]{1,0:T(8,128)(2,1)}, u32[]{:S(2)}) copy-start(bf16[72,256]{1,0:T(8,128)(2,1)} %get-tuple-element.38) | copy-start | bytes 110596
  96.6 33.4 %all-to-all-start.2 = ((bf16[16,256,128]{2,1,0:T(8,128)(2,1)}), bf16[16,256,128]{2,1,0:T(8,128)(2,1)S(1)}, u32[]{:S(2)}, u32[]{:S(2)}) async-start(bf16[16,256,128]{2,1,0:T(8,128)(2,1)} %add_convert_fusion), calls=%async_computation.2 | async-start | bytes 2097152 | tf_op jit(solution)/shard_map/all_to_all | solution.py:27
  100.6 16.8 %collective-permute-start.6 = (bf16[72,256]{1,0:T(8,128)(2,1)S(1)}, bf16[72,256]{1,0:T(8,128)(2,1)S(1)}, u32[]{:S(2)}, u32[]{:S(2)}) collective-permute-start(bf16[72,256]{1,0:T(8,128)(2,1)S(1)} %copy-done.22), channel_id=1, source_target_pairs={{0,0},{1,33},{2,10},{3,43},{4,60},{5,29},{6,22},{7,55},{8,8},{9,41... | collective-permute-start | bytes 110600 | tf_op jit(solution)/shard_map/ppermute | solution.py:320
  106.4 13.1 %collective-permute-start.7 = (bf16[72,256]{1,0:T(8,128)(2,1)S(1)}, bf16[72,256]{1,0:T(8,128)(2,1)S(1)}, u32[]{:S(2)}, u32[]{:S(2)}) collective-permute-start(bf16[72,256]{1,0:T(8,128)(2,1)S(1)} %copy-done.21), channel_id=1, source_target_pairs={{0,1},{1,34},{2,11},{3,44},{4,61},{5,30},{6,23},{7,48},{8,9},{9,42... | collective-permute-start | bytes 110600 | tf_op jit(solution)/shard_map/ppermute | solution.py:320
  110.1 11.8 %collective-permute-start.8 = (bf16[72,256]{1,0:T(8,128)(2,1)S(1)}, bf16[72,256]{1,0:T(8,128)(2,1)S(1)}, u32[]{:S(2)}, u32[]{:S(2)}) collective-permute-start(bf16[72,256]{1,0:T(8,128)(2,1)S(1)} %copy-done.20), channel_id=1, source_target_pairs={{0,2},{1,35},{2,12},{3,45},{4,62},{5,31},{6,16},{7,49},{8,10},{9,4... | collective-permute-start | bytes 110600 | tf_op jit(solution)/shard_map/ppermute | solution.py:320
  110.5 12.5 %collective-permute-start.9 = (bf16[72,256]{1,0:T(8,128)(2,1)S(1)}, bf16[72,256]{1,0:T(8,128)(2,1)S(1)}, u32[]{:S(2)}, u32[]{:S(2)}) collective-permute-start(bf16[72,256]{1,0:T(8,128)(2,1)S(1)} %copy-done.19), channel_id=1, source_target_pairs={{0,3},{1,36},{2,13},{3,46},{4,63},{5,24},{6,17},{7,50},{8,11},{9,4... | collective-permute-start | bytes 110600 | tf_op jit(solution)/shard_map/ppermute | solution.py:320
  114.9 8.6 %collective-permute-start.10 = (bf16[72,256]{1,0:T(8,128)(2,1)S(1)}, bf16[72,256]{1,0:T(8,128)(2,1)S(1)}, u32[]{:S(2)}, u32[]{:S(2)}) collective-permute-start(bf16[72,256]{1,0:T(8,128)(2,1)S(1)} %copy-done.18), channel_id=1, source_target_pairs={{0,4},{1,37},{2,14},{3,47},{4,56},{5,25},{6,18},{7,51},{8,12},{9,4... | collective-permute-start | bytes 110600 | tf_op jit(solution)/shard_map/ppermute | solution.py:320
  117.3 6.3 %collective-permute-start.11 = (bf16[72,256]{1,0:T(8,128)(2,1)S(1)}, bf16[72,256]{1,0:T(8,128)(2,1)S(1)}, u32[]{:S(2)}, u32[]{:S(2)}) collective-permute-start(bf16[72,256]{1,0:T(8,128)(2,1)S(1)} %copy-done.17), channel_id=1, source_target_pairs={{0,5},{1,38},{2,15},{3,40},{4,57},{5,26},{6,19},{7,52},{8,13},{9,4... | collective-permute-start | bytes 110600 | tf_op jit(solution)/shard_map/ppermute | solution.py:320
  119.5 5.7 %collective-permute-start.12 = (bf16[72,256]{1,0:T(8,128)(2,1)S(1)}, bf16[72,256]{1,0:T(8,128)(2,1)S(1)}, u32[]{:S(2)}, u32[]{:S(2)}) collective-permute-start(bf16[72,256]{1,0:T(8,128)(2,1)S(1)} %copy-done.16), channel_id=1, source_target_pairs={{0,6},{1,39},{2,8},{3,41},{4,58},{5,27},{6,20},{7,53},{8,14},{9,47... | collective-permute-start | bytes 110600 | tf_op jit(solution)/shard_map/ppermute | solution.py:320
  121.8 5.9 %collective-permute-start.13 = (bf16[72,256]{1,0:T(8,128)(2,1)S(1)}, bf16[72,256]{1,0:T(8,128)(2,1)S(1)}, u32[]{:S(2)}, u32[]{:S(2)}) collective-permute-start(bf16[72,256]{1,0:T(8,128)(2,1)S(1)} %copy-done.15), channel_id=1, source_target_pairs={{0,7},{1,32},{2,9},{3,42},{4,59},{5,28},{6,21},{7,54},{8,15},{9,40... | collective-permute-start | bytes 110600 | tf_op jit(solution)/shard_map/ppermute | solution.py:320
  (15 other events, 58.3 us)

commit v4 on v3

v4 whole, which is shorter than its diff:
```python
import functools

import jax
import jax.numpy as jnp
from jax import lax
from jax.experimental import pallas as pl
from jax.experimental.pallas import tpu as pltpu
from jax.sharding import Mesh
from jax.sharding import PartitionSpec as P


NCOH = 16
PLANE = ("y", "x")
COLUMN = ("z", "x", "c")
ALL = ("y", "z", "x", "c")
SHIFT = (0, 4, 1, 5, 7, 3, 2, 6)
F32 = jnp.float32
BF16 = jnp.bfloat16
LANES = 128
RADIX = 128
STEP = 4
VMEM = pl.BlockSpec(memory_space=pltpu.VMEM)


def call(kernel, out_shape, *operands, scratch=()):
    return pl.pallas_call(
        kernel,
        in_specs=[VMEM] * len(operands),
        out_specs=jax.tree.map(lambda _: VMEM, out_shape),
        out_shape=out_shape,
        scratch_shapes=list(scratch),
        compiler_params=pltpu.CompilerParams(vmem_limit_bytes=24 << 20),
    )(*operands)


def f32(*shape):
    return jax.ShapeDtypeStruct(shape, F32)


def bf16(*shape):
    return jax.ShapeDtypeStruct(shape, BF16)


def first_item(items):
    column = lax.axis_index("x") * lax.axis_size("c") + lax.axis_index("c")
    shift = sum(jnp.where(column == k, by, 0) for k, by in enumerate(SHIFT))
    nz = lax.axis_size("z")
    return (lax.axis_index("y") * nz + (lax.axis_index("z") + shift) % nz) * items


def exchange(value, axis):
    return lax.all_to_all(value, axis, split_axis=0, concat_axis=0, tiled=True)


def copies(value, n):
    return jnp.broadcast_to(value[None], (n, *value.shape))


def scores(bank, users):
    return lax.dot_general(bank, users, (((1,), (1,)), ((), ())), preferred_element_type=F32)


def iota(shape, dim):
    return lax.broadcasted_iota(jnp.int32, shape, dim)


def shard_users(packed, at, rows):
    return jnp.concatenate([packed[at + s, :rows, :] for s in range(STEP)], axis=0)


def shard_row(packed, at, row, half):
    cut = slice(half * LANES, (half + 1) * LANES)
    tiles = [packed[at + s, row : row + 8, cut].astype(F32)[0:1] for s in range(STEP)]
    return jnp.concatenate(tiles, axis=1)


def cohort_row(packed, at, rows, half):
    cut = slice(half * LANES, (half + 1) * LANES)
    tiles = [packed[at + s, rows : rows + 8, cut].astype(F32)[1:2] for s in range(STEP)]
    return jnp.concatenate(tiles, axis=1)


def local_positives(packed, at, rows, first):
    high = shard_row(packed, at, rows, 0)
    low = shard_row(packed, at, rows, 1)
    return (high * RADIX + low).astype(jnp.int32) - first


def column_to_row(column):
    shape = (NCOH, LANES)
    spread = jnp.where(iota(shape, 0) == iota(shape, 1), column, F32(0))
    return jnp.sum(spread, axis=0, keepdims=True)


def row_to_column(row):
    shape = (NCOH, LANES)
    spread = jnp.where(iota(shape, 0) == iota(shape, 1), row, F32(0))
    return jnp.sum(spread, axis=1, keepdims=True)


def forward_kernel(rows, packed, bank, stats, coh, counts):
    shards = packed.shape[0]
    first = first_item(bank.shape[0])
    positive = jnp.zeros((NCOH, 1), F32)
    count = jnp.zeros((NCOH, 1), F32)
    for at in range(0, shards, STEP):
        logits = scores(bank[...], shard_users(packed, at, rows))
        top = jnp.max(logits, axis=0, keepdims=True)
        total = jnp.sum(jnp.exp(logits - top), axis=0, keepdims=True)
        pos = local_positives(packed, at, rows, first)
        own = jnp.sum(jnp.where(iota(logits.shape, 0) == pos, logits, F32(0)), axis=0, keepdims=True)
        lse = top + jnp.log(total)
        mine = cohort_row(packed, at, rows, 0)
        ids = iota((NCOH, mine.shape[1]), 0).astype(F32)
        positive += jnp.sum(jnp.where(ids == mine, own, F32(0)), axis=1, keepdims=True)
        count += jnp.sum(jnp.where(ids == mine, F32(1), F32(0)), axis=1, keepdims=True)
        for s in range(STEP):
            cut = slice(s * LANES, (s + 1) * LANES)
            stats[at + s : at + s + 1, :] = lse[:, cut]
            coh[at + s : at + s + 1, :] = mine[:, cut]
    stats[shards:, :] = jnp.broadcast_to(column_to_row(positive), (8, LANES))
    counts[...] = jnp.broadcast_to(column_to_row(count), (8, LANES))


def forward(packed, bank, rows):
    shards = packed.shape[0]
    shapes = (f32(shards + 8, LANES), f32(shards, LANES), f32(8, LANES))
    return call(functools.partial(forward_kernel, rows), shapes, packed, bank)


def join_kernel(near, far, other_near, other_far, count, other_count, out):
    shards = near.shape[0] - 8

    def join(a, b):
        top = jnp.maximum(a, b)
        return top + jnp.log(jnp.exp(a - top) + jnp.exp(b - top))

    first = join(near[:shards], other_far[:shards])
    second = join(far[:shards], other_near[:shards])
    positive = near[shards:] + far[shards:] + other_near[shards:] + other_far[shards:]
    extra = jnp.where(iota(positive.shape, 0) == 0, positive, count[...] + other_count[...])
    for k in range(out.shape[0]):
        out[k, :shards] = first
        out[k, shards : 2 * shards] = second
        out[k, 2 * shards :] = extra


def settle(scale, repeats, stats, coh_near, coh_far, lse_out, weight_out, loss_out):
    shards = coh_near.shape[0]
    both = 2 * shards
    top = stats[0, :both]
    for k in range(1, stats.shape[0]):
        top = jnp.maximum(top, stats[k, :both])
    total = jnp.exp(stats[0, :both] - top)
    rest = stats[0, both:]
    for k in range(1, stats.shape[0]):
        total += jnp.exp(stats[k, :both] - top)
        rest += stats[k, both:]
    lse = top + jnp.log(total)
    lse_out[...] = lse
    per_cohort = scale * repeats / row_to_column(rest[1:2])
    weight_out[...] = jnp.broadcast_to(per_cohort, weight_out.shape)
    weights = jnp.zeros((both, LANES), F32)
    cohorts = jnp.concatenate([coh_near[...], coh_far[...]], axis=0)
    for c in range(NCOH):
        weights = jnp.where(cohorts == F32(c), per_cohort[c : c + 1, :], weights)
    loss = jnp.sum(weights * lse, keepdims=True)
    loss -= jnp.sum(per_cohort * row_to_column(rest[0:1]), keepdims=True)
    loss_out[...] = jnp.broadcast_to(loss, loss_out.shape)


def backward_core(rows, half, packed, bank, lse, weight, user_part, total):
    shards = packed.shape[0]
    bank_t = bank[...].T
    first = first_item(bank.shape[0])
    for at in range(0, shards, STEP):
        users = shard_users(packed, at, rows)
        logits = scores(bank[...], users)
        pos = local_positives(packed, at, rows, first)
        mine = cohort_row(packed, at, rows, 0)
        ids = iota((NCOH, mine.shape[1]), 0).astype(F32)
        weights = jnp.sum(jnp.where(ids == mine, weight[:, 0:1], F32(0)), axis=0, keepdims=True)
        line = half * shards + at
        level = jnp.concatenate([lse[line + s : line + s + 1, :] for s in range(STEP)], axis=1)
        hot = jnp.where(iota(logits.shape, 0) == pos, F32(1), F32(0))
        dlogits = (weights * (jnp.exp(logits - level) - hot)).astype(BF16)
        part = jnp.dot(bank_t, dlogits, preferred_element_type=F32).astype(BF16)
        for s in range(STEP):
            user_part[at + s] = part[:, s * LANES : (s + 1) * LANES]
        grad = jnp.dot(dlogits, users, preferred_element_type=F32)
        total = grad if total is None else total + grad
    return total


def backward_far_kernel(rows, scale, repeats, packed, bank, stats, coh_near, coh_far, *outs):
    user_part, bank_part, lse, weight, loss = outs
    settle(scale, repeats, stats, coh_near, coh_far, lse, weight, loss)
    bank_part[...] = backward_core(rows, 1, packed, bank, lse, weight, user_part, None)


def digits_of(value):
    high = value.astype(BF16)
    rest = value - high.astype(F32)
    mid = rest.astype(BF16)
    low = (rest - mid.astype(F32)).astype(BF16)
    row = iota(value.shape, 0)
    zero = F32(0)
    tile = jnp.where(row == 0, high.astype(F32), zero)
    tile = jnp.where(row == 1, mid.astype(F32), tile)
    return jnp.where(row == 2, low.astype(F32), tile).astype(BF16)


def read_digits(tile):
    return jnp.sum(tile.astype(F32), axis=0, keepdims=True)[:, :LANES]


def write_digits(out, at, value):
    tile = digits_of(jnp.broadcast_to(value, (8, LANES)))
    out[at : at + 8, :LANES] = tile
    out[at : at + 8, LANES:] = tile


def backward_near_kernel(rows, packed, bank, lse, weight, far_part, loss, user_part, out, acc):
    acc[...] = backward_core(rows, 0, packed, bank, lse, weight, user_part, far_part[...])
    nx, nc = lax.axis_size("x"), lax.axis_size("c")
    height = acc.shape[0] // (nx * nc)
    core = lax.axis_index("c")
    for side, owner in enumerate((1 - core, core)):
        for r in range(nx):
            piece = (lax.axis_index("x") + r) % nx * nc + owner
            at = pl.multiple_of(piece * height, height)
            to = side * (nx * height + 8) + r * height
            out[to : to + height, :] = acc[pl.ds(at, height), :].astype(BF16)
    write_digits(out, nx * height, loss[...])


def halve_kernel(mine, theirs, *pieces):
    below = theirs.shape[0]
    height = (below - 8) // len(pieces)
    loss = read_digits(mine[below - 8 : below, :]) + read_digits(theirs[below - 8 :, :])
    for r, piece in enumerate(pieces):
        cut = slice(below + r * height, below + (r + 1) * height)
        own = mine[cut, :].astype(F32) + theirs[r * height : (r + 1) * height, :].astype(F32)
        piece[:height, :] = own.astype(BF16)
        write_digits(piece, height, loss)


def gather_kernel(share, *refs):
    pieces, (grad, loss) = refs[:-2], refs[-2:]
    height = grad.shape[0]
    total = pieces[0][...].astype(F32)
    for piece in pieces[1:]:
        total = total + piece[...].astype(F32)
    grad[...] = total[:height]
    loss[...] = jnp.sum(total[height:], axis=0, keepdims=True)[:, :LANES] * share


def step(users, bank, positives, cohorts):
    rows, width = users.shape
    ny, nz, nx, nc = (lax.axis_size(a) for a in ALL)
    plane = ny * nx
    total_users = rows * plane * nz * nc
    cross = [(k, 1 - k) for k in range(nc)]

    cols = nx * nc
    fetch = [
        (((z + SHIFT[k]) % nz) * cols + k, z * cols + k) for z in range(nz) for k in range(cols)
    ]
    turn = lambda y, x: (y * nx + x) % nz
    counts_from = [
        ((y * nz + (z + turn(y, x)) % nz) * nx + x, (y * nz + z) * nx + x)
        for y in range(ny)
        for z in range(nz)
        for x in range(nx)
    ]
    repeats = plane // nz

    item_block = lax.ppermute(bank, COLUMN, fetch)
    digits = jnp.concatenate([positives // RADIX, positives % RADIX])[None]
    labels = jnp.concatenate([cohorts, jnp.zeros_like(cohorts)])[None]
    extra = jnp.concatenate([digits, labels, jnp.zeros((6, width), jnp.int32)]).astype(BF16)
    packed = jnp.concatenate([users, extra])
    near = exchange(copies(packed, plane), PLANE)
    far = lax.ppermute(near, "c", cross)

    near_stats, near_coh, count = forward(near, item_block, rows)
    count = lax.ppermute(count, ("y", "z", "x"), counts_from)
    other_near = lax.ppermute(near_stats, "c", cross)
    far_stats, far_coh, _ = forward(far, item_block, rows)
    other_count = lax.ppermute(count, "c", cross)
    other_far = lax.ppermute(far_stats, "c", cross)
    stats = call(
        join_kernel,
        f32(plane, 2 * plane + 8, LANES),
        *(near_stats, far_stats, other_near, other_far, count, other_count),
    )
    stats = exchange(stats, PLANE)

    far_part, bank_part, lse, weight, loss = call(
        functools.partial(backward_far_kernel, rows, total_users / NCOH, repeats),
        (
            bf16(plane, width, rows),
            f32(*bank.shape),
            f32(2 * plane, LANES),
            f32(NCOH, LANES),
            f32(8, LANES),
        ),
        *(far, item_block, stats, near_coh, far_coh),
    )
    far_part = lax.ppermute(far_part, "c", cross)
    near_part, bank_part = call(
        functools.partial(backward_near_kernel, rows),
        (bf16(plane, width, rows), bf16(bank.shape[0] + 8, width)),
        *(near, item_block, lse, weight, bank_part, loss),
        scratch=[pltpu.VMEM(bank.shape, F32)],
    )
    bank_part = lax.ppermute(bank_part, COLUMN, [(b, a) for a, b in fetch])
    user_part = near_part + far_part
    user_part = exchange(user_part, PLANE)
    half = bank.shape[0] // nc
    height = half // nx
    theirs = lax.ppermute(bank_part[: half + 8], "c", cross)
    pieces = call(halve_kernel, (bf16(height + 8, width),) * nx, bank_part, theirs)
    arrived = [pieces[0]]
    for r in range(1, nx):
        arrived.append(lax.ppermute(pieces[r], "x", [(k, (k + r) % nx) for k in range(nx)]))
    bank_grad, loss = call(
        functools.partial(gather_kernel, 1.0 / total_users),
        (f32(height, width), f32(1, LANES)),
        *arrived,
    )
    user_grad = jnp.sum(user_part.astype(F32), axis=0).T
    return loss[0, 0], user_grad, bank_grad


def solution(mesh):
    torus = Mesh(mesh.devices.reshape(4, 8, 4, 2), ALL)
    return jax.shard_map(
        step,
        mesh=torus,
        in_specs=(P(ALL, None), P(("y", "z"), None), P(ALL), P(ALL)),
        out_specs=(P(), P(ALL, None), P(ALL, None)),
        check_vma=False,
    )
```

time: 134 us -> 108 us (0.81)
  the two profiles are of different devices: /device:TPU:1 before, /device:TPU:2 now
where the time goes in v4:
time: 108 us; the launch traced here: 106 us
  blocking collectives  39.1 us (36%)
  starting transfers between devices  36.1 us (33%)
  waiting for transfers between devices  16.4 us (15%)
  Pallas kernels  9.43 us (9%)
  other arithmetic  3.68 us (3%)
    all_to_all x2, blocking collectives, exchange(): return lax.all_to_all(value, axis, split_axis=0, concat_axis=0, tiled=True)  39.1 us
    pallas_call x7, Pallas kernels, call(): pl.pallas_call(kernel, in_specs=[VMEM] * len(operands), out_specs=jax.tre...  9.43 us
    ppermute x1, starting transfers between devices, step(): item_block = lax.ppermute(bank, COLUMN, fetch)  7.75 us
    ppermute x1, starting transfers between devices, step(): theirs = lax.ppermute(bank_part[:half + 8], 'c', cross)  6.45 us
    ppermute x1, waiting for transfers between devices, step(): bank_part = lax.ppermute(bank_part, COLUMN, [(b, a) for a, b in fetch])  6.32 us
    ppermute x1, starting transfers between devices, step(): other_near = lax.ppermute(near_stats, 'c', cross)  5.92 us
    all_to_all x1, starting transfers between devices, exchange(): return lax.all_to_all(value, axis, split_axis=0, concat_axis=0, tiled=True)  4.9 us
    ppermute x1, starting transfers between devices, step(): count = lax.ppermute(count, ('y', 'z', 'x'), counts_from)  4.3 us
  transfers between devices with their start and end apart: 13, of which 8 were waited for; matrix products, arithmetic and copies ran while one was open for 0% of the time, Pallas kernels for 7%

profile of v4, /device:TPU:2, one launch (start us, length us, event | category | flops | bytes accessed | tf_op | source)
XLA Modules:
  0.0 106.3 jit_solution(343586530001492867)
XLA Ops:
  2.1 0.9 maximum_maximum_fusion
  3.1 23.9 %all_to_all.15.packed = bf16[16,136,256]{2,1,0:T(8,128)(2,1)S(1)} all-to-all(bf16[16,136,256]{2,1,0:T(8,128)(2,1)S(1)} %broadcast_in_dim.21), channel_id=1, replica_groups=mesh['y'=4,'z'=8,'x'=4,'c'=2] {'y','x'}, dimensions={0} | all-to-all | bytes 2228224 | tf_op jit(solution)/shard_map/all_to_all | solution.py:52
  27.0 7.8 %collective-permute-start = (bf16[512,256]{1,0:T(8,128)(2,1)S(1)}, bf16[512,256]{1,0:T(8,128)(2,1)S(1)}, u32[]{:S(2)}, u32[]{:S(2)}) collective-permute-start(bf16[512,256]{1,0:T(8,128)(2,1)S(1)} %copy-done), channel_id=1, source_target_pairs={{0,0},{33,1},{10,2},{43,3},{60,4},{29,5},{22,6},{55,7},{8,8},{41,9... | collective-permute-start | bytes 786440 | tf_op jit(solution)/shard_map/ppermute | solution.py:278
  34.8 3.9 %collective-permute-done.bank = bf16[512,256]{1,0:T(8,128)(2,1)S(1)} collective-permute-done((bf16[512,256]{1,0:T(8,128)(2,1)S(1)}, bf16[512,256]{1,0:T(8,128)(2,1)S(1)}, u32[]{:S(2)}, u32[]{:S(2)}) %collective-permute-start) | collective-permute-done | bytes 262176 | tf_op jit(solution)/shard_map/ppermute | solution.py:278
  38.7 1.8 %shard_map.67 = (f32[24,128]{1,0:T(8,128)S(1)}, f32[16,128]{1,0:T(8,128)S(1)}, f32[8,128]{1,0:T(8,128)S(1)}) custom-call(bf16[16,136,256]{2,1,0:T(8,128)(2,1)S(1)} %all_to_all.15.packed, bf16[512,256]{1,0:T(8,128)(2,1)S(1)} %collective-permute-done.bank), custom_call_target="tpu_custom_call" | custom-call | tf_op jit(solution)/shard_map/pallas_call | solution.py:26
  40.4 5.9 %collective-permute-start.2 = (f32[24,128]{1,0:T(8,128)S(1)}, f32[24,128]{1,0:T(8,128)S(1)}, u32[]{:S(2)}, u32[]{:S(2)}) collective-permute-start(f32[24,128]{1,0:T(8,128)S(1)} %get-tuple-element.21.near), channel_id=1, source_target_pairs={{0,1},{1,0},{2,3},{3,2},{4,5},{5,4},{6,7},{7,6},{8,9},{9,8},{10,11... | collective-permute-start | bytes 36872 | tf_op jit(solution)/shard_map/ppermute | solution.py:288
  46.4 2.3 %shard_map.68 = (f32[24,128]{1,0:T(8,128)S(1)}, f32[16,128]{1,0:T(8,128)S(1)}, f32[8,128]{1,0:T(8,128)}) custom-call(bf16[16,136,256]{2,1,0:T(8,128)(2,1)S(1)} %collective-permute-done.1.packed, bf16[512,256]{1,0:T(8,128)(2,1)S(1)} %collective-permute-done.bank), custom_call_target="tpu_custom_call" | custom-call | tf_op jit(solution)/shard_map/pallas_call | solution.py:26
  48.7 4.3 %collective-permute-start.4 = (f32[8,128]{1,0:T(8,128)S(1)}, f32[8,128]{1,0:T(8,128)S(1)}, u32[]{:S(2)}, u32[]{:S(2)}) collective-permute-start(f32[8,128]{1,0:T(8,128)S(1)} %get-tuple-element.23), channel_id=1, source_target_pairs={{0,0},{10,2},{20,4},{30,6},{8,8},{18,10},{28,12},{38,14},{16,16},{... | collective-permute-start | bytes 12296 | tf_op jit(solution)/shard_map/ppermute | solution.py:287
  53.0 1.3 %collective-permute-done.4.count = f32[8,128]{1,0:T(8,128)S(1)} collective-permute-done((f32[8,128]{1,0:T(8,128)S(1)}, f32[8,128]{1,0:T(8,128)S(1)}, u32[]{:S(2)}, u32[]{:S(2)}) %collective-permute-start.4) | collective-permute-done | bytes 4128 | tf_op jit(solution)/shard_map/ppermute | solution.py:287
  54.3 1.2 %collective-permute-done.5.other_count = f32[8,128]{1,0:T(8,128)S(1)} collective-permute-done((f32[8,128]{1,0:T(8,128)S(1)}, f32[8,128]{1,0:T(8,128)S(1)}, u32[]{:S(2)}, u32[]{:S(2)}) %collective-permute-start.5) | collective-permute-done | bytes 4128 | tf_op jit(solution)/shard_map/ppermute | solution.py:290
  55.5 15.2 %all_to_all.16.stats = f32[16,40,128]{2,1,0:T(8,128)S(1)} all-to-all(f32[16,40,128]{2,1,0:T(8,128)S(1)} %shard_map.69), channel_id=1, replica_groups=mesh['y'=4,'z'=8,'x'=4,'c'=2] {'y','x'}, dimensions={0} | all-to-all | bytes 655360 | tf_op jit(solution)/shard_map/all_to_all | solution.py:52
  70.7 2.3 %shard_map.70 = (bf16[16,256,128]{2,1,0:T(8,128)(2,1)S(1)}, f32[512,256]{1,0:T(8,128)S(1)}, f32[32,128]{1,0:T(8,128)S(1)}, f32[16,128]{1,0:T(8,128)S(1)}, f32[8,128]{1,0:T(8,128)S(1)}) custom-call(bf16[16,136,256]{2,1,0:T(8,128)(2,1)S(1)} %collective-permute-done.1.packed, bf16[512,256]{1,0:T(8,128)(2,1)S(1)} %collective-permute-done.bank, ...), custom_call_target="tpu_custom_call" | custom-call | tf_op jit(solution)/shard_map/pallas_call | solution.py:26
  73.0 2.4 %shard_map.71 = (bf16[16,256,128]{2,1,0:T(8,128)(2,1)S(1)}, bf16[520,256]{1,0:T(8,128)(2,1)S(1)}) custom-call(bf16[16,136,256]{2,1,0:T(8,128)(2,1)S(1)} %all_to_all.15.packed, bf16[512,256]{1,0:T(8,128)(2,1)S(1)} %collective-permute-done.bank, f32[32,128]{1,0:T(8,128)S(1)} %get-tuple-element.26.lse, f32[16,128]{1,0:T(8,128)S(1)} %get-tuple-element.27.weight, ...), custom_call_target="tpu_custom_call" | custom-call | tf_op jit(solution)/shard_map/pallas_call | solution.py:26
  75.7 1.3 %add.13 = bf16[16,256,128]{2,1,0:T(8,128)(2,1)} add(bf16[16,256,128]{2,1,0:T(8,128)(2,1)S(1)} %get-tuple-element.36, bf16[16,256,128]{2,1,0:T(8,128)(2,1)S(1)} %collective-permute-done.11) | non-fusion elementwise | flops 524288 | bytes 3145728 | tf_op jit(solution)/shard_map/add | solution.py:318
  77.0 4.9 %all-to-all-start.2 = ((bf16[16,256,128]{2,1,0:T(8,128)(2,1)}), bf16[16,256,128]{2,1,0:T(8,128)(2,1)S(1)}, u32[]{:S(2)}, u32[]{:S(2)}) async-start(bf16[16,256,128]{2,1,0:T(8,128)(2,1)} %add.13), calls=%async_computation.2 | async-start | bytes 2097152 | tf_op jit(solution)/shard_map/all_to_all | solution.py:52
  81.9 3.2 %collective-permute-start.6 = (bf16[520,256]{1,0:T(8,128)(2,1)S(1)}, bf16[520,256]{1,0:T(8,128)(2,1)S(1)}, u32[]{:S(2)}, u32[]{:S(2)}) collective-permute-start(bf16[520,256]{1,0:T(8,128)(2,1)S(1)} %get-tuple-element.30), channel_id=1, source_target_pairs={{0,0},{1,33},{2,10},{3,43},{4,60},{5,29},{6,22},{7,55},{8,8},{9,41... | collective-permute-start | bytes 798728 | tf_op jit(solution)/shard_map/ppermute | solution.py:317
  85.1 6.3 %collective-permute-done.6.mine = bf16[520,256]{1,0:T(8,128)(2,1)S(1)} collective-permute-done((bf16[520,256]{1,0:T(8,128)(2,1)S(1)}, bf16[520,256]{1,0:T(8,128)(2,1)S(1)}, u32[]{:S(2)}, u32[]{:S(2)}) %collective-permute-start.6) | collective-permute-done | bytes 266272 | tf_op jit(solution)/shard_map/ppermute | solution.py:317
  91.4 6.4 %collective-permute-start.7 = (bf16[264,256]{1,0:T(8,128)(2,1)S(1)}, bf16[264,256]{1,0:T(8,128)(2,1)S(1)}, u32[]{:S(2)}, u32[]{:S(2)}) collective-permute-start(bf16[264,256]{1,0:T(8,128)(2,1)S(1)} %slice.8), channel_id=1, source_target_pairs={{0,1},{1,0},{2,3},{3,2},{4,5},{5,4},{6,7},{7,6},{8,9},{9,8},{10,11... | collective-permute-start | bytes 405512 | tf_op jit(solution)/shard_map/ppermute | solution.py:322
  97.8 1.0 collective-permute-done.7.theirs
  99.0 0.8 collective-permute-start.9
  99.8 2.5 %collective-permute-start.10 = (bf16[72,256]{1,0:T(8,128)(2,1)S(1)}, bf16[72,256]{1,0:T(8,128)(2,1)S(1)}, u32[]{:S(2)}, u32[]{:S(2)}) collective-permute-start(bf16[72,256]{1,0:T(8,128)(2,1)S(1)} %get-tuple-element.34), channel_id=1, source_target_pairs={{0,6},{2,0},{4,2},{6,4},{1,7},{3,1},{5,3},{7,5},{8,14},{10,8},{12,... | collective-permute-start | bytes 110600 | tf_op jit(solution)/shard_map/ppermute | solution.py:326
  102.3 0.7 collective-permute-done.8.refs_1_
  103.1 1.7 %collective-permute-done.9.refs_2_ = bf16[72,256]{1,0:T(8,128)(2,1)S(1)} collective-permute-done((bf16[72,256]{1,0:T(8,128)(2,1)S(1)}, bf16[72,256]{1,0:T(8,128)(2,1)S(1)}, u32[]{:S(2)}, u32[]{:S(2)}) %collective-permute-start.9) | collective-permute-done | bytes 36896 | tf_op jit(solution)/shard_map/ppermute | solution.py:326
  105.6 0.8 copy.7
  (27 shorter events, 2.9 us)
Async XLA Ops:
  3.1 23.9 %copy-start = (bf16[512,256]{1,0:T(8,128)(2,1)S(1)}, bf16[512,256]{1,0:T(8,128)(2,1)}, u32[]{:S(2)}) copy-start(bf16[512,256]{1,0:T(8,128)(2,1)} %param.5) | copy-start | bytes 786436
  27.0 19.3 %collective-permute-start.1 = (bf16[16,136,256]{2,1,0:T(8,128)(2,1)S(1)}, bf16[16,136,256]{2,1,0:T(8,128)(2,1)S(1)}, u32[]{:S(2)}, u32[]{:S(2)}) collective-permute-start(bf16[16,136,256]{2,1,0:T(8,128)(2,1)S(1)} %all_to_all.15.packed), channel_id=1, source_target_pairs={{0,1},{1,0},{2,3},{3,2},{4,5},{5,4},{6,7},{7,6},{8,9},{9,8},{10,11... | collective-permute-start | bytes 3342344 | tf_op jit(solution)/shard_map/ppermute | solution.py:284
  27.0 11.6 %collective-permute-start = (bf16[512,256]{1,0:T(8,128)(2,1)S(1)}, bf16[512,256]{1,0:T(8,128)(2,1)S(1)}, u32[]{:S(2)}, u32[]{:S(2)}) collective-permute-start(bf16[512,256]{1,0:T(8,128)(2,1)S(1)} %copy-done), channel_id=1, source_target_pairs={{0,0},{33,1},{10,2},{43,3},{60,4},{29,5},{22,6},{55,7},{8,8},{41,9... | collective-permute-start | bytes 786440 | tf_op jit(solution)/shard_map/ppermute | solution.py:278
  40.4 15.0 %collective-permute-start.2 = (f32[24,128]{1,0:T(8,128)S(1)}, f32[24,128]{1,0:T(8,128)S(1)}, u32[]{:S(2)}, u32[]{:S(2)}) collective-permute-start(f32[24,128]{1,0:T(8,128)S(1)} %get-tuple-element.21.near), channel_id=1, source_target_pairs={{0,1},{1,0},{2,3},{3,2},{4,5},{5,4},{6,7},{7,6},{8,9},{9,8},{10,11... | collective-permute-start | bytes 36872 | tf_op jit(solution)/shard_map/ppermute | solution.py:288
  48.7 6.8 %collective-permute-start.3 = (f32[24,128]{1,0:T(8,128)S(1)}, f32[24,128]{1,0:T(8,128)S(1)}, u32[]{:S(2)}, u32[]{:S(2)}) collective-permute-start(f32[24,128]{1,0:T(8,128)S(1)} %get-tuple-element.22.far), channel_id=1, source_target_pairs={{0,1},{1,0},{2,3},{3,2},{4,5},{5,4},{6,7},{7,6},{8,9},{9,8},{10,11... | collective-permute-start | bytes 36872 | tf_op jit(solution)/shard_map/ppermute | solution.py:291
  48.7 5.6 %collective-permute-start.4 = (f32[8,128]{1,0:T(8,128)S(1)}, f32[8,128]{1,0:T(8,128)S(1)}, u32[]{:S(2)}, u32[]{:S(2)}) collective-permute-start(f32[8,128]{1,0:T(8,128)S(1)} %get-tuple-element.23), channel_id=1, source_target_pairs={{0,0},{10,2},{20,4},{30,6},{8,8},{18,10},{28,12},{38,14},{16,16},{... | collective-permute-start | bytes 12296 | tf_op jit(solution)/shard_map/ppermute | solution.py:287
  54.3 1.2 %collective-permute-start.5 = (f32[8,128]{1,0:T(8,128)S(1)}, f32[8,128]{1,0:T(8,128)S(1)}, u32[]{:S(2)}, u32[]{:S(2)}) collective-permute-start(f32[8,128]{1,0:T(8,128)S(1)} %collective-permute-done.4.count), channel_id=1, source_target_pairs={{0,1},{1,0},{2,3},{3,2},{4,5},{5,4},{6,7},{7,6},{8,9},{9,8},{10,11... | collective-permute-start | bytes 12296 | tf_op jit(solution)/shard_map/ppermute | solution.py:290
  72.9 2.7 %collective-permute-start.11 = (bf16[16,256,128]{2,1,0:T(8,128)(2,1)S(1)}, bf16[16,256,128]{2,1,0:T(8,128)(2,1)S(1)}, u32[]{:S(2)}, u32[]{:S(2)}) collective-permute-start(bf16[16,256,128]{2,1,0:T(8,128)(2,1)S(1)} %get-tuple-element.37), channel_id=1, source_target_pairs={{0,1},{1,0},{2,3},{3,2},{4,5},{5,4},{6,7},{7,6},{8,9},{9,8},{10,11... | collective-permute-start | bytes 3145736 | tf_op jit(solution)/shard_map/ppermute | solution.py:310
  77.0 28.5 %all-to-all-start.2 = ((bf16[16,256,128]{2,1,0:T(8,128)(2,1)}), bf16[16,256,128]{2,1,0:T(8,128)(2,1)S(1)}, u32[]{:S(2)}, u32[]{:S(2)}) async-start(bf16[16,256,128]{2,1,0:T(8,128)(2,1)} %add.13), calls=%async_computation.2 | async-start | bytes 2097152 | tf_op jit(solution)/shard_map/all_to_all | solution.py:52
  81.9 9.5 %collective-permute-start.6 = (bf16[520,256]{1,0:T(8,128)(2,1)S(1)}, bf16[520,256]{1,0:T(8,128)(2,1)S(1)}, u32[]{:S(2)}, u32[]{:S(2)}) collective-permute-start(bf16[520,256]{1,0:T(8,128)(2,1)S(1)} %get-tuple-element.30), channel_id=1, source_target_pairs={{0,0},{1,33},{2,10},{3,43},{4,60},{5,29},{6,22},{7,55},{8,8},{9,41... | collective-permute-start | bytes 798728 | tf_op jit(solution)/shard_map/ppermute | solution.py:317
  91.4 7.4 %collective-permute-start.7 = (bf16[264,256]{1,0:T(8,128)(2,1)S(1)}, bf16[264,256]{1,0:T(8,128)(2,1)S(1)}, u32[]{:S(2)}, u32[]{:S(2)}) collective-permute-start(bf16[264,256]{1,0:T(8,128)(2,1)S(1)} %slice.8), channel_id=1, source_target_pairs={{0,1},{1,0},{2,3},{3,2},{4,5},{5,4},{6,7},{7,6},{8,9},{9,8},{10,11... | collective-permute-start | bytes 405512 | tf_op jit(solution)/shard_map/ppermute | solution.py:322
  98.9 4.2 %collective-permute-start.8 = (bf16[72,256]{1,0:T(8,128)(2,1)S(1)}, bf16[72,256]{1,0:T(8,128)(2,1)S(1)}, u32[]{:S(2)}, u32[]{:S(2)}) collective-permute-start(bf16[72,256]{1,0:T(8,128)(2,1)S(1)} %get-tuple-element.32), channel_id=1, source_target_pairs={{0,2},{2,4},{4,6},{6,0},{1,3},{3,5},{5,7},{7,1},{8,10},{10,12},{12... | collective-permute-start | bytes 110600 | tf_op jit(solution)/shard_map/ppermute | solution.py:326
  99.0 5.8 %collective-permute-start.9 = (bf16[72,256]{1,0:T(8,128)(2,1)S(1)}, bf16[72,256]{1,0:T(8,128)(2,1)S(1)}, u32[]{:S(2)}, u32[]{:S(2)}) collective-permute-start(bf16[72,256]{1,0:T(8,128)(2,1)S(1)} %get-tuple-element.33), channel_id=1, source_target_pairs={{0,4},{2,6},{4,0},{6,2},{1,5},{3,7},{5,1},{7,3},{8,12},{10,14},{12... | collective-permute-start | bytes 110600 | tf_op jit(solution)/shard_map/ppermute | solution.py:326
  99.8 5.0 %collective-permute-start.10 = (bf16[72,256]{1,0:T(8,128)(2,1)S(1)}, bf16[72,256]{1,0:T(8,128)(2,1)S(1)}, u32[]{:S(2)}, u32[]{:S(2)}) collective-permute-start(bf16[72,256]{1,0:T(8,128)(2,1)S(1)} %get-tuple-element.34), channel_id=1, source_target_pairs={{0,6},{2,0},{4,2},{6,4},{1,7},{3,1},{5,3},{7,5},{8,14},{10,8},{12,... | collective-permute-start | bytes 110600 | tf_op jit(solution)/shard_map/ppermute | solution.py:326

commit v5 on v4

--- a/solution.py
+++ b/solution.py
@@ -22,14 +22,14 @@
 VMEM = pl.BlockSpec(memory_space=pltpu.VMEM)
 
 
-def call(kernel, out_shape, *operands, scratch=()):
+def call(kernel, out_shape, *operands, scratch=(), limit=24 << 20):
     return pl.pallas_call(
         kernel,
         in_specs=[VMEM] * len(operands),
         out_specs=jax.tree.map(lambda _: VMEM, out_shape),
         out_shape=out_shape,
         scratch_shapes=list(scratch),
-        compiler_params=pltpu.CompilerParams(vmem_limit_bytes=24 << 20),
+        compiler_params=pltpu.CompilerParams(vmem_limit_bytes=limit),
     )(*operands)
 
 
@@ -52,10 +52,6 @@
     return lax.all_to_all(value, axis, split_axis=0, concat_axis=0, tiled=True)
 
 
-def copies(value, n):
-    return jnp.broadcast_to(value[None], (n, *value.shape))
-
-
 def scores(bank, users):
     return lax.dot_general(bank, users, (((1,), (1,)), ((), ())), preferred_element_type=F32)
 
@@ -98,11 +94,28 @@
     return jnp.sum(spread, axis=1, keepdims=True)
 
 
-def forward_kernel(rows, packed, bank, stats, coh, counts):
+def pack_kernel(users, positives, cohorts, out, count):
+    rows, _ = users.shape
+    pos = positives[...]
+    high = (pos // RADIX).astype(F32)
+    low = (pos % RADIX).astype(F32)
+    mine = cohorts[...].astype(F32)
+    row = iota((8, LANES), 0)
+    left = jnp.where(row == 0, high, jnp.where(row == 1, mine, F32(0))).astype(BF16)
+    right = jnp.where(row == 0, low, F32(0)).astype(BF16)
+    for k in range(out.shape[0]):
+        out[k, :rows, :] = users[...]
+        out[k, rows:, :LANES] = left
+        out[k, rows:, LANES:] = right
+    ids = iota((NCOH, LANES), 0).astype(F32)
+    column = jnp.sum(jnp.where(ids == mine, F32(1), F32(0)), axis=1, keepdims=True)
+    count[...] = jnp.broadcast_to(column_to_row(column), (8, LANES))
+
+
+def forward_kernel(rows, packed, bank, stats, coh):
     shards = packed.shape[0]
     first = first_item(bank.shape[0])
     positive = jnp.zeros((NCOH, 1), F32)
-    count = jnp.zeros((NCOH, 1), F32)
     for at in range(0, shards, STEP):
         logits = scores(bank[...], shard_users(packed, at, rows))
         top = jnp.max(logits, axis=0, keepdims=True)
@@ -113,22 +126,20 @@
         mine = cohort_row(packed, at, rows, 0)
         ids = iota((NCOH, mine.shape[1]), 0).astype(F32)
         positive += jnp.sum(jnp.where(ids == mine, own, F32(0)), axis=1, keepdims=True)
-        count += jnp.sum(jnp.where(ids == mine, F32(1), F32(0)), axis=1, keepdims=True)
         for s in range(STEP):
             cut = slice(s * LANES, (s + 1) * LANES)
             stats[at + s : at + s + 1, :] = lse[:, cut]
             coh[at + s : at + s + 1, :] = mine[:, cut]
     stats[shards:, :] = jnp.broadcast_to(column_to_row(positive), (8, LANES))
-    counts[...] = jnp.broadcast_to(column_to_row(count), (8, LANES))
 
 
 def forward(packed, bank, rows):
     shards = packed.shape[0]
-    shapes = (f32(shards + 8, LANES), f32(shards, LANES), f32(8, LANES))
+    shapes = (f32(shards + 8, LANES), f32(shards, LANES))
     return call(functools.partial(forward_kernel, rows), shapes, packed, bank)
 
 
-def join_kernel(near, far, other_near, other_far, count, other_count, out):
+def join_kernel(near, far, other_near, other_far, count, out):
     shards = near.shape[0] - 8
 
     def join(a, b):
@@ -138,14 +149,14 @@
     first = join(near[:shards], other_far[:shards])
     second = join(far[:shards], other_near[:shards])
     positive = near[shards:] + far[shards:] + other_near[shards:] + other_far[shards:]
-    extra = jnp.where(iota(positive.shape, 0) == 0, positive, count[...] + other_count[...])
+    extra = jnp.where(iota(positive.shape, 0) == 0, positive, count[...])
     for k in range(out.shape[0]):
         out[k, :shards] = first
         out[k, shards : 2 * shards] = second
         out[k, 2 * shards :] = extra
 
 
-def settle(scale, repeats, stats, coh_near, coh_far, lse_out, weight_out, loss_out):
+def settle(scale, stats, coh_near, coh_far, lse_out, weight_out, loss_out):
     shards = coh_near.shape[0]
     both = 2 * shards
     top = stats[0, :both]
@@ -158,7 +169,7 @@
         rest += stats[k, both:]
     lse = top + jnp.log(total)
     lse_out[...] = lse
-    per_cohort = scale * repeats / row_to_column(rest[1:2])
+    per_cohort = scale / row_to_column(rest[1:2])
     weight_out[...] = jnp.broadcast_to(per_cohort, weight_out.shape)
     weights = jnp.zeros((both, LANES), F32)
     cohorts = jnp.concatenate([coh_near[...], coh_far[...]], axis=0)
@@ -192,9 +203,9 @@
     return total
 
 
-def backward_far_kernel(rows, scale, repeats, packed, bank, stats, coh_near, coh_far, *outs):
+def backward_far_kernel(rows, scale, packed, bank, stats, coh_near, coh_far, *outs):
     user_part, bank_part, lse, weight, loss = outs
-    settle(scale, repeats, stats, coh_near, coh_far, lse, weight, loss)
+    settle(scale, stats, coh_near, coh_far, lse, weight, loss)
     bank_part[...] = backward_core(rows, 1, packed, bank, lse, weight, user_part, None)
 
 
@@ -266,38 +277,32 @@
     fetch = [
         (((z + SHIFT[k]) % nz) * cols + k, z * cols + k) for z in range(nz) for k in range(cols)
     ]
-    turn = lambda y, x: (y * nx + x) % nz
-    counts_from = [
-        ((y * nz + (z + turn(y, x)) % nz) * nx + x, (y * nz + z) * nx + x)
-        for y in range(ny)
-        for z in range(nz)
-        for x in range(nx)
-    ]
-    repeats = plane // nz
-
+    packed, count = call(
+        pack_kernel,
+        (bf16(plane, rows + 8, width), f32(8, LANES)),
+        *(users, positives[None], cohorts[None]),
+        limit=None,
+    )
+    near = exchange(packed, PLANE)
     item_block = lax.ppermute(bank, COLUMN, fetch)
-    digits = jnp.concatenate([positives // RADIX, positives % RADIX])[None]
-    labels = jnp.concatenate([cohorts, jnp.zeros_like(cohorts)])[None]
-    extra = jnp.concatenate([digits, labels, jnp.zeros((6, width), jnp.int32)]).astype(BF16)
-    packed = jnp.concatenate([users, extra])
-    near = exchange(copies(packed, plane), PLANE)
+    for axis, by in (("z", 1), ("z", 2), ("z", 4), ("c", 1)):
+        ways = [(k, k ^ by) for k in range(lax.axis_size(axis))]
+        count = count + lax.ppermute(count, axis, ways)
     far = lax.ppermute(near, "c", cross)
 
-    near_stats, near_coh, count = forward(near, item_block, rows)
-    count = lax.ppermute(count, ("y", "z", "x"), counts_from)
+    near_stats, near_coh = forward(near, item_block, rows)
     other_near = lax.ppermute(near_stats, "c", cross)
-    far_stats, far_coh, _ = forward(far, item_block, rows)
-    other_count = lax.ppermute(count, "c", cross)
+    far_stats, far_coh = forward(far, item_block, rows)
     other_far = lax.ppermute(far_stats, "c", cross)
     stats = call(
         join_kernel,
         f32(plane, 2 * plane + 8, LANES),
-        *(near_stats, far_stats, other_near, other_far, count, other_count),
+        *(near_stats, far_stats, other_near, other_far, count),
     )
     stats = exchange(stats, PLANE)
 
     far_part, bank_part, lse, weight, loss = call(
-        functools.partial(backward_far_kernel, rows, total_users / NCOH, repeats),
+        functools.partial(backward_far_kernel, rows, total_users / NCOH),
         (
             bf16(plane, width, rows),
             f32(*bank.shape),

time: 108 us -> 108 us (level)
  waiting for transfers between devices: 16.4 us -> 18.7 us
  other arithmetic: 3.68 us -> 1.45 us
  blocking collectives: 39.1 us -> 37.2 us
  Pallas kernels: 9.43 us -> 10.9 us
    ppermute x2 -> x4, waiting for transfers between devices: 2.47 us -> 7.79 us  [step(): count = count + lax.ppermute(count, axis, ways)]
    ppermute x1, waiting for transfers between devices: 3.87 us -> 0.06 us  [step(): item_block = lax.ppermute(bank, COLUMN, fetch)]
    all_to_all x2, blocking collectives: 39.1 us -> 37.2 us  [exchange(): return lax.all_to_all(value, axis, split_axis=0, concat_axis=0, tiled=True)]
    pallas_call x7 -> x8, Pallas kernels: 9.43 us -> 10.9 us  [call(): pl.pallas_call(kernel, in_specs=[VMEM] * len(operands), out_specs=jax.tre...]
    another operation x2 -> x0, other arithmetic: 1.33 us -> none
    ppermute x3, waiting for transfers between devices: 2.45 us -> 3.68 us  [step(): lax.ppermute(pieces[r], 'x', [(k, (k + r) % nx) for k in range(nx)])]
    ppermute x2 -> x4, starting transfers between devices: 4.3 us -> 4.77 us  [step(): count = count + lax.ppermute(count, axis, ways)]
  transfers between devices with their start and end apart: 13 -> 15, of which waited for: 8 -> 9; matrix products, arithmetic and copies ran while one was open for 0% -> 0% of each run, Pallas kernels for 7% -> 6%
where the time goes in v5:
time: 108 us; the launch traced here: 106 us
  blocking collectives  37.2 us (34%)
  starting transfers between devices  36.3 us (34%)
  waiting for transfers between devices  18.7 us (17%)
  Pallas kernels  10.9 us (10%)
  other arithmetic  1.45 us (1%)
    all_to_all x2, blocking collectives, exchange(): return lax.all_to_all(value, axis, split_axis=0, concat_axis=0, tiled=True)  37.2 us
    pallas_call x8, Pallas kernels, call(): pl.pallas_call(kernel, in_specs=[VMEM] * len(operands), out_specs=jax.tre...  10.9 us
    ppermute x4, waiting for transfers between devices, step(): count = count + lax.ppermute(count, axis, ways)  7.79 us
    ppermute x1, starting transfers between devices, step(): item_block = lax.ppermute(bank, COLUMN, fetch)  7.75 us
    ppermute x1, starting transfers between devices, step(): theirs = lax.ppermute(bank_part[:half + 8], 'c', cross)  6.31 us
    ppermute x1, starting transfers between devices, step(): other_near = lax.ppermute(near_stats, 'c', cross)  6.04 us
    ppermute x1, waiting for transfers between devices, step(): bank_part = lax.ppermute(bank_part, COLUMN, [(b, a) for a, b in fetch])  5.9 us
    all_to_all x1, starting transfers between devices, exchange(): return lax.all_to_all(value, axis, split_axis=0, concat_axis=0, tiled=True)  4.91 us
  transfers between devices with their start and end apart: 15, of which 9 were waited for; matrix products, arithmetic and copies ran while one was open for 0% of the time, Pallas kernels for 6%

profile of v5, /device:TPU:2, one launch (start us, length us, event | category | flops | bytes accessed | tf_op | source)
XLA Modules:
  0.0 106.0 jit_solution(8116856116627801491)
XLA Ops:
  0.6 2.0 %shard_map.67 = (bf16[16,136,256]{2,1,0:T(8,128)(2,1)}, f32[8,128]{1,0:T(8,128)}) custom-call(bf16[128,256]{1,0:T(8,128)(2,1)} %users.1, s32[1,128]{1,0:T(1,128)} %bitcast.6, s32[1,128]{1,0:T(1,128)} %bitcast.7), custom_call_target="tpu_custom_call" | custom-call | tf_op jit(solution)/shard_map/pallas_call | solution.py:26
  2.6 24.1 %all_to_all.15.packed = bf16[16,136,256]{2,1,0:T(8,128)(2,1)S(1)} all-to-all(bf16[16,136,256]{2,1,0:T(8,128)(2,1)} %get-tuple-element.22), channel_id=1, replica_groups=mesh['y'=4,'z'=8,'x'=4,'c'=2] {'y','x'}, dimensions={0} | all-to-all | bytes 2228224 | tf_op jit(solution)/shard_map/all_to_all | solution.py:52
  26.7 7.8 %collective-permute-start = (bf16[512,256]{1,0:T(8,128)(2,1)S(1)}, bf16[512,256]{1,0:T(8,128)(2,1)S(1)}, u32[]{:S(2)}, u32[]{:S(2)}) collective-permute-start(bf16[512,256]{1,0:T(8,128)(2,1)S(1)} %copy-done.1), channel_id=1, source_target_pairs={{0,0},{33,1},{10,2},{43,3},{60,4},{29,5},{22,6},{55,7},{8,8},{41,9... | collective-permute-start | bytes 786440 | tf_op jit(solution)/shard_map/ppermute | solution.py:287
  34.6 3.6 %collective-permute-done.4 = f32[8,128]{1,0:T(8,128)S(1)} collective-permute-done((f32[8,128]{1,0:T(8,128)S(1)}, f32[8,128]{1,0:T(8,128)S(1)}, u32[]{:S(2)}, u32[]{:S(2)}) %collective-permute-start.4) | collective-permute-done | bytes 4128 | tf_op jit(solution)/shard_map/ppermute | solution.py:290
  38.4 1.8 %shard_map.68 = (f32[24,128]{1,0:T(8,128)S(1)}, f32[16,128]{1,0:T(8,128)S(1)}) custom-call(bf16[16,136,256]{2,1,0:T(8,128)(2,1)S(1)} %all_to_all.15.packed, bf16[512,256]{1,0:T(8,128)(2,1)S(1)} %collective-permute-done.bank), custom_call_target="tpu_custom_call" | custom-call | tf_op jit(solution)/shard_map/pallas_call | solution.py:26
  40.1 6.0 %collective-permute-start.2 = (f32[24,128]{1,0:T(8,128)S(1)}, f32[24,128]{1,0:T(8,128)S(1)}, u32[]{:S(2)}, u32[]{:S(2)}) collective-permute-start(f32[24,128]{1,0:T(8,128)S(1)} %get-tuple-element.23.near), channel_id=1, source_target_pairs={{0,1},{1,0},{2,3},{3,2},{4,5},{5,4},{6,7},{7,6},{8,9},{9,8},{10,11... | collective-permute-start | bytes 36872 | tf_op jit(solution)/shard_map/ppermute | solution.py:294
  46.2 1.8 %shard_map.69 = (f32[24,128]{1,0:T(8,128)S(1)}, f32[16,128]{1,0:T(8,128)S(1)}) custom-call(bf16[16,136,256]{2,1,0:T(8,128)(2,1)S(1)} %collective-permute-done.1.packed, bf16[512,256]{1,0:T(8,128)(2,1)S(1)} %collective-permute-done.bank), custom_call_target="tpu_custom_call" | custom-call | tf_op jit(solution)/shard_map/pallas_call | solution.py:26
  48.1 4.6 %collective-permute-start.6 = (f32[8,128]{1,0:T(8,128)S(1)}, f32[8,128]{1,0:T(8,128)S(1)}, u32[]{:S(2)}, u32[]{:S(2)}) collective-permute-start(f32[8,128]{1,0:T(8,128)S(1)} %add.16), channel_id=1, source_target_pairs={{0,32},{8,40},{16,48},{24,56},{32,0},{40,8},{48,16},{56,24},{1,33}... | collective-permute-start | bytes 12296 | tf_op jit(solution)/shard_map/ppermute | solution.py:290
  52.6 3.0 %collective-permute-done.6 = f32[8,128]{1,0:T(8,128)S(1)} collective-permute-done((f32[8,128]{1,0:T(8,128)S(1)}, f32[8,128]{1,0:T(8,128)S(1)}, u32[]{:S(2)}, u32[]{:S(2)}) %collective-permute-start.6) | collective-permute-done | bytes 4128 | tf_op jit(solution)/shard_map/ppermute | solution.py:290
  55.7 1.2 %collective-permute-done.7 = f32[8,128]{1,0:T(8,128)S(1)} collective-permute-done((f32[8,128]{1,0:T(8,128)S(1)}, f32[8,128]{1,0:T(8,128)S(1)}, u32[]{:S(2)}, u32[]{:S(2)}) %collective-permute-start.7) | collective-permute-done | bytes 4128 | tf_op jit(solution)/shard_map/ppermute | solution.py:290
  56.9 13.1 %all_to_all.16.stats = f32[16,40,128]{2,1,0:T(8,128)S(1)} all-to-all(f32[16,40,128]{2,1,0:T(8,128)S(1)} %shard_map.70), channel_id=1, replica_groups=mesh['y'=4,'z'=8,'x'=4,'c'=2] {'y','x'}, dimensions={0} | all-to-all | bytes 655360 | tf_op jit(solution)/shard_map/all_to_all | solution.py:52
  70.0 2.3 %shard_map.71 = (bf16[16,256,128]{2,1,0:T(8,128)(2,1)S(1)}, f32[512,256]{1,0:T(8,128)S(1)}, f32[32,128]{1,0:T(8,128)S(1)}, f32[16,128]{1,0:T(8,128)S(1)}, f32[8,128]{1,0:T(8,128)S(1)}) custom-call(bf16[16,136,256]{2,1,0:T(8,128)(2,1)S(1)} %collective-permute-done.1.packed, bf16[512,256]{1,0:T(8,128)(2,1)S(1)} %collective-permute-done.bank, ...), custom_call_target="tpu_custom_call" | custom-call | tf_op jit(solution)/shard_map/pallas_call | solution.py:26
  72.5 2.3 %shard_map.72 = (bf16[16,256,128]{2,1,0:T(8,128)(2,1)S(1)}, bf16[520,256]{1,0:T(8,128)(2,1)S(1)}) custom-call(bf16[16,136,256]{2,1,0:T(8,128)(2,1)S(1)} %all_to_all.15.packed, bf16[512,256]{1,0:T(8,128)(2,1)S(1)} %collective-permute-done.bank, f32[32,128]{1,0:T(8,128)S(1)} %get-tuple-element.28.lse, f32[16,128]{1,0:T(8,128)S(1)} %get-tuple-element.29.weight, ...), custom_call_target="tpu_custom_call" | custom-call | tf_op jit(solution)/shard_map/pallas_call | solution.py:26
  75.2 1.3 %add.19 = bf16[16,256,128]{2,1,0:T(8,128)(2,1)} add(bf16[16,256,128]{2,1,0:T(8,128)(2,1)S(1)} %get-tuple-element.38, bf16[16,256,128]{2,1,0:T(8,128)(2,1)S(1)} %collective-permute-done.13) | non-fusion elementwise | flops 524288 | bytes 3145728 | tf_op jit(solution)/shard_map/add | solution.py:323
  76.5 4.9 %all-to-all-start.2 = ((bf16[16,256,128]{2,1,0:T(8,128)(2,1)}), bf16[16,256,128]{2,1,0:T(8,128)(2,1)S(1)}, u32[]{:S(2)}, u32[]{:S(2)}) async-start(bf16[16,256,128]{2,1,0:T(8,128)(2,1)} %add.19), calls=%async_computation.2 | async-start | bytes 2097152 | tf_op jit(solution)/shard_map/all_to_all | solution.py:52
  81.4 3.6 %collective-permute-start.8 = (bf16[520,256]{1,0:T(8,128)(2,1)S(1)}, bf16[520,256]{1,0:T(8,128)(2,1)S(1)}, u32[]{:S(2)}, u32[]{:S(2)}) collective-permute-start(bf16[520,256]{1,0:T(8,128)(2,1)S(1)} %get-tuple-element.32), channel_id=1, source_target_pairs={{0,0},{1,33},{2,10},{3,43},{4,60},{5,29},{6,22},{7,55},{8,8},{9,41... | collective-permute-start | bytes 798728 | tf_op jit(solution)/shard_map/ppermute | solution.py:322
  85.0 5.9 %collective-permute-done.8.mine = bf16[520,256]{1,0:T(8,128)(2,1)S(1)} collective-permute-done((bf16[520,256]{1,0:T(8,128)(2,1)S(1)}, bf16[520,256]{1,0:T(8,128)(2,1)S(1)}, u32[]{:S(2)}, u32[]{:S(2)}) %collective-permute-start.8) | collective-permute-done | bytes 266272 | tf_op jit(solution)/shard_map/ppermute | solution.py:322
  90.9 6.3 %collective-permute-start.9 = (bf16[264,256]{1,0:T(8,128)(2,1)S(1)}, bf16[264,256]{1,0:T(8,128)(2,1)S(1)}, u32[]{:S(2)}, u32[]{:S(2)}) collective-permute-start(bf16[264,256]{1,0:T(8,128)(2,1)S(1)} %slice.8), channel_id=1, source_target_pairs={{0,1},{1,0},{2,3},{3,2},{4,5},{5,4},{6,7},{7,6},{8,9},{9,8},{10,11... | collective-permute-start | bytes 405512 | tf_op jit(solution)/shard_map/ppermute | solution.py:327
  97.2 1.0 collective-permute-done.9.theirs
  98.6 2.2 %collective-permute-start.12 = (bf16[72,256]{1,0:T(8,128)(2,1)S(1)}, bf16[72,256]{1,0:T(8,128)(2,1)S(1)}, u32[]{:S(2)}, u32[]{:S(2)}) collective-permute-start(bf16[72,256]{1,0:T(8,128)(2,1)S(1)} %get-tuple-element.36), channel_id=1, source_target_pairs={{0,6},{2,0},{4,2},{6,4},{1,7},{3,1},{5,3},{7,5},{8,14},{10,8},{12,... | collective-permute-start | bytes 110600 | tf_op jit(solution)/shard_map/ppermute | solution.py:331
  100.7 1.7 %collective-permute-done.10.refs_1_ = bf16[72,256]{1,0:T(8,128)(2,1)S(1)} collective-permute-done((bf16[72,256]{1,0:T(8,128)(2,1)S(1)}, bf16[72,256]{1,0:T(8,128)(2,1)S(1)}, u32[]{:S(2)}, u32[]{:S(2)}) %collective-permute-start.10) | collective-permute-done | bytes 36896 | tf_op jit(solution)/shard_map/ppermute | solution.py:331
  102.5 2.0 %collective-permute-done.11.refs_2_ = bf16[72,256]{1,0:T(8,128)(2,1)S(1)} collective-permute-done((bf16[72,256]{1,0:T(8,128)(2,1)S(1)}, bf16[72,256]{1,0:T(8,128)(2,1)S(1)}, u32[]{:S(2)}, u32[]{:S(2)}) %collective-permute-start.11) | collective-permute-done | bytes 36896 | tf_op jit(solution)/shard_map/ppermute | solution.py:331
  104.4 0.7 shard_map.74
  105.2 0.8 copy.7
  (28 shorter events, 1.5 us)
Async XLA Ops:
  2.6 24.1 %copy-start.1 = (bf16[512,256]{1,0:T(8,128)(2,1)S(1)}, bf16[512,256]{1,0:T(8,128)(2,1)}, u32[]{:S(2)}) copy-start(bf16[512,256]{1,0:T(8,128)(2,1)} %param.5) | copy-start | bytes 786436
  2.6 31.9 %copy-start = (f32[8,128]{1,0:T(8,128)S(1)}, f32[8,128]{1,0:T(8,128)}, u32[]{:S(2)}) copy-start(f32[8,128]{1,0:T(8,128)} %get-tuple-element.25) | copy-start | bytes 12292
  26.7 19.4 %collective-permute-start.1 = (bf16[16,136,256]{2,1,0:T(8,128)(2,1)S(1)}, bf16[16,136,256]{2,1,0:T(8,128)(2,1)S(1)}, u32[]{:S(2)}, u32[]{:S(2)}) collective-permute-start(bf16[16,136,256]{2,1,0:T(8,128)(2,1)S(1)} %all_to_all.15.packed), channel_id=1, source_target_pairs={{0,1},{1,0},{2,3},{3,2},{4,5},{5,4},{6,7},{7,6},{8,9},{9,8},{10,11... | collective-permute-start | bytes 3342344 | tf_op jit(solution)/shard_map/ppermute | solution.py:291
  26.7 11.6 %collective-permute-start = (bf16[512,256]{1,0:T(8,128)(2,1)S(1)}, bf16[512,256]{1,0:T(8,128)(2,1)S(1)}, u32[]{:S(2)}, u32[]{:S(2)}) collective-permute-start(bf16[512,256]{1,0:T(8,128)(2,1)S(1)} %copy-done.1), channel_id=1, source_target_pairs={{0,0},{33,1},{10,2},{43,3},{60,4},{29,5},{22,6},{55,7},{8,8},{41,9... | collective-permute-start | bytes 786440 | tf_op jit(solution)/shard_map/ppermute | solution.py:287
  34.5 3.7 %collective-permute-start.4 = (f32[8,128]{1,0:T(8,128)S(1)}, f32[8,128]{1,0:T(8,128)S(1)}, u32[]{:S(2)}, u32[]{:S(2)}) collective-permute-start(f32[8,128]{1,0:T(8,128)S(1)} %copy-done), channel_id=1, source_target_pairs={{0,8},{8,0},{16,24},{24,16},{32,40},{40,32},{48,56},{56,48},{1,9},... | collective-permute-start | bytes 12296 | tf_op jit(solution)/shard_map/ppermute | solution.py:290
  38.2 9.9 %collective-permute-start.5 = (f32[8,128]{1,0:T(8,128)S(1)}, f32[8,128]{1,0:T(8,128)S(1)}, u32[]{:S(2)}, u32[]{:S(2)}) collective-permute-start(f32[8,128]{1,0:T(8,128)S(1)} %add.15), channel_id=1, source_target_pairs={{0,16},{8,24},{16,0},{24,8},{32,48},{40,56},{48,32},{56,40},{1,17}... | collective-permute-start | bytes 12296 | tf_op jit(solution)/shard_map/ppermute | solution.py:290
  40.1 16.7 %collective-permute-start.2 = (f32[24,128]{1,0:T(8,128)S(1)}, f32[24,128]{1,0:T(8,128)S(1)}, u32[]{:S(2)}, u32[]{:S(2)}) collective-permute-start(f32[24,128]{1,0:T(8,128)S(1)} %get-tuple-element.23.near), channel_id=1, source_target_pairs={{0,1},{1,0},{2,3},{3,2},{4,5},{5,4},{6,7},{7,6},{8,9},{9,8},{10,11... | collective-permute-start | bytes 36872 | tf_op jit(solution)/shard_map/ppermute | solution.py:294
  47.9 8.9 %collective-permute-start.3 = (f32[24,128]{1,0:T(8,128)S(1)}, f32[24,128]{1,0:T(8,128)S(1)}, u32[]{:S(2)}, u32[]{:S(2)}) collective-permute-start(f32[24,128]{1,0:T(8,128)S(1)} %get-tuple-element.24.far), channel_id=1, source_target_pairs={{0,1},{1,0},{2,3},{3,2},{4,5},{5,4},{6,7},{7,6},{8,9},{9,8},{10,11... | collective-permute-start | bytes 36872 | tf_op jit(solution)/shard_map/ppermute | solution.py:296
  48.1 7.6 %collective-permute-start.6 = (f32[8,128]{1,0:T(8,128)S(1)}, f32[8,128]{1,0:T(8,128)S(1)}, u32[]{:S(2)}, u32[]{:S(2)}) collective-permute-start(f32[8,128]{1,0:T(8,128)S(1)} %add.16), channel_id=1, source_target_pairs={{0,32},{8,40},{16,48},{24,56},{32,0},{40,8},{48,16},{56,24},{1,33}... | collective-permute-start | bytes 12296 | tf_op jit(solution)/shard_map/ppermute | solution.py:290
  55.7 1.2 %collective-permute-start.7 = (f32[8,128]{1,0:T(8,128)S(1)}, f32[8,128]{1,0:T(8,128)S(1)}, u32[]{:S(2)}, u32[]{:S(2)}) collective-permute-start(f32[8,128]{1,0:T(8,128)S(1)} %add.17), channel_id=1, source_target_pairs={{0,1},{1,0},{2,3},{3,2},{4,5},{5,4},{6,7},{7,6},{8,9},{9,8},{10,11... | collective-permute-start | bytes 12296 | tf_op jit(solution)/shard_map/ppermute | solution.py:290
  72.2 2.9 %collective-permute-start.13 = (bf16[16,256,128]{2,1,0:T(8,128)(2,1)S(1)}, bf16[16,256,128]{2,1,0:T(8,128)(2,1)S(1)}, u32[]{:S(2)}, u32[]{:S(2)}) collective-permute-start(bf16[16,256,128]{2,1,0:T(8,128)(2,1)S(1)} %get-tuple-element.39), channel_id=1, source_target_pairs={{0,1},{1,0},{2,3},{3,2},{4,5},{5,4},{6,7},{7,6},{8,9},{9,8},{10,11... | collective-permute-start | bytes 3145736 | tf_op jit(solution)/shard_map/ppermute | solution.py:315
  76.5 28.6 %all-to-all-start.2 = ((bf16[16,256,128]{2,1,0:T(8,128)(2,1)}), bf16[16,256,128]{2,1,0:T(8,128)(2,1)S(1)}, u32[]{:S(2)}, u32[]{:S(2)}) async-start(bf16[16,256,128]{2,1,0:T(8,128)(2,1)} %add.19), calls=%async_computation.2 | async-start | bytes 2097152 | tf_op jit(solution)/shard_map/all_to_all | solution.py:52
  81.4 9.5 %collective-permute-start.8 = (bf16[520,256]{1,0:T(8,128)(2,1)S(1)}, bf16[520,256]{1,0:T(8,128)(2,1)S(1)}, u32[]{:S(2)}, u32[]{:S(2)}) collective-permute-start(bf16[520,256]{1,0:T(8,128)(2,1)S(1)} %get-tuple-element.32), channel_id=1, source_target_pairs={{0,0},{1,33},{2,10},{3,43},{4,60},{5,29},{6,22},{7,55},{8,8},{9,41... | collective-permute-start | bytes 798728 | tf_op jit(solution)/shard_map/ppermute | solution.py:322
  90.9 7.3 %collective-permute-start.9 = (bf16[264,256]{1,0:T(8,128)(2,1)S(1)}, bf16[264,256]{1,0:T(8,128)(2,1)S(1)}, u32[]{:S(2)}, u32[]{:S(2)}) collective-permute-start(bf16[264,256]{1,0:T(8,128)(2,1)S(1)} %slice.8), channel_id=1, source_target_pairs={{0,1},{1,0},{2,3},{3,2},{4,5},{5,4},{6,7},{7,6},{8,9},{9,8},{10,11... | collective-permute-start | bytes 405512 | tf_op jit(solution)/shard_map/ppermute | solution.py:327
  98.2 4.2 %collective-permute-start.10 = (bf16[72,256]{1,0:T(8,128)(2,1)S(1)}, bf16[72,256]{1,0:T(8,128)(2,1)S(1)}, u32[]{:S(2)}, u32[]{:S(2)}) collective-permute-start(bf16[72,256]{1,0:T(8,128)(2,1)S(1)} %get-tuple-element.34), channel_id=1, source_target_pairs={{0,2},{2,4},{4,6},{6,0},{1,3},{3,5},{5,7},{7,1},{8,10},{10,12},{12... | collective-permute-start | bytes 110600 | tf_op jit(solution)/shard_map/ppermute | solution.py:331
  98.6 5.8 %collective-permute-start.11 = (bf16[72,256]{1,0:T(8,128)(2,1)S(1)}, bf16[72,256]{1,0:T(8,128)(2,1)S(1)}, u32[]{:S(2)}, u32[]{:S(2)}) collective-permute-start(bf16[72,256]{1,0:T(8,128)(2,1)S(1)} %get-tuple-element.35), channel_id=1, source_target_pairs={{0,4},{2,6},{4,0},{6,2},{1,5},{3,7},{5,1},{7,3},{8,12},{10,14},{12... | collective-permute-start | bytes 110600 | tf_op jit(solution)/shard_map/ppermute | solution.py:331
  98.6 5.8 %collective-permute-start.12 = (bf16[72,256]{1,0:T(8,128)(2,1)S(1)}, bf16[72,256]{1,0:T(8,128)(2,1)S(1)}, u32[]{:S(2)}, u32[]{:S(2)}) collective-permute-start(bf16[72,256]{1,0:T(8,128)(2,1)S(1)} %get-tuple-element.36), channel_id=1, source_target_pairs={{0,6},{2,0},{4,2},{6,4},{1,7},{3,1},{5,3},{7,5},{8,14},{10,8},{12,... | collective-permute-start | bytes 110600 | tf_op jit(solution)/shard_map/ppermute | solution.py:331

commit v6 on v5

--- a/solution.py
+++ b/solution.py
@@ -139,7 +139,7 @@
     return call(functools.partial(forward_kernel, rows), shapes, packed, bank)
 
 
-def join_kernel(near, far, other_near, other_far, count, out):
+def join_kernel(near, far, other_near, other_far, count, other_count, out):
     shards = near.shape[0] - 8
 
     def join(a, b):
@@ -149,7 +149,7 @@
     first = join(near[:shards], other_far[:shards])
     second = join(far[:shards], other_near[:shards])
     positive = near[shards:] + far[shards:] + other_near[shards:] + other_far[shards:]
-    extra = jnp.where(iota(positive.shape, 0) == 0, positive, count[...])
+    extra = jnp.where(iota(positive.shape, 0) == 0, positive, count[...] + other_count[...])
     for k in range(out.shape[0]):
         out[k, :shards] = first
         out[k, shards : 2 * shards] = second
@@ -180,33 +180,33 @@
     loss_out[...] = jnp.broadcast_to(loss, loss_out.shape)
 
 
-def backward_core(rows, half, packed, bank, lse, weight, user_part, total):
+def dlogits_at(rows, half, at, packed, bank, lse, weight):
     shards = packed.shape[0]
+    users = shard_users(packed, at, rows)
+    logits = scores(bank[...], users)
+    pos = local_positives(packed, at, rows, first_item(bank.shape[0]))
+    mine = cohort_row(packed, at, rows, 0)
+    ids = iota((NCOH, mine.shape[1]), 0).astype(F32)
+    weights = jnp.sum(jnp.where(ids == mine, weight[:, 0:1], F32(0)), axis=0, keepdims=True)
+    line = half * shards + at
+    level = jnp.concatenate([lse[line + s : line + s + 1, :] for s in range(STEP)], axis=1)
+    hot = jnp.where(iota(logits.shape, 0) == pos, F32(1), F32(0))
+    return users, (weights * (jnp.exp(logits - level) - hot)).astype(BF16)
+
+
+def backward_far_kernel(rows, scale, packed, bank, stats, coh_near, coh_far, *outs):
+    user_part, bank_part, lse, weight, loss = outs
+    settle(scale, stats, coh_near, coh_far, lse, weight, loss)
     bank_t = bank[...].T
-    first = first_item(bank.shape[0])
-    for at in range(0, shards, STEP):
-        users = shard_users(packed, at, rows)
-        logits = scores(bank[...], users)
-        pos = local_positives(packed, at, rows, first)
-        mine = cohort_row(packed, at, rows, 0)
-        ids = iota((NCOH, mine.shape[1]), 0).astype(F32)
-        weights = jnp.sum(jnp.where(ids == mine, weight[:, 0:1], F32(0)), axis=0, keepdims=True)
-        line = half * shards + at
-        level = jnp.concatenate([lse[line + s : line + s + 1, :] for s in range(STEP)], axis=1)
-        hot = jnp.where(iota(logits.shape, 0) == pos, F32(1), F32(0))
-        dlogits = (weights * (jnp.exp(logits - level) - hot)).astype(BF16)
+    total = None
+    for at in range(0, packed.shape[0], STEP):
+        users, dlogits = dlogits_at(rows, 1, at, packed, bank, lse, weight)
         part = jnp.dot(bank_t, dlogits, preferred_element_type=F32).astype(BF16)
         for s in range(STEP):
             user_part[at + s] = part[:, s * LANES : (s + 1) * LANES]
         grad = jnp.dot(dlogits, users, preferred_element_type=F32)
         total = grad if total is None else total + grad
-    return total
-
-
-def backward_far_kernel(rows, scale, packed, bank, stats, coh_near, coh_far, *outs):
-    user_part, bank_part, lse, weight, loss = outs
-    settle(scale, stats, coh_near, coh_far, lse, weight, loss)
-    bank_part[...] = backward_core(rows, 1, packed, bank, lse, weight, user_part, None)
+    bank_part[...] = total
 
 
 def digits_of(value):
@@ -231,8 +231,13 @@
     out[at : at + 8, LANES:] = tile
 
 
-def backward_near_kernel(rows, packed, bank, lse, weight, far_part, loss, user_part, out, acc):
-    acc[...] = backward_core(rows, 0, packed, bank, lse, weight, user_part, far_part[...])
+def backward_near_kernel(rows, packed, bank, lse, weight, far_part, loss, kept, out, acc):
+    total = far_part[...]
+    for step in range(packed.shape[0] // STEP):
+        users, dlogits = dlogits_at(rows, 0, step * STEP, packed, bank, lse, weight)
+        kept[step] = dlogits
+        total = total + jnp.dot(dlogits, users, preferred_element_type=F32)
+    acc[...] = total
     nx, nc = lax.axis_size("x"), lax.axis_size("c")
     height = acc.shape[0] // (nx * nc)
     core = lax.axis_index("c")
@@ -245,6 +250,23 @@
     write_digits(out, nx * height, loss[...])
 
 
+def users_near_kernel(kept, bank, far_part, user_part):
+    bank_t = bank[...].T
+    for step in range(kept.shape[0]):
+        part = jnp.dot(bank_t, kept[step], preferred_element_type=F32)
+        for s in range(STEP):
+            mine = part[:, s * LANES : (s + 1) * LANES]
+            at = step * STEP + s
+            user_part[at] = (mine + far_part[at].astype(F32)).astype(BF16)
+
+
+def finish_kernel(parts, out):
+    total = parts[0].astype(F32)
+    for k in range(1, parts.shape[0]):
+        total = total + parts[k].astype(F32)
+    out[...] = total.T
+
+
 def halve_kernel(mine, theirs, *pieces):
     below = theirs.shape[0]
     height = (below - 8) // len(pieces)
@@ -285,9 +307,11 @@
     )
     near = exchange(packed, PLANE)
     item_block = lax.ppermute(bank, COLUMN, fetch)
-    for axis, by in (("z", 1), ("z", 2), ("z", 4), ("c", 1)):
+    for axis, by in (("c", 1), ("z", 1), ("z", 2), ("z", 4)):
         ways = [(k, k ^ by) for k in range(lax.axis_size(axis))]
-        count = count + lax.ppermute(count, axis, ways)
+        other_count = lax.ppermute(count, axis, ways)
+        if by < 4:
+            count = count + other_count
     far = lax.ppermute(near, "c", cross)
 
     near_stats, near_coh = forward(near, item_block, rows)
@@ -297,7 +321,7 @@
     stats = call(
         join_kernel,
         f32(plane, 2 * plane + 8, LANES),
-        *(near_stats, far_stats, other_near, other_far, count),
+        *(near_stats, far_stats, other_near, other_far, count, other_count),
     )
     stats = exchange(stats, PLANE)
 
@@ -313,14 +337,14 @@
         *(far, item_block, stats, near_coh, far_coh),
     )
     far_part = lax.ppermute(far_part, "c", cross)
-    near_part, bank_part = call(
+    kept, bank_part = call(
         functools.partial(backward_near_kernel, rows),
-        (bf16(plane, width, rows), bf16(bank.shape[0] + 8, width)),
+        (bf16(plane // STEP, bank.shape[0], STEP * rows), bf16(bank.shape[0] + 8, width)),
         *(near, item_block, lse, weight, bank_part, loss),
         scratch=[pltpu.VMEM(bank.shape, F32)],
     )
     bank_part = lax.ppermute(bank_part, COLUMN, [(b, a) for a, b in fetch])
-    user_part = near_part + far_part
+    user_part = call(users_near_kernel, bf16(plane, width, rows), *(kept, item_block, far_part))
     user_part = exchange(user_part, PLANE)
     half = bank.shape[0] // nc
     height = half // nx
@@ -329,12 +353,13 @@
     arrived = [pieces[0]]
     for r in range(1, nx):
         arrived.append(lax.ppermute(pieces[r], "x", [(k, (k + r) % nx) for k in range(nx)]))
+    user_grad = call(finish_kernel, f32(rows, width), user_part)
+    user_grad, *arrived = lax.optimization_barrier((user_grad, *arrived))
     bank_grad, loss = call(
         functools.partial(gather_kernel, 1.0 / total_users),
         (f32(height, width), f32(1, LANES)),
         *arrived,
     )
-    user_grad = jnp.sum(user_part.astype(F32), axis=0).T
     return loss[0, 0], user_grad, bank_grad
 
 

time: 108 us -> 109 us (level)
  waiting for transfers between devices: 18.7 us -> 20.5 us
  Pallas kernels: 10.9 us -> 12.5 us
  other arithmetic: 1.45 us -> 0.01 us
  starting transfers between devices: 36.3 us -> 37.4 us
    ppermute x4, starting transfers between devices: 4.77 us -> 7.08 us  [step(): other_count = lax.ppermute(count, axis, ways)]
    pallas_call x8 -> x10, Pallas kernels: 10.9 us -> 12.5 us  [call(): pl.pallas_call(kernel, in_specs=[VMEM] * len(operands), out_specs=jax.tre...]
    add x5 -> x3, other arithmetic: 1.31 us -> 0.01 us  [step(): count = count + other_count]
    ppermute x3, waiting for transfers between devices: 3.68 us -> 2.55 us  [step(): lax.ppermute(pieces[r], 'x', [(k, (k + r) % nx) for k in range(nx)])]
  transfers between devices with their start and end apart: 15 -> 15, of which waited for: 9 -> 9; matrix products, arithmetic and copies ran while one was open for 0% -> 0% of each run, Pallas kernels for 6% -> 5%
where the time goes in v6:
time: 109 us; the launch traced here: 108 us
  starting transfers between devices  37.4 us (34%)
  blocking collectives  36.6 us (34%)
  waiting for transfers between devices  20.5 us (19%)
  Pallas kernels  12.5 us (11%)
    all_to_all x2, blocking collectives, exchange(): return lax.all_to_all(value, axis, split_axis=0, concat_axis=0, tiled=True)  36.6 us
    pallas_call x10, Pallas kernels, call(): pl.pallas_call(kernel, in_specs=[VMEM] * len(operands), out_specs=jax.tre...  12.5 us
    ppermute x4, waiting for transfers between devices, step(): other_count = lax.ppermute(count, axis, ways)  8.06 us
    ppermute x1, starting transfers between devices, step(): item_block = lax.ppermute(bank, COLUMN, fetch)  7.75 us
    ppermute x4, starting transfers between devices, step(): other_count = lax.ppermute(count, axis, ways)  7.08 us
    ppermute x1, waiting for transfers between devices, step(): bank_part = lax.ppermute(bank_part, COLUMN, [(b, a) for a, b in fetch])  6.88 us
    ppermute x1, starting transfers between devices, step(): theirs = lax.ppermute(bank_part[:half + 8], 'c', cross)  5.95 us
    ppermute x1, starting transfers between devices, step(): other_near = lax.ppermute(near_stats, 'c', cross)  5.93 us
  transfers between devices with their start and end apart: 15, of which 9 were waited for; matrix products, arithmetic and copies ran while one was open for 0% of the time, Pallas kernels for 5%

profile of v6, /device:TPU:2, one launch (start us, length us, event | category | flops | bytes accessed | tf_op | source)
XLA Modules:
  0.0 107.7 jit_solution(6853297089633118349)
XLA Ops:
  0.6 2.0 %shard_map.67 = (bf16[16,136,256]{2,1,0:T(8,128)(2,1)}, f32[8,128]{1,0:T(8,128)}) custom-call(bf16[128,256]{1,0:T(8,128)(2,1)} %users.1, s32[1,128]{1,0:T(1,128)} %bitcast.4, s32[1,128]{1,0:T(1,128)} %bitcast.5), custom_call_target="tpu_custom_call" | custom-call | tf_op jit(solution)/shard_map/pallas_call | solution.py:26
  2.6 24.1 %all_to_all.15.packed = bf16[16,136,256]{2,1,0:T(8,128)(2,1)S(1)} all-to-all(bf16[16,136,256]{2,1,0:T(8,128)(2,1)} %get-tuple-element.27), channel_id=1, replica_groups=mesh['y'=4,'z'=8,'x'=4,'c'=2] {'y','x'}, dimensions={0} | all-to-all | bytes 2228224 | tf_op jit(solution)/shard_map/all_to_all | solution.py:52
  26.7 7.8 %collective-permute-start = (bf16[512,256]{1,0:T(8,128)(2,1)S(1)}, bf16[512,256]{1,0:T(8,128)(2,1)S(1)}, u32[]{:S(2)}, u32[]{:S(2)}) collective-permute-start(bf16[512,256]{1,0:T(8,128)(2,1)S(1)} %copy-done.1), channel_id=1, source_target_pairs={{0,0},{33,1},{10,2},{43,3},{60,4},{29,5},{22,6},{55,7},{8,8},{41,9... | collective-permute-start | bytes 786440 | tf_op jit(solution)/shard_map/ppermute | solution.py:309
  34.6 1.2 %collective-permute-done.4 = f32[8,128]{1,0:T(8,128)S(1)} collective-permute-done((f32[8,128]{1,0:T(8,128)S(1)}, f32[8,128]{1,0:T(8,128)S(1)}, u32[]{:S(2)}, u32[]{:S(2)}) %collective-permute-start.4) | collective-permute-done | bytes 4128 | tf_op jit(solution)/shard_map/ppermute | solution.py:312
  35.8 1.8 %collective-permute-start.5 = (f32[8,128]{1,0:T(8,128)S(1)}, f32[8,128]{1,0:T(8,128)S(1)}, u32[]{:S(2)}, u32[]{:S(2)}) collective-permute-start(f32[8,128]{1,0:T(8,128)S(1)} %add.9), channel_id=1, source_target_pairs={{0,8},{8,0},{16,24},{24,16},{32,40},{40,32},{48,56},{56,48},{1,9},... | collective-permute-start | bytes 12296 | tf_op jit(solution)/shard_map/ppermute | solution.py:312
  38.4 1.7 %shard_map.68 = (f32[24,128]{1,0:T(8,128)S(1)}, f32[16,128]{1,0:T(8,128)S(1)}) custom-call(bf16[16,136,256]{2,1,0:T(8,128)(2,1)S(1)} %all_to_all.15.packed, bf16[512,256]{1,0:T(8,128)(2,1)S(1)} %collective-permute-done.bank), custom_call_target="tpu_custom_call" | custom-call | tf_op jit(solution)/shard_map/pallas_call | solution.py:26
  40.1 5.9 %collective-permute-start.2 = (f32[24,128]{1,0:T(8,128)S(1)}, f32[24,128]{1,0:T(8,128)S(1)}, u32[]{:S(2)}, u32[]{:S(2)}) collective-permute-start(f32[24,128]{1,0:T(8,128)S(1)} %get-tuple-element.28.near), channel_id=1, source_target_pairs={{0,1},{1,0},{2,3},{3,2},{4,5},{5,4},{6,7},{7,6},{8,9},{9,8},{10,11... | collective-permute-start | bytes 36872 | tf_op jit(solution)/shard_map/ppermute | solution.py:318
  46.0 1.7 %shard_map.69 = (f32[24,128]{1,0:T(8,128)S(1)}, f32[16,128]{1,0:T(8,128)S(1)}) custom-call(bf16[16,136,256]{2,1,0:T(8,128)(2,1)S(1)} %collective-permute-done.1.packed, bf16[512,256]{1,0:T(8,128)(2,1)S(1)} %collective-permute-done.bank), custom_call_target="tpu_custom_call" | custom-call | tf_op jit(solution)/shard_map/pallas_call | solution.py:26
  48.5 4.0 %collective-permute-done.6 = f32[8,128]{1,0:T(8,128)S(1)} collective-permute-done((f32[8,128]{1,0:T(8,128)S(1)}, f32[8,128]{1,0:T(8,128)S(1)}, u32[]{:S(2)}, u32[]{:S(2)}) %collective-permute-start.6) | collective-permute-done | bytes 4128 | tf_op jit(solution)/shard_map/ppermute | solution.py:312
  52.5 4.6 %collective-permute-start.7 = (f32[8,128]{1,0:T(8,128)S(1)}, f32[8,128]{1,0:T(8,128)S(1)}, u32[]{:S(2)}, u32[]{:S(2)}) collective-permute-start(f32[8,128]{1,0:T(8,128)S(1)} %add.11.count), channel_id=1, source_target_pairs={{0,32},{8,40},{16,48},{24,56},{32,0},{40,8},{48,16},{56,24},{1,33}... | collective-permute-start | bytes 12296 | tf_op jit(solution)/shard_map/ppermute | solution.py:312
  57.1 2.9 %collective-permute-done.7.other_count = f32[8,128]{1,0:T(8,128)S(1)} collective-permute-done((f32[8,128]{1,0:T(8,128)S(1)}, f32[8,128]{1,0:T(8,128)S(1)}, u32[]{:S(2)}, u32[]{:S(2)}) %collective-permute-start.7) | collective-permute-done | bytes 4128 | tf_op jit(solution)/shard_map/ppermute | solution.py:312
  60.1 12.5 %all_to_all.16.stats = f32[16,40,128]{2,1,0:T(8,128)S(1)} all-to-all(f32[16,40,128]{2,1,0:T(8,128)S(1)} %shard_map.70), channel_id=1, replica_groups=mesh['y'=4,'z'=8,'x'=4,'c'=2] {'y','x'}, dimensions={0} | all-to-all | bytes 655360 | tf_op jit(solution)/shard_map/all_to_all | solution.py:52
  72.5 2.2 %shard_map.71 = (bf16[16,256,128]{2,1,0:T(8,128)(2,1)S(1)}, f32[512,256]{1,0:T(8,128)S(1)}, f32[32,128]{1,0:T(8,128)S(1)}, f32[16,128]{1,0:T(8,128)S(1)}, f32[8,128]{1,0:T(8,128)S(1)}) custom-call(bf16[16,136,256]{2,1,0:T(8,128)(2,1)S(1)} %collective-permute-done.1.packed, bf16[512,256]{1,0:T(8,128)(2,1)S(1)} %collective-permute-done.bank, ...), custom_call_target="tpu_custom_call" | custom-call | tf_op jit(solution)/shard_map/pallas_call | solution.py:26
  75.1 1.5 %shard_map.72 = (bf16[4,512,512]{2,1,0:T(8,128)(2,1)S(1)}, bf16[520,256]{1,0:T(8,128)(2,1)S(1)}) custom-call(bf16[16,136,256]{2,1,0:T(8,128)(2,1)S(1)} %all_to_all.15.packed, bf16[512,256]{1,0:T(8,128)(2,1)S(1)} %collective-permute-done.bank, f32[32,128]{1,0:T(8,128)S(1)} %get-tuple-element.33.lse, f32[16,128]{1,0:T(8,128)S(1)} %get-tuple-element.34.weight, ...), custom_call_target="tpu_custom_call" | custom-call | tf_op jit(solution)/shard_map/pallas_call | solution.py:26
  76.6 1.1 %collective-permute-done.8.far_part = bf16[16,256,128]{2,1,0:T(8,128)(2,1)S(1)} collective-permute-done((bf16[16,256,128]{2,1,0:T(8,128)(2,1)S(1)}, bf16[16,256,128]{2,1,0:T(8,128)(2,1)S(1)}, u32[]{:S(2)}, u32[]{:S(2)}) %collective-permute-start.8) | collective-permute-done | bytes 1048608 | tf_op jit(solution)/shard_map/ppermute | solution.py:339
  77.7 1.7 %shard_map.73 = bf16[16,256,128]{2,1,0:T(8,128)(2,1)} custom-call(bf16[4,512,512]{2,1,0:T(8,128)(2,1)S(1)} %get-tuple-element.37.kept, bf16[512,256]{1,0:T(8,128)(2,1)S(1)} %collective-permute-done.bank, bf16[16,256,128]{2,1,0:T(8,128)(2,1)S(1)} %collective-permute-done.8.far_part), custom_call_target="tpu_custom_call" | custom-call | tf_op jit(solution)/shard_map/pallas_call | solution.py:26
  79.4 4.9 %all-to-all-start.2 = ((bf16[16,256,128]{2,1,0:T(8,128)(2,1)}), bf16[16,256,128]{2,1,0:T(8,128)(2,1)S(1)}, u32[]{:S(2)}, u32[]{:S(2)}) async-start(bf16[16,256,128]{2,1,0:T(8,128)(2,1)} %shard_map.73), calls=%async_computation.2 | async-start | bytes 2097152 | tf_op jit(solution)/shard_map/all_to_all | solution.py:52
  84.3 2.6 %collective-permute-start.9 = (bf16[520,256]{1,0:T(8,128)(2,1)S(1)}, bf16[520,256]{1,0:T(8,128)(2,1)S(1)}, u32[]{:S(2)}, u32[]{:S(2)}) collective-permute-start(bf16[520,256]{1,0:T(8,128)(2,1)S(1)} %get-tuple-element.39), channel_id=1, source_target_pairs={{0,0},{1,33},{2,10},{3,43},{4,60},{5,29},{6,22},{7,55},{8,8},{9,41... | collective-permute-start | bytes 798728 | tf_op jit(solution)/shard_map/ppermute | solution.py:346
  87.0 6.9 %collective-permute-done.9.mine = bf16[520,256]{1,0:T(8,128)(2,1)S(1)} collective-permute-done((bf16[520,256]{1,0:T(8,128)(2,1)S(1)}, bf16[520,256]{1,0:T(8,128)(2,1)S(1)}, u32[]{:S(2)}, u32[]{:S(2)}) %collective-permute-start.9) | collective-permute-done | bytes 266272 | tf_op jit(solution)/shard_map/ppermute | solution.py:346
  93.9 6.0 %collective-permute-start.10 = (bf16[264,256]{1,0:T(8,128)(2,1)S(1)}, bf16[264,256]{1,0:T(8,128)(2,1)S(1)}, u32[]{:S(2)}, u32[]{:S(2)}) collective-permute-start(bf16[264,256]{1,0:T(8,128)(2,1)S(1)} %slice.8), channel_id=1, source_target_pairs={{0,1},{1,0},{2,3},{3,2},{4,5},{5,4},{6,7},{7,6},{8,9},{9,8},{10,11... | collective-permute-start | bytes 405512 | tf_op jit(solution)/shard_map/ppermute | solution.py:351
  99.8 1.0 collective-permute-done.10.theirs
  101.5 2.2 %collective-permute-start.13 = (bf16[72,256]{1,0:T(8,128)(2,1)S(1)}, bf16[72,256]{1,0:T(8,128)(2,1)S(1)}, u32[]{:S(2)}, u32[]{:S(2)}) collective-permute-start(bf16[72,256]{1,0:T(8,128)(2,1)S(1)} %get-tuple-element.43), channel_id=1, source_target_pairs={{0,6},{2,0},{4,2},{6,4},{1,7},{3,1},{5,3},{7,5},{8,14},{10,8},{12,... | collective-permute-start | bytes 110600 | tf_op jit(solution)/shard_map/ppermute | solution.py:355
  103.6 0.9 shard_map.74
  105.2 1.8 %collective-permute-done.12.refs_2_ = bf16[72,256]{1,0:T(8,128)(2,1)S(1)} collective-permute-done((bf16[72,256]{1,0:T(8,128)(2,1)S(1)}, bf16[72,256]{1,0:T(8,128)(2,1)S(1)}, u32[]{:S(2)}, u32[]{:S(2)}) %collective-permute-start.12) | collective-permute-done | bytes 36896 | tf_op jit(solution)/shard_map/ppermute | solution.py:355
  (26 shorter events, 4.0 us)
Async XLA Ops:
  2.6 24.1 %copy-start.1 = (bf16[512,256]{1,0:T(8,128)(2,1)S(1)}, bf16[512,256]{1,0:T(8,128)(2,1)}, u32[]{:S(2)}) copy-start(bf16[512,256]{1,0:T(8,128)(2,1)} %param.5) | copy-start | bytes 786436
  2.6 31.9 %copy-start = (f32[8,128]{1,0:T(8,128)S(1)}, f32[8,128]{1,0:T(8,128)}, u32[]{:S(2)}) copy-start(f32[8,128]{1,0:T(8,128)} %get-tuple-element.30) | copy-start | bytes 12292
  26.7 19.3 %collective-permute-start.1 = (bf16[16,136,256]{2,1,0:T(8,128)(2,1)S(1)}, bf16[16,136,256]{2,1,0:T(8,128)(2,1)S(1)}, u32[]{:S(2)}, u32[]{:S(2)}) collective-permute-start(bf16[16,136,256]{2,1,0:T(8,128)(2,1)S(1)} %all_to_all.15.packed), channel_id=1, source_target_pairs={{0,1},{1,0},{2,3},{3,2},{4,5},{5,4},{6,7},{7,6},{8,9},{9,8},{10,11... | collective-permute-start | bytes 3342344 | tf_op jit(solution)/shard_map/ppermute | solution.py:315
  26.7 11.6 %collective-permute-start = (bf16[512,256]{1,0:T(8,128)(2,1)S(1)}, bf16[512,256]{1,0:T(8,128)(2,1)S(1)}, u32[]{:S(2)}, u32[]{:S(2)}) collective-permute-start(bf16[512,256]{1,0:T(8,128)(2,1)S(1)} %copy-done.1), channel_id=1, source_target_pairs={{0,0},{33,1},{10,2},{43,3},{60,4},{29,5},{22,6},{55,7},{8,8},{41,9... | collective-permute-start | bytes 786440 | tf_op jit(solution)/shard_map/ppermute | solution.py:309
  34.5 1.3 %collective-permute-start.4 = (f32[8,128]{1,0:T(8,128)S(1)}, f32[8,128]{1,0:T(8,128)S(1)}, u32[]{:S(2)}, u32[]{:S(2)}) collective-permute-start(f32[8,128]{1,0:T(8,128)S(1)} %copy-done), channel_id=1, source_target_pairs={{0,1},{1,0},{2,3},{3,2},{4,5},{5,4},{6,7},{7,6},{8,9},{9,8},{10,11... | collective-permute-start | bytes 12296 | tf_op jit(solution)/shard_map/ppermute | solution.py:312
  35.8 12.1 %collective-permute-start.5 = (f32[8,128]{1,0:T(8,128)S(1)}, f32[8,128]{1,0:T(8,128)S(1)}, u32[]{:S(2)}, u32[]{:S(2)}) collective-permute-start(f32[8,128]{1,0:T(8,128)S(1)} %add.9), channel_id=1, source_target_pairs={{0,8},{8,0},{16,24},{24,16},{32,40},{40,32},{48,56},{56,48},{1,9},... | collective-permute-start | bytes 12296 | tf_op jit(solution)/shard_map/ppermute | solution.py:312
  40.1 19.9 %collective-permute-start.2 = (f32[24,128]{1,0:T(8,128)S(1)}, f32[24,128]{1,0:T(8,128)S(1)}, u32[]{:S(2)}, u32[]{:S(2)}) collective-permute-start(f32[24,128]{1,0:T(8,128)S(1)} %get-tuple-element.28.near), channel_id=1, source_target_pairs={{0,1},{1,0},{2,3},{3,2},{4,5},{5,4},{6,7},{7,6},{8,9},{9,8},{10,11... | collective-permute-start | bytes 36872 | tf_op jit(solution)/shard_map/ppermute | solution.py:318
  47.8 12.2 %collective-permute-start.3 = (f32[24,128]{1,0:T(8,128)S(1)}, f32[24,128]{1,0:T(8,128)S(1)}, u32[]{:S(2)}, u32[]{:S(2)}) collective-permute-start(f32[24,128]{1,0:T(8,128)S(1)} %get-tuple-element.29.far), channel_id=1, source_target_pairs={{0,1},{1,0},{2,3},{3,2},{4,5},{5,4},{6,7},{7,6},{8,9},{9,8},{10,11... | collective-permute-start | bytes 36872 | tf_op jit(solution)/shard_map/ppermute | solution.py:320
  47.9 4.6 %collective-permute-start.6 = (f32[8,128]{1,0:T(8,128)S(1)}, f32[8,128]{1,0:T(8,128)S(1)}, u32[]{:S(2)}, u32[]{:S(2)}) collective-permute-start(f32[8,128]{1,0:T(8,128)S(1)} %add.10), channel_id=1, source_target_pairs={{0,16},{8,24},{16,0},{24,8},{32,48},{40,56},{48,32},{56,40},{1,17}... | collective-permute-start | bytes 12296 | tf_op jit(solution)/shard_map/ppermute | solution.py:312
  52.5 7.5 %collective-permute-start.7 = (f32[8,128]{1,0:T(8,128)S(1)}, f32[8,128]{1,0:T(8,128)S(1)}, u32[]{:S(2)}, u32[]{:S(2)}) collective-permute-start(f32[8,128]{1,0:T(8,128)S(1)} %add.11.count), channel_id=1, source_target_pairs={{0,32},{8,40},{16,48},{24,56},{32,0},{40,8},{48,16},{56,24},{1,33}... | collective-permute-start | bytes 12296 | tf_op jit(solution)/shard_map/ppermute | solution.py:312
  74.8 2.9 %collective-permute-start.8 = (bf16[16,256,128]{2,1,0:T(8,128)(2,1)S(1)}, bf16[16,256,128]{2,1,0:T(8,128)(2,1)S(1)}, u32[]{:S(2)}, u32[]{:S(2)}) collective-permute-start(bf16[16,256,128]{2,1,0:T(8,128)(2,1)S(1)} %get-tuple-element.38), channel_id=1, source_target_pairs={{0,1},{1,0},{2,3},{3,2},{4,5},{5,4},{6,7},{7,6},{8,9},{9,8},{10,11... | collective-permute-start | bytes 3145736 | tf_op jit(solution)/shard_map/ppermute | solution.py:339
  79.4 24.2 %all-to-all-start.2 = ((bf16[16,256,128]{2,1,0:T(8,128)(2,1)}), bf16[16,256,128]{2,1,0:T(8,128)(2,1)S(1)}, u32[]{:S(2)}, u32[]{:S(2)}) async-start(bf16[16,256,128]{2,1,0:T(8,128)(2,1)} %shard_map.73), calls=%async_computation.2 | async-start | bytes 2097152 | tf_op jit(solution)/shard_map/all_to_all | solution.py:52
  84.3 9.5 %collective-permute-start.9 = (bf16[520,256]{1,0:T(8,128)(2,1)S(1)}, bf16[520,256]{1,0:T(8,128)(2,1)S(1)}, u32[]{:S(2)}, u32[]{:S(2)}) collective-permute-start(bf16[520,256]{1,0:T(8,128)(2,1)S(1)} %get-tuple-element.39), channel_id=1, source_target_pairs={{0,0},{1,33},{2,10},{3,43},{4,60},{5,29},{6,22},{7,55},{8,8},{9,41... | collective-permute-start | bytes 798728 | tf_op jit(solution)/shard_map/ppermute | solution.py:346
  93.9 6.9 %collective-permute-start.10 = (bf16[264,256]{1,0:T(8,128)(2,1)S(1)}, bf16[264,256]{1,0:T(8,128)(2,1)S(1)}, u32[]{:S(2)}, u32[]{:S(2)}) collective-permute-start(bf16[264,256]{1,0:T(8,128)(2,1)S(1)} %slice.8), channel_id=1, source_target_pairs={{0,1},{1,0},{2,3},{3,2},{4,5},{5,4},{6,7},{7,6},{8,9},{9,8},{10,11... | collective-permute-start | bytes 405512 | tf_op jit(solution)/shard_map/ppermute | solution.py:351
  100.9 4.4 %collective-permute-start.11 = (bf16[72,256]{1,0:T(8,128)(2,1)S(1)}, bf16[72,256]{1,0:T(8,128)(2,1)S(1)}, u32[]{:S(2)}, u32[]{:S(2)}) collective-permute-start(bf16[72,256]{1,0:T(8,128)(2,1)S(1)} %get-tuple-element.41), channel_id=1, source_target_pairs={{0,2},{2,4},{4,6},{6,0},{1,3},{3,5},{5,7},{7,1},{8,10},{10,12},{12... | collective-permute-start | bytes 110600 | tf_op jit(solution)/shard_map/ppermute | solution.py:355
  101.5 5.6 %collective-permute-start.12 = (bf16[72,256]{1,0:T(8,128)(2,1)S(1)}, bf16[72,256]{1,0:T(8,128)(2,1)S(1)}, u32[]{:S(2)}, u32[]{:S(2)}) collective-permute-start(bf16[72,256]{1,0:T(8,128)(2,1)S(1)} %get-tuple-element.42), channel_id=1, source_target_pairs={{0,4},{2,6},{4,0},{6,2},{1,5},{3,7},{5,1},{7,3},{8,12},{10,14},{12... | collective-permute-start | bytes 110600 | tf_op jit(solution)/shard_map/ppermute | solution.py:355
  101.5 5.6 %collective-permute-start.13 = (bf16[72,256]{1,0:T(8,128)(2,1)S(1)}, bf16[72,256]{1,0:T(8,128)(2,1)S(1)}, u32[]{:S(2)}, u32[]{:S(2)}) collective-permute-start(bf16[72,256]{1,0:T(8,128)(2,1)S(1)} %get-tuple-element.43), channel_id=1, source_target_pairs={{0,6},{2,0},{4,2},{6,4},{1,7},{3,1},{5,3},{7,5},{8,14},{10,8},{12,... | collective-permute-start | bytes 110600 | tf_op jit(solution)/shard_map/ppermute | solution.py:355

commit v7 on v6

--- a/solution.py
+++ b/solution.py
@@ -260,13 +260,6 @@
             user_part[at] = (mine + far_part[at].astype(F32)).astype(BF16)
 
 
-def finish_kernel(parts, out):
-    total = parts[0].astype(F32)
-    for k in range(1, parts.shape[0]):
-        total = total + parts[k].astype(F32)
-    out[...] = total.T
-
-
 def halve_kernel(mine, theirs, *pieces):
     below = theirs.shape[0]
     height = (below - 8) // len(pieces)
@@ -278,13 +271,17 @@
         write_digits(piece, height, loss)
 
 
-def gather_kernel(share, *refs):
-    pieces, (grad, loss) = refs[:-2], refs[-2:]
-    height = grad.shape[0]
+def finish_kernel(share, parts, *refs):
+    pieces, (user_grad, bank_grad, loss) = refs[:-3], refs[-3:]
+    total = parts[0].astype(F32)
+    for k in range(1, parts.shape[0]):
+        total = total + parts[k].astype(F32)
+    user_grad[...] = total.T
+    height = bank_grad.shape[0]
     total = pieces[0][...].astype(F32)
     for piece in pieces[1:]:
         total = total + piece[...].astype(F32)
-    grad[...] = total[:height]
+    bank_grad[...] = total[:height]
     loss[...] = jnp.sum(total[height:], axis=0, keepdims=True)[:, :LANES] * share
 
 
@@ -307,10 +304,10 @@
     )
     near = exchange(packed, PLANE)
     item_block = lax.ppermute(bank, COLUMN, fetch)
-    for axis, by in (("c", 1), ("z", 1), ("z", 2), ("z", 4)):
+    for axis, by in (("z", 4), ("z", 2), ("c", 1), ("z", 1)):
         ways = [(k, k ^ by) for k in range(lax.axis_size(axis))]
         other_count = lax.ppermute(count, axis, ways)
-        if by < 4:
+        if (axis, by) != ("z", 1):
             count = count + other_count
     far = lax.ppermute(near, "c", cross)
 
@@ -353,12 +350,10 @@
     arrived = [pieces[0]]
     for r in range(1, nx):
         arrived.append(lax.ppermute(pieces[r], "x", [(k, (k + r) % nx) for k in range(nx)]))
-    user_grad = call(finish_kernel, f32(rows, width), user_part)
-    user_grad, *arrived = lax.optimization_barrier((user_grad, *arrived))
-    bank_grad, loss = call(
-        functools.partial(gather_kernel, 1.0 / total_users),
-        (f32(height, width), f32(1, LANES)),
-        *arrived,
+    user_grad, bank_grad, loss = call(
+        functools.partial(finish_kernel, 1.0 / total_users),
+        (f32(rows, width), f32(height, width), f32(1, LANES)),
+        *(user_part, *arrived),
     )
     return loss[0, 0], user_grad, bank_grad
 

time: 109 us -> 104 us (0.954)
  starting transfers between devices: 37.4 us -> 32 us
  waiting for transfers between devices: 20.5 us -> 22.7 us
  blocking collectives: 36.6 us -> 35.5 us
    ppermute x4, starting transfers between devices: 7.08 us -> 2.88 us  [step(): other_count = lax.ppermute(count, axis, ways)]
    ppermute x4, waiting for transfers between devices: 8.06 us -> 10.8 us  [step(): other_count = lax.ppermute(count, axis, ways)]
    ppermute x1, starting transfers between devices: 5.93 us -> 3.22 us  [step(): other_near = lax.ppermute(near_stats, 'c', cross)]
    ppermute x3, starting transfers between devices: 2.77 us -> 4.44 us  [step(): lax.ppermute(pieces[r], 'x', [(k, (k + r) % nx) for k in range(nx)])]
    all_to_all x2, blocking collectives: 36.6 us -> 35.5 us  [exchange(): return lax.all_to_all(value, axis, split_axis=0, concat_axis=0, tiled=True)]
    pallas_call x10 -> x9, Pallas kernels: 12.5 us -> 11.8 us  [call(): pl.pallas_call(kernel, in_specs=[VMEM] * len(operands), out_specs=jax.tre...]
  transfers between devices with their start and end apart: 15 -> 15, of which waited for: 9 -> 7; matrix products, arithmetic and copies ran while one was open for 0% -> 0% of each run, Pallas kernels for 5% -> 5%
where the time goes in v7:
time: 104 us; the launch traced here: 103 us
  blocking collectives  35.5 us (34%)
  starting transfers between devices  32 us (31%)
  waiting for transfers between devices  22.7 us (22%)
  Pallas kernels  11.8 us (11%)
    all_to_all x2, blocking collectives, exchange(): return lax.all_to_all(value, axis, split_axis=0, concat_axis=0, tiled=True)  35.5 us
    pallas_call x9, Pallas kernels, call(): pl.pallas_call(kernel, in_specs=[VMEM] * len(operands), out_specs=jax.tre...  11.8 us
    ppermute x4, waiting for transfers between devices, step(): other_count = lax.ppermute(count, axis, ways)  10.8 us
    ppermute x1, starting transfers between devices, step(): item_block = lax.ppermute(bank, COLUMN, fetch)  7.75 us
    ppermute x1, waiting for transfers between devices, step(): bank_part = lax.ppermute(bank_part, COLUMN, [(b, a) for a, b in fetch])  6.5 us
    ppermute x1, starting transfers between devices, step(): theirs = lax.ppermute(bank_part[:half + 8], 'c', cross)  5.43 us
    all_to_all x1, starting transfers between devices, exchange(): return lax.all_to_all(value, axis, split_axis=0, concat_axis=0, tiled=True)  4.9 us
    ppermute x3, starting transfers between devices, step(): lax.ppermute(pieces[r], 'x', [(k, (k + r) % nx) for k in range(nx)])  4.44 us
  transfers between devices with their start and end apart: 15, of which 7 were waited for; matrix products, arithmetic and copies ran while one was open for 0% of the time, Pallas kernels for 5%

profile of v7, /device:TPU:2, one launch (start us, length us, event | category | flops | bytes accessed | tf_op | source)
XLA Modules:
  0.0 102.8 jit_solution(18051103257659970173)
XLA Ops:
  0.6 2.0 %shard_map.67 = (bf16[16,136,256]{2,1,0:T(8,128)(2,1)}, f32[8,128]{1,0:T(8,128)}) custom-call(bf16[128,256]{1,0:T(8,128)(2,1)} %users.1, s32[1,128]{1,0:T(1,128)} %bitcast.4, s32[1,128]{1,0:T(1,128)} %bitcast.5), custom_call_target="tpu_custom_call" | custom-call | tf_op jit(solution)/shard_map/pallas_call | solution.py:26
  2.6 24.1 %all_to_all.15.packed = bf16[16,136,256]{2,1,0:T(8,128)(2,1)S(1)} all-to-all(bf16[16,136,256]{2,1,0:T(8,128)(2,1)} %get-tuple-element.23), channel_id=1, replica_groups=mesh['y'=4,'z'=8,'x'=4,'c'=2] {'y','x'}, dimensions={0} | all-to-all | bytes 2228224 | tf_op jit(solution)/shard_map/all_to_all | solution.py:52
  26.7 7.8 %collective-permute-start = (bf16[512,256]{1,0:T(8,128)(2,1)S(1)}, bf16[512,256]{1,0:T(8,128)(2,1)S(1)}, u32[]{:S(2)}, u32[]{:S(2)}) collective-permute-start(bf16[512,256]{1,0:T(8,128)(2,1)S(1)} %copy-done.1), channel_id=1, source_target_pairs={{0,0},{33,1},{10,2},{43,3},{60,4},{29,5},{22,6},{55,7},{8,8},{41,9... | collective-permute-start | bytes 786440 | tf_op jit(solution)/shard_map/ppermute | solution.py:306
  34.5 1.5 %collective-permute-start.4 = (f32[8,128]{1,0:T(8,128)S(1)}, f32[8,128]{1,0:T(8,128)S(1)}, u32[]{:S(2)}, u32[]{:S(2)}) collective-permute-start(f32[8,128]{1,0:T(8,128)S(1)} %copy-done), channel_id=1, source_target_pairs={{0,32},{8,40},{16,48},{24,56},{32,0},{40,8},{48,16},{56,24},{1,33}... | collective-permute-start | bytes 12296 | tf_op jit(solution)/shard_map/ppermute | solution.py:309
  36.0 6.4 %collective-permute-done.4 = f32[8,128]{1,0:T(8,128)S(1)} collective-permute-done((f32[8,128]{1,0:T(8,128)S(1)}, f32[8,128]{1,0:T(8,128)S(1)}, u32[]{:S(2)}, u32[]{:S(2)}) %collective-permute-start.4) | collective-permute-done | bytes 4128 | tf_op jit(solution)/shard_map/ppermute | solution.py:309
  42.4 0.9 collective-permute-start.5
  43.3 1.7 %shard_map.68 = (f32[24,128]{1,0:T(8,128)S(1)}, f32[16,128]{1,0:T(8,128)S(1)}) custom-call(bf16[16,136,256]{2,1,0:T(8,128)(2,1)S(1)} %all_to_all.15.packed, bf16[512,256]{1,0:T(8,128)(2,1)S(1)} %collective-permute-done.bank), custom_call_target="tpu_custom_call" | custom-call | tf_op jit(solution)/shard_map/pallas_call | solution.py:26
  45.0 3.2 %collective-permute-start.2 = (f32[24,128]{1,0:T(8,128)S(1)}, f32[24,128]{1,0:T(8,128)S(1)}, u32[]{:S(2)}, u32[]{:S(2)}) collective-permute-start(f32[24,128]{1,0:T(8,128)S(1)} %get-tuple-element.24.near), channel_id=1, source_target_pairs={{0,1},{1,0},{2,3},{3,2},{4,5},{5,4},{6,7},{7,6},{8,9},{9,8},{10,11... | collective-permute-start | bytes 36872 | tf_op jit(solution)/shard_map/ppermute | solution.py:315
  48.2 1.7 %shard_map.69 = (f32[24,128]{1,0:T(8,128)S(1)}, f32[16,128]{1,0:T(8,128)S(1)}) custom-call(bf16[16,136,256]{2,1,0:T(8,128)(2,1)S(1)} %collective-permute-done.1.packed, bf16[512,256]{1,0:T(8,128)(2,1)S(1)} %collective-permute-done.bank), custom_call_target="tpu_custom_call" | custom-call | tf_op jit(solution)/shard_map/pallas_call | solution.py:26
  51.4 3.6 %collective-permute-done.7.other_count = f32[8,128]{1,0:T(8,128)S(1)} collective-permute-done((f32[8,128]{1,0:T(8,128)S(1)}, f32[8,128]{1,0:T(8,128)S(1)}, u32[]{:S(2)}, u32[]{:S(2)}) %collective-permute-start.7) | collective-permute-done | bytes 4128 | tf_op jit(solution)/shard_map/ppermute | solution.py:309
  55.0 11.4 %all_to_all.16.stats = f32[16,40,128]{2,1,0:T(8,128)S(1)} all-to-all(f32[16,40,128]{2,1,0:T(8,128)S(1)} %shard_map.70), channel_id=1, replica_groups=mesh['y'=4,'z'=8,'x'=4,'c'=2] {'y','x'}, dimensions={0} | all-to-all | bytes 655360 | tf_op jit(solution)/shard_map/all_to_all | solution.py:52
  66.4 2.2 %shard_map.71 = (bf16[16,256,128]{2,1,0:T(8,128)(2,1)S(1)}, f32[512,256]{1,0:T(8,128)S(1)}, f32[32,128]{1,0:T(8,128)S(1)}, f32[16,128]{1,0:T(8,128)S(1)}, f32[8,128]{1,0:T(8,128)S(1)}) custom-call(bf16[16,136,256]{2,1,0:T(8,128)(2,1)S(1)} %collective-permute-done.1.packed, bf16[512,256]{1,0:T(8,128)(2,1)S(1)} %collective-permute-done.bank, ...), custom_call_target="tpu_custom_call" | custom-call | tf_op jit(solution)/shard_map/pallas_call | solution.py:26
  69.0 1.5 %shard_map.72 = (bf16[4,512,512]{2,1,0:T(8,128)(2,1)S(1)}, bf16[520,256]{1,0:T(8,128)(2,1)S(1)}) custom-call(bf16[16,136,256]{2,1,0:T(8,128)(2,1)S(1)} %all_to_all.15.packed, bf16[512,256]{1,0:T(8,128)(2,1)S(1)} %collective-permute-done.bank, f32[32,128]{1,0:T(8,128)S(1)} %get-tuple-element.29.lse, f32[16,128]{1,0:T(8,128)S(1)} %get-tuple-element.30.weight, ...), custom_call_target="tpu_custom_call" | custom-call | tf_op jit(solution)/shard_map/pallas_call | solution.py:26
  70.5 1.1 %collective-permute-done.8.far_part = bf16[16,256,128]{2,1,0:T(8,128)(2,1)S(1)} collective-permute-done((bf16[16,256,128]{2,1,0:T(8,128)(2,1)S(1)}, bf16[16,256,128]{2,1,0:T(8,128)(2,1)S(1)}, u32[]{:S(2)}, u32[]{:S(2)}) %collective-permute-start.8) | collective-permute-done | bytes 1048608 | tf_op jit(solution)/shard_map/ppermute | solution.py:336
  71.6 1.7 %shard_map.73 = bf16[16,256,128]{2,1,0:T(8,128)(2,1)} custom-call(bf16[4,512,512]{2,1,0:T(8,128)(2,1)S(1)} %get-tuple-element.33.kept, bf16[512,256]{1,0:T(8,128)(2,1)S(1)} %collective-permute-done.bank, bf16[16,256,128]{2,1,0:T(8,128)(2,1)S(1)} %collective-permute-done.8.far_part), custom_call_target="tpu_custom_call" | custom-call | tf_op jit(solution)/shard_map/pallas_call | solution.py:26
  73.3 4.9 %all-to-all-start.2 = ((bf16[16,256,128]{2,1,0:T(8,128)(2,1)}), bf16[16,256,128]{2,1,0:T(8,128)(2,1)S(1)}, u32[]{:S(2)}, u32[]{:S(2)}) async-start(bf16[16,256,128]{2,1,0:T(8,128)(2,1)} %shard_map.73), calls=%async_computation.2 | async-start | bytes 2097152 | tf_op jit(solution)/shard_map/all_to_all | solution.py:52
  78.2 3.0 %collective-permute-start.9 = (bf16[520,256]{1,0:T(8,128)(2,1)S(1)}, bf16[520,256]{1,0:T(8,128)(2,1)S(1)}, u32[]{:S(2)}, u32[]{:S(2)}) collective-permute-start(bf16[520,256]{1,0:T(8,128)(2,1)S(1)} %get-tuple-element.35), channel_id=1, source_target_pairs={{0,0},{1,33},{2,10},{3,43},{4,60},{5,29},{6,22},{7,55},{8,8},{9,41... | collective-permute-start | bytes 798728 | tf_op jit(solution)/shard_map/ppermute | solution.py:343
  81.2 6.5 %collective-permute-done.9.mine = bf16[520,256]{1,0:T(8,128)(2,1)S(1)} collective-permute-done((bf16[520,256]{1,0:T(8,128)(2,1)S(1)}, bf16[520,256]{1,0:T(8,128)(2,1)S(1)}, u32[]{:S(2)}, u32[]{:S(2)}) %collective-permute-start.9) | collective-permute-done | bytes 266272 | tf_op jit(solution)/shard_map/ppermute | solution.py:343
  87.8 5.4 %collective-permute-start.10 = (bf16[264,256]{1,0:T(8,128)(2,1)S(1)}, bf16[264,256]{1,0:T(8,128)(2,1)S(1)}, u32[]{:S(2)}, u32[]{:S(2)}) collective-permute-start(bf16[264,256]{1,0:T(8,128)(2,1)S(1)} %slice.8), channel_id=1, source_target_pairs={{0,1},{1,0},{2,3},{3,2},{4,5},{5,4},{6,7},{7,6},{8,9},{9,8},{10,11... | collective-permute-start | bytes 405512 | tf_op jit(solution)/shard_map/ppermute | solution.py:348
  93.2 1.0 collective-permute-done.10.theirs
  94.2 2.3 %collective-permute-start.11 = (bf16[72,256]{1,0:T(8,128)(2,1)S(1)}, bf16[72,256]{1,0:T(8,128)(2,1)S(1)}, u32[]{:S(2)}, u32[]{:S(2)}) collective-permute-start(bf16[72,256]{1,0:T(8,128)(2,1)S(1)} %get-tuple-element.37), channel_id=1, source_target_pairs={{0,2},{2,4},{4,6},{6,0},{1,3},{3,5},{5,7},{7,1},{8,10},{10,12},{12... | collective-permute-start | bytes 110600 | tf_op jit(solution)/shard_map/ppermute | solution.py:352
  96.5 2.2 %collective-permute-start.13 = (bf16[72,256]{1,0:T(8,128)(2,1)S(1)}, bf16[72,256]{1,0:T(8,128)(2,1)S(1)}, u32[]{:S(2)}, u32[]{:S(2)}) collective-permute-start(bf16[72,256]{1,0:T(8,128)(2,1)S(1)} %get-tuple-element.39), channel_id=1, source_target_pairs={{0,6},{2,0},{4,2},{6,4},{1,7},{3,1},{5,3},{7,5},{8,14},{10,8},{12,... | collective-permute-start | bytes 110600 | tf_op jit(solution)/shard_map/ppermute | solution.py:352
  98.7 3.3 %collective-permute-done.12.refs_2_ = bf16[72,256]{1,0:T(8,128)(2,1)S(1)} collective-permute-done((bf16[72,256]{1,0:T(8,128)(2,1)S(1)}, bf16[72,256]{1,0:T(8,128)(2,1)S(1)}, u32[]{:S(2)}, u32[]{:S(2)}) %collective-permute-start.12) | collective-permute-done | bytes 36896 | tf_op jit(solution)/shard_map/ppermute | solution.py:352
  102.0 0.9 shard_map.75
  (25 shorter events, 1.8 us)
Async XLA Ops:
  2.6 24.1 %copy-start.1 = (bf16[512,256]{1,0:T(8,128)(2,1)S(1)}, bf16[512,256]{1,0:T(8,128)(2,1)}, u32[]{:S(2)}) copy-start(bf16[512,256]{1,0:T(8,128)(2,1)} %param.5) | copy-start | bytes 786436
  2.6 31.9 %copy-start = (f32[8,128]{1,0:T(8,128)S(1)}, f32[8,128]{1,0:T(8,128)}, u32[]{:S(2)}) copy-start(f32[8,128]{1,0:T(8,128)} %get-tuple-element.26) | copy-start | bytes 12292
  26.7 21.5 %collective-permute-start.1 = (bf16[16,136,256]{2,1,0:T(8,128)(2,1)S(1)}, bf16[16,136,256]{2,1,0:T(8,128)(2,1)S(1)}, u32[]{:S(2)}, u32[]{:S(2)}) collective-permute-start(bf16[16,136,256]{2,1,0:T(8,128)(2,1)S(1)} %all_to_all.15.packed), channel_id=1, source_target_pairs={{0,1},{1,0},{2,3},{3,2},{4,5},{5,4},{6,7},{7,6},{8,9},{9,8},{10,11... | collective-permute-start | bytes 3342344 | tf_op jit(solution)/shard_map/ppermute | solution.py:312
  26.7 16.5 %collective-permute-start = (bf16[512,256]{1,0:T(8,128)(2,1)S(1)}, bf16[512,256]{1,0:T(8,128)(2,1)S(1)}, u32[]{:S(2)}, u32[]{:S(2)}) collective-permute-start(bf16[512,256]{1,0:T(8,128)(2,1)S(1)} %copy-done.1), channel_id=1, source_target_pairs={{0,0},{33,1},{10,2},{43,3},{60,4},{29,5},{22,6},{55,7},{8,8},{41,9... | collective-permute-start | bytes 786440 | tf_op jit(solution)/shard_map/ppermute | solution.py:306
  34.5 7.9 %collective-permute-start.4 = (f32[8,128]{1,0:T(8,128)S(1)}, f32[8,128]{1,0:T(8,128)S(1)}, u32[]{:S(2)}, u32[]{:S(2)}) collective-permute-start(f32[8,128]{1,0:T(8,128)S(1)} %copy-done), channel_id=1, source_target_pairs={{0,32},{8,40},{16,48},{24,56},{32,0},{40,8},{48,16},{56,24},{1,33}... | collective-permute-start | bytes 12296 | tf_op jit(solution)/shard_map/ppermute | solution.py:309
  42.4 7.7 %collective-permute-start.5 = (f32[8,128]{1,0:T(8,128)S(1)}, f32[8,128]{1,0:T(8,128)S(1)}, u32[]{:S(2)}, u32[]{:S(2)}) collective-permute-start(f32[8,128]{1,0:T(8,128)S(1)} %add.9), channel_id=1, source_target_pairs={{0,16},{8,24},{16,0},{24,8},{32,48},{40,56},{48,32},{56,40},{1,17}... | collective-permute-start | bytes 12296 | tf_op jit(solution)/shard_map/ppermute | solution.py:309
  45.0 10.0 %collective-permute-start.2 = (f32[24,128]{1,0:T(8,128)S(1)}, f32[24,128]{1,0:T(8,128)S(1)}, u32[]{:S(2)}, u32[]{:S(2)}) collective-permute-start(f32[24,128]{1,0:T(8,128)S(1)} %get-tuple-element.24.near), channel_id=1, source_target_pairs={{0,1},{1,0},{2,3},{3,2},{4,5},{5,4},{6,7},{7,6},{8,9},{9,8},{10,11... | collective-permute-start | bytes 36872 | tf_op jit(solution)/shard_map/ppermute | solution.py:315
  50.0 5.0 %collective-permute-start.3 = (f32[24,128]{1,0:T(8,128)S(1)}, f32[24,128]{1,0:T(8,128)S(1)}, u32[]{:S(2)}, u32[]{:S(2)}) collective-permute-start(f32[24,128]{1,0:T(8,128)S(1)} %get-tuple-element.25.far), channel_id=1, source_target_pairs={{0,1},{1,0},{2,3},{3,2},{4,5},{5,4},{6,7},{7,6},{8,9},{9,8},{10,11... | collective-permute-start | bytes 36872 | tf_op jit(solution)/shard_map/ppermute | solution.py:317
  50.1 1.3 %collective-permute-start.6 = (f32[8,128]{1,0:T(8,128)S(1)}, f32[8,128]{1,0:T(8,128)S(1)}, u32[]{:S(2)}, u32[]{:S(2)}) collective-permute-start(f32[8,128]{1,0:T(8,128)S(1)} %add.10), channel_id=1, source_target_pairs={{0,1},{1,0},{2,3},{3,2},{4,5},{5,4},{6,7},{7,6},{8,9},{9,8},{10,11... | collective-permute-start | bytes 12296 | tf_op jit(solution)/shard_map/ppermute | solution.py:309
  51.4 3.6 %collective-permute-start.7 = (f32[8,128]{1,0:T(8,128)S(1)}, f32[8,128]{1,0:T(8,128)S(1)}, u32[]{:S(2)}, u32[]{:S(2)}) collective-permute-start(f32[8,128]{1,0:T(8,128)S(1)} %add.11.count), channel_id=1, source_target_pairs={{0,8},{8,0},{16,24},{24,16},{32,40},{40,32},{48,56},{56,48},{1,9},... | collective-permute-start | bytes 12296 | tf_op jit(solution)/shard_map/ppermute | solution.py:309
  68.7 2.9 %collective-permute-start.8 = (bf16[16,256,128]{2,1,0:T(8,128)(2,1)S(1)}, bf16[16,256,128]{2,1,0:T(8,128)(2,1)S(1)}, u32[]{:S(2)}, u32[]{:S(2)}) collective-permute-start(bf16[16,256,128]{2,1,0:T(8,128)(2,1)S(1)} %get-tuple-element.34), channel_id=1, source_target_pairs={{0,1},{1,0},{2,3},{3,2},{4,5},{5,4},{6,7},{7,6},{8,9},{9,8},{10,11... | collective-permute-start | bytes 3145736 | tf_op jit(solution)/shard_map/ppermute | solution.py:336
  73.3 28.6 %all-to-all-start.2 = ((bf16[16,256,128]{2,1,0:T(8,128)(2,1)}), bf16[16,256,128]{2,1,0:T(8,128)(2,1)S(1)}, u32[]{:S(2)}, u32[]{:S(2)}) async-start(bf16[16,256,128]{2,1,0:T(8,128)(2,1)} %shard_map.73), calls=%async_computation.2 | async-start | bytes 2097152 | tf_op jit(solution)/shard_map/all_to_all | solution.py:52
  78.2 9.5 %collective-permute-start.9 = (bf16[520,256]{1,0:T(8,128)(2,1)S(1)}, bf16[520,256]{1,0:T(8,128)(2,1)S(1)}, u32[]{:S(2)}, u32[]{:S(2)}) collective-permute-start(bf16[520,256]{1,0:T(8,128)(2,1)S(1)} %get-tuple-element.35), channel_id=1, source_target_pairs={{0,0},{1,33},{2,10},{3,43},{4,60},{5,29},{6,22},{7,55},{8,8},{9,41... | collective-permute-start | bytes 798728 | tf_op jit(solution)/shard_map/ppermute | solution.py:343
  87.8 6.4 %collective-permute-start.10 = (bf16[264,256]{1,0:T(8,128)(2,1)S(1)}, bf16[264,256]{1,0:T(8,128)(2,1)S(1)}, u32[]{:S(2)}, u32[]{:S(2)}) collective-permute-start(bf16[264,256]{1,0:T(8,128)(2,1)S(1)} %slice.8), channel_id=1, source_target_pairs={{0,1},{1,0},{2,3},{3,2},{4,5},{5,4},{6,7},{7,6},{8,9},{9,8},{10,11... | collective-permute-start | bytes 405512 | tf_op jit(solution)/shard_map/ppermute | solution.py:348
  94.2 4.4 %collective-permute-start.11 = (bf16[72,256]{1,0:T(8,128)(2,1)S(1)}, bf16[72,256]{1,0:T(8,128)(2,1)S(1)}, u32[]{:S(2)}, u32[]{:S(2)}) collective-permute-start(bf16[72,256]{1,0:T(8,128)(2,1)S(1)} %get-tuple-element.37), channel_id=1, source_target_pairs={{0,2},{2,4},{4,6},{6,0},{1,3},{3,5},{5,7},{7,1},{8,10},{10,12},{12... | collective-permute-start | bytes 110600 | tf_op jit(solution)/shard_map/ppermute | solution.py:352
  96.5 5.5 %collective-permute-start.12 = (bf16[72,256]{1,0:T(8,128)(2,1)S(1)}, bf16[72,256]{1,0:T(8,128)(2,1)S(1)}, u32[]{:S(2)}, u32[]{:S(2)}) collective-permute-start(bf16[72,256]{1,0:T(8,128)(2,1)S(1)} %get-tuple-element.38), channel_id=1, source_target_pairs={{0,4},{2,6},{4,0},{6,2},{1,5},{3,7},{5,1},{7,3},{8,12},{10,14},{12... | collective-permute-start | bytes 110600 | tf_op jit(solution)/shard_map/ppermute | solution.py:352
  96.5 5.5 %collective-permute-start.13 = (bf16[72,256]{1,0:T(8,128)(2,1)S(1)}, bf16[72,256]{1,0:T(8,128)(2,1)S(1)}, u32[]{:S(2)}, u32[]{:S(2)}) collective-permute-start(bf16[72,256]{1,0:T(8,128)(2,1)S(1)} %get-tuple-element.39), channel_id=1, source_target_pairs={{0,6},{2,0},{4,2},{6,4},{1,7},{3,1},{5,3},{7,5},{8,14},{10,8},{12,... | collective-permute-start | bytes 110600 | tf_op jit(solution)/shard_map/ppermute | solution.py:352

commit v8 on v7

--- a/solution.py
+++ b/solution.py
@@ -169,7 +169,8 @@
         rest += stats[k, both:]
     lse = top + jnp.log(total)
     lse_out[...] = lse
-    per_cohort = scale / row_to_column(rest[1:2])
+    counts = row_to_column(rest[1:2])
+    per_cohort = jnp.where(counts > 0, scale / jnp.maximum(counts, F32(1)), F32(0))
     weight_out[...] = jnp.broadcast_to(per_cohort, weight_out.shape)
     weights = jnp.zeros((both, LANES), F32)
     cohorts = jnp.concatenate([coh_near[...], coh_far[...]], axis=0)
@@ -304,11 +305,11 @@
     )
     near = exchange(packed, PLANE)
     item_block = lax.ppermute(bank, COLUMN, fetch)
-    for axis, by in (("z", 4), ("z", 2), ("c", 1), ("z", 1)):
-        ways = [(k, k ^ by) for k in range(lax.axis_size(axis))]
-        other_count = lax.ppermute(count, axis, ways)
-        if (axis, by) != ("z", 1):
-            count = count + other_count
+    flip = lambda axis, by: [(k, k ^ by) for k in range(lax.axis_size(axis))]
+    others = [lax.ppermute(count, "z", flip("z", by)) for by in (4, 6, 2)]
+    count = count + others[0] + others[1] + others[2]
+    count = count + lax.ppermute(count, "c", cross)
+    other_count = lax.ppermute(count, "z", flip("z", 1))
     far = lax.ppermute(near, "c", cross)
 
     near_stats, near_coh = forward(near, item_block, rows)

time: 104 us -> 103 us (level)
  waiting for transfers between devices: 22.7 us -> 15.8 us
  starting transfers between devices: 32 us -> 35.8 us
  blocking collectives: 35.5 us -> 36.9 us
    ppermute x4 -> x5, waiting for transfers between devices: 10.8 us -> 2.91 us  [the longest x1 2.07 us: step(): other_count = lax.ppermute(count, 'z', flip('z', 1))]
    ppermute x4 -> x5, starting transfers between devices: 2.88 us -> 8.67 us  [the longest x3 6.58 us: step(): others = [lax.ppermute(count, 'z', flip('z', by)) for by in (4, 6, 2)]]
    ppermute x3, starting transfers between devices: 4.44 us -> 2.86 us  [step(): lax.ppermute(pieces[r], 'x', [(k, (k + r) % nx) for k in range(nx)])]
    all_to_all x2, blocking collectives: 35.5 us -> 36.9 us  [exchange(): return lax.all_to_all(value, axis, split_axis=0, concat_axis=0, tiled=True)]
  transfers between devices with their start and end apart: 15 -> 16, of which waited for: 7 -> 7; matrix products, arithmetic and copies ran while one was open for 0% -> 0% of each run, Pallas kernels for 5% -> 5%
where the time goes in v8:
time: 103 us; the launch traced here: 101 us
  blocking collectives  36.9 us (36%)
  starting transfers between devices  35.8 us (35%)
  waiting for transfers between devices  15.8 us (15%)
  Pallas kernels  11.9 us (12%)
    all_to_all x2, blocking collectives, exchange(): return lax.all_to_all(value, axis, split_axis=0, concat_axis=0, tiled=True)  36.9 us
    pallas_call x9, Pallas kernels, call(): pl.pallas_call(kernel, in_specs=[VMEM] * len(operands), out_specs=jax.tre...  11.9 us
    ppermute x1, starting transfers between devices, step(): item_block = lax.ppermute(bank, COLUMN, fetch)  7.75 us
    ppermute x1, waiting for transfers between devices, step(): bank_part = lax.ppermute(bank_part, COLUMN, [(b, a) for a, b in fetch])  7.42 us
    ppermute x3, starting transfers between devices, step(): others = [lax.ppermute(count, 'z', flip('z', by)) for by in (4, 6, 2)]  6.58 us
    ppermute x1, starting transfers between devices, step(): theirs = lax.ppermute(bank_part[:half + 8], 'c', cross)  5.93 us
    all_to_all x1, starting transfers between devices, exchange(): return lax.all_to_all(value, axis, split_axis=0, concat_axis=0, tiled=True)  4.9 us
    ppermute x3, waiting for transfers between devices, step(): lax.ppermute(pieces[r], 'x', [(k, (k + r) % nx) for k in range(nx)])  3.33 us
  transfers between devices with their start and end apart: 16, of which 7 were waited for; matrix products, arithmetic and copies ran while one was open for 0% of the time, Pallas kernels for 5%

profile of v8, /device:TPU:2, one launch (start us, length us, event | category | flops | bytes accessed | tf_op | source)
XLA Modules:
  0.0 101.1 jit_solution(603286801196241415)
XLA Ops:
  0.6 2.0 %shard_map.67 = (bf16[16,136,256]{2,1,0:T(8,128)(2,1)}, f32[8,128]{1,0:T(8,128)}) custom-call(bf16[128,256]{1,0:T(8,128)(2,1)} %users.1, s32[1,128]{1,0:T(1,128)} %bitcast.4, s32[1,128]{1,0:T(1,128)} %bitcast.5), custom_call_target="tpu_custom_call" | custom-call | tf_op jit(solution)/shard_map/pallas_call | solution.py:26
  2.6 24.1 %all_to_all.15.packed = bf16[16,136,256]{2,1,0:T(8,128)(2,1)S(1)} all-to-all(bf16[16,136,256]{2,1,0:T(8,128)(2,1)} %get-tuple-element.23), channel_id=1, replica_groups=mesh['y'=4,'z'=8,'x'=4,'c'=2] {'y','x'}, dimensions={0} | all-to-all | bytes 2228224 | tf_op jit(solution)/shard_map/all_to_all | solution.py:52
  26.7 7.8 %collective-permute-start = (bf16[512,256]{1,0:T(8,128)(2,1)S(1)}, bf16[512,256]{1,0:T(8,128)(2,1)S(1)}, u32[]{:S(2)}, u32[]{:S(2)}) collective-permute-start(bf16[512,256]{1,0:T(8,128)(2,1)S(1)} %copy-done.1), channel_id=1, source_target_pairs={{0,0},{33,1},{10,2},{43,3},{60,4},{29,5},{22,6},{55,7},{8,8},{41,9... | collective-permute-start | bytes 786440 | tf_op jit(solution)/shard_map/ppermute | solution.py:307
  34.6 2.0 %collective-permute-start.5 = (f32[8,128]{1,0:T(8,128)S(1)}, f32[8,128]{1,0:T(8,128)S(1)}, u32[]{:S(2)}, u32[]{:S(2)}) collective-permute-start(f32[8,128]{1,0:T(8,128)S(1)} %copy-done), channel_id=1, source_target_pairs={{0,48},{8,56},{16,32},{24,40},{32,16},{40,24},{48,0},{56,8},{1,49}... | collective-permute-start | bytes 12296 | tf_op jit(solution)/shard_map/ppermute | solution.py:309
  36.6 4.5 %collective-permute-start.4 = (f32[8,128]{1,0:T(8,128)S(1)}, f32[8,128]{1,0:T(8,128)S(1)}, u32[]{:S(2)}, u32[]{:S(2)}) collective-permute-start(f32[8,128]{1,0:T(8,128)S(1)} %copy-done), channel_id=1, source_target_pairs={{0,32},{8,40},{16,48},{24,56},{32,0},{40,8},{48,16},{56,24},{1,33}... | collective-permute-start | bytes 12296 | tf_op jit(solution)/shard_map/ppermute | solution.py:309
  41.1 1.7 %shard_map.68 = (f32[24,128]{1,0:T(8,128)S(1)}, f32[16,128]{1,0:T(8,128)S(1)}) custom-call(bf16[16,136,256]{2,1,0:T(8,128)(2,1)S(1)} %all_to_all.15.packed, bf16[512,256]{1,0:T(8,128)(2,1)S(1)} %collective-permute-done.bank), custom_call_target="tpu_custom_call" | custom-call | tf_op jit(solution)/shard_map/pallas_call | solution.py:26
  42.8 3.2 %collective-permute-start.2 = (f32[24,128]{1,0:T(8,128)S(1)}, f32[24,128]{1,0:T(8,128)S(1)}, u32[]{:S(2)}, u32[]{:S(2)}) collective-permute-start(f32[24,128]{1,0:T(8,128)S(1)} %get-tuple-element.24.near), channel_id=1, source_target_pairs={{0,1},{1,0},{2,3},{3,2},{4,5},{5,4},{6,7},{7,6},{8,9},{9,8},{10,11... | collective-permute-start | bytes 36872 | tf_op jit(solution)/shard_map/ppermute | solution.py:316
  46.1 1.7 %shard_map.69 = (f32[24,128]{1,0:T(8,128)S(1)}, f32[16,128]{1,0:T(8,128)S(1)}) custom-call(bf16[16,136,256]{2,1,0:T(8,128)(2,1)S(1)} %collective-permute-done.1.packed, bf16[512,256]{1,0:T(8,128)(2,1)S(1)} %collective-permute-done.bank), custom_call_target="tpu_custom_call" | custom-call | tf_op jit(solution)/shard_map/pallas_call | solution.py:26
  49.3 1.5 %collective-permute-start.8 = (f32[8,128]{1,0:T(8,128)S(1)}, f32[8,128]{1,0:T(8,128)S(1)}, u32[]{:S(2)}, u32[]{:S(2)}) collective-permute-start(f32[8,128]{1,0:T(8,128)S(1)} %add.15.count), channel_id=1, source_target_pairs={{0,8},{8,0},{16,24},{24,16},{32,40},{40,32},{48,56},{56,48},{1,9},... | collective-permute-start | bytes 12296 | tf_op jit(solution)/shard_map/ppermute | solution.py:312
  50.9 2.1 %collective-permute-done.8.other_count = f32[8,128]{1,0:T(8,128)S(1)} collective-permute-done((f32[8,128]{1,0:T(8,128)S(1)}, f32[8,128]{1,0:T(8,128)S(1)}, u32[]{:S(2)}, u32[]{:S(2)}) %collective-permute-start.8) | collective-permute-done | bytes 4128 | tf_op jit(solution)/shard_map/ppermute | solution.py:312
  53.0 12.8 %all_to_all.16.stats = f32[16,40,128]{2,1,0:T(8,128)S(1)} all-to-all(f32[16,40,128]{2,1,0:T(8,128)S(1)} %shard_map.70), channel_id=1, replica_groups=mesh['y'=4,'z'=8,'x'=4,'c'=2] {'y','x'}, dimensions={0} | all-to-all | bytes 655360 | tf_op jit(solution)/shard_map/all_to_all | solution.py:52
  65.7 2.2 %shard_map.71 = (bf16[16,256,128]{2,1,0:T(8,128)(2,1)S(1)}, f32[512,256]{1,0:T(8,128)S(1)}, f32[32,128]{1,0:T(8,128)S(1)}, f32[16,128]{1,0:T(8,128)S(1)}, f32[8,128]{1,0:T(8,128)S(1)}) custom-call(bf16[16,136,256]{2,1,0:T(8,128)(2,1)S(1)} %collective-permute-done.1.packed, bf16[512,256]{1,0:T(8,128)(2,1)S(1)} %collective-permute-done.bank, ...), custom_call_target="tpu_custom_call" | custom-call | tf_op jit(solution)/shard_map/pallas_call | solution.py:26
  68.3 1.5 %shard_map.72 = (bf16[4,512,512]{2,1,0:T(8,128)(2,1)S(1)}, bf16[520,256]{1,0:T(8,128)(2,1)S(1)}) custom-call(bf16[16,136,256]{2,1,0:T(8,128)(2,1)S(1)} %all_to_all.15.packed, bf16[512,256]{1,0:T(8,128)(2,1)S(1)} %collective-permute-done.bank, f32[32,128]{1,0:T(8,128)S(1)} %get-tuple-element.29.lse, f32[16,128]{1,0:T(8,128)S(1)} %get-tuple-element.30.weight, ...), custom_call_target="tpu_custom_call" | custom-call | tf_op jit(solution)/shard_map/pallas_call | solution.py:26
  69.8 1.1 %collective-permute-done.9.far_part = bf16[16,256,128]{2,1,0:T(8,128)(2,1)S(1)} collective-permute-done((bf16[16,256,128]{2,1,0:T(8,128)(2,1)S(1)}, bf16[16,256,128]{2,1,0:T(8,128)(2,1)S(1)}, u32[]{:S(2)}, u32[]{:S(2)}) %collective-permute-start.9) | collective-permute-done | bytes 1048608 | tf_op jit(solution)/shard_map/ppermute | solution.py:337
  70.9 1.7 %shard_map.73 = bf16[16,256,128]{2,1,0:T(8,128)(2,1)} custom-call(bf16[4,512,512]{2,1,0:T(8,128)(2,1)S(1)} %get-tuple-element.33.kept, bf16[512,256]{1,0:T(8,128)(2,1)S(1)} %collective-permute-done.bank, bf16[16,256,128]{2,1,0:T(8,128)(2,1)S(1)} %collective-permute-done.9.far_part), custom_call_target="tpu_custom_call" | custom-call | tf_op jit(solution)/shard_map/pallas_call | solution.py:26
  72.6 4.9 %all-to-all-start.2 = ((bf16[16,256,128]{2,1,0:T(8,128)(2,1)}), bf16[16,256,128]{2,1,0:T(8,128)(2,1)S(1)}, u32[]{:S(2)}, u32[]{:S(2)}) async-start(bf16[16,256,128]{2,1,0:T(8,128)(2,1)} %shard_map.73), calls=%async_computation.2 | async-start | bytes 2097152 | tf_op jit(solution)/shard_map/all_to_all | solution.py:52
  77.6 2.1 %collective-permute-start.10 = (bf16[520,256]{1,0:T(8,128)(2,1)S(1)}, bf16[520,256]{1,0:T(8,128)(2,1)S(1)}, u32[]{:S(2)}, u32[]{:S(2)}) collective-permute-start(bf16[520,256]{1,0:T(8,128)(2,1)S(1)} %get-tuple-element.35), channel_id=1, source_target_pairs={{0,0},{1,33},{2,10},{3,43},{4,60},{5,29},{6,22},{7,55},{8,8},{9,41... | collective-permute-start | bytes 798728 | tf_op jit(solution)/shard_map/ppermute | solution.py:344
  79.6 7.4 %collective-permute-done.10.mine = bf16[520,256]{1,0:T(8,128)(2,1)S(1)} collective-permute-done((bf16[520,256]{1,0:T(8,128)(2,1)S(1)}, bf16[520,256]{1,0:T(8,128)(2,1)S(1)}, u32[]{:S(2)}, u32[]{:S(2)}) %collective-permute-start.10) | collective-permute-done | bytes 266272 | tf_op jit(solution)/shard_map/ppermute | solution.py:344
  87.1 5.9 %collective-permute-start.11 = (bf16[264,256]{1,0:T(8,128)(2,1)S(1)}, bf16[264,256]{1,0:T(8,128)(2,1)S(1)}, u32[]{:S(2)}, u32[]{:S(2)}) collective-permute-start(bf16[264,256]{1,0:T(8,128)(2,1)S(1)} %slice.8), channel_id=1, source_target_pairs={{0,1},{1,0},{2,3},{3,2},{4,5},{5,4},{6,7},{7,6},{8,9},{9,8},{10,11... | collective-permute-start | bytes 405512 | tf_op jit(solution)/shard_map/ppermute | solution.py:349
  93.0 1.0 collective-permute-done.11.theirs
  94.7 2.2 %collective-permute-start.14 = (bf16[72,256]{1,0:T(8,128)(2,1)S(1)}, bf16[72,256]{1,0:T(8,128)(2,1)S(1)}, u32[]{:S(2)}, u32[]{:S(2)}) collective-permute-start(bf16[72,256]{1,0:T(8,128)(2,1)S(1)} %get-tuple-element.39), channel_id=1, source_target_pairs={{0,6},{2,0},{4,2},{6,4},{1,7},{3,1},{5,3},{7,5},{8,14},{10,8},{12,... | collective-permute-start | bytes 110600 | tf_op jit(solution)/shard_map/ppermute | solution.py:353
  96.9 1.4 %collective-permute-done.12.refs_1_ = bf16[72,256]{1,0:T(8,128)(2,1)S(1)} collective-permute-done((bf16[72,256]{1,0:T(8,128)(2,1)S(1)}, bf16[72,256]{1,0:T(8,128)(2,1)S(1)}, u32[]{:S(2)}, u32[]{:S(2)}) %collective-permute-start.12) | collective-permute-done | bytes 36896 | tf_op jit(solution)/shard_map/ppermute | solution.py:353
  98.3 1.9 %collective-permute-done.13.refs_2_ = bf16[72,256]{1,0:T(8,128)(2,1)S(1)} collective-permute-done((bf16[72,256]{1,0:T(8,128)(2,1)S(1)}, bf16[72,256]{1,0:T(8,128)(2,1)S(1)}, u32[]{:S(2)}, u32[]{:S(2)}) %collective-permute-start.13) | collective-permute-done | bytes 36896 | tf_op jit(solution)/shard_map/ppermute | solution.py:353
  100.2 0.9 shard_map.75
  (26 shorter events, 2.7 us)
Async XLA Ops:
  2.6 24.1 %copy-start.1 = (bf16[512,256]{1,0:T(8,128)(2,1)S(1)}, bf16[512,256]{1,0:T(8,128)(2,1)}, u32[]{:S(2)}) copy-start(bf16[512,256]{1,0:T(8,128)(2,1)} %param.5) | copy-start | bytes 786436
  2.6 31.9 %copy-start = (f32[8,128]{1,0:T(8,128)S(1)}, f32[8,128]{1,0:T(8,128)}, u32[]{:S(2)}) copy-start(f32[8,128]{1,0:T(8,128)} %get-tuple-element.26) | copy-start | bytes 12292
  26.7 19.3 %collective-permute-start.1 = (bf16[16,136,256]{2,1,0:T(8,128)(2,1)S(1)}, bf16[16,136,256]{2,1,0:T(8,128)(2,1)S(1)}, u32[]{:S(2)}, u32[]{:S(2)}) collective-permute-start(bf16[16,136,256]{2,1,0:T(8,128)(2,1)S(1)} %all_to_all.15.packed), channel_id=1, source_target_pairs={{0,1},{1,0},{2,3},{3,2},{4,5},{5,4},{6,7},{7,6},{8,9},{9,8},{10,11... | collective-permute-start | bytes 3342344 | tf_op jit(solution)/shard_map/ppermute | solution.py:313
  26.7 14.4 %collective-permute-start = (bf16[512,256]{1,0:T(8,128)(2,1)S(1)}, bf16[512,256]{1,0:T(8,128)(2,1)S(1)}, u32[]{:S(2)}, u32[]{:S(2)}) collective-permute-start(bf16[512,256]{1,0:T(8,128)(2,1)S(1)} %copy-done.1), channel_id=1, source_target_pairs={{0,0},{33,1},{10,2},{43,3},{60,4},{29,5},{22,6},{55,7},{8,8},{41,9... | collective-permute-start | bytes 786440 | tf_op jit(solution)/shard_map/ppermute | solution.py:307
  34.5 13.4 %collective-permute-start.6 = (f32[8,128]{1,0:T(8,128)S(1)}, f32[8,128]{1,0:T(8,128)S(1)}, u32[]{:S(2)}, u32[]{:S(2)}) collective-permute-start(f32[8,128]{1,0:T(8,128)S(1)} %copy-done), channel_id=1, source_target_pairs={{0,16},{8,24},{16,0},{24,8},{32,48},{40,56},{48,32},{56,40},{1,17}... | collective-permute-start | bytes 12296 | tf_op jit(solution)/shard_map/ppermute | solution.py:309
  34.6 13.3 %collective-permute-start.5 = (f32[8,128]{1,0:T(8,128)S(1)}, f32[8,128]{1,0:T(8,128)S(1)}, u32[]{:S(2)}, u32[]{:S(2)}) collective-permute-start(f32[8,128]{1,0:T(8,128)S(1)} %copy-done), channel_id=1, source_target_pairs={{0,48},{8,56},{16,32},{24,40},{32,16},{40,24},{48,0},{56,8},{1,49}... | collective-permute-start | bytes 12296 | tf_op jit(solution)/shard_map/ppermute | solution.py:309
  36.6 11.3 %collective-permute-start.4 = (f32[8,128]{1,0:T(8,128)S(1)}, f32[8,128]{1,0:T(8,128)S(1)}, u32[]{:S(2)}, u32[]{:S(2)}) collective-permute-start(f32[8,128]{1,0:T(8,128)S(1)} %copy-done), channel_id=1, source_target_pairs={{0,32},{8,40},{16,48},{24,56},{32,0},{40,8},{48,16},{56,24},{1,33}... | collective-permute-start | bytes 12296 | tf_op jit(solution)/shard_map/ppermute | solution.py:309
  42.8 10.1 %collective-permute-start.2 = (f32[24,128]{1,0:T(8,128)S(1)}, f32[24,128]{1,0:T(8,128)S(1)}, u32[]{:S(2)}, u32[]{:S(2)}) collective-permute-start(f32[24,128]{1,0:T(8,128)S(1)} %get-tuple-element.24.near), channel_id=1, source_target_pairs={{0,1},{1,0},{2,3},{3,2},{4,5},{5,4},{6,7},{7,6},{8,9},{9,8},{10,11... | collective-permute-start | bytes 36872 | tf_op jit(solution)/shard_map/ppermute | solution.py:316
  47.8 5.1 %collective-permute-start.3 = (f32[24,128]{1,0:T(8,128)S(1)}, f32[24,128]{1,0:T(8,128)S(1)}, u32[]{:S(2)}, u32[]{:S(2)}) collective-permute-start(f32[24,128]{1,0:T(8,128)S(1)} %get-tuple-element.25.far), channel_id=1, source_target_pairs={{0,1},{1,0},{2,3},{3,2},{4,5},{5,4},{6,7},{7,6},{8,9},{9,8},{10,11... | collective-permute-start | bytes 36872 | tf_op jit(solution)/shard_map/ppermute | solution.py:318
  47.9 1.4 %collective-permute-start.7 = (f32[8,128]{1,0:T(8,128)S(1)}, f32[8,128]{1,0:T(8,128)S(1)}, u32[]{:S(2)}, u32[]{:S(2)}) collective-permute-start(f32[8,128]{1,0:T(8,128)S(1)} %add_add_fusion), channel_id=1, source_target_pairs={{0,1},{1,0},{2,3},{3,2},{4,5},{5,4},{6,7},{7,6},{8,9},{9,8},{10,11... | collective-permute-start | bytes 12296 | tf_op jit(solution)/shard_map/ppermute | solution.py:311
  49.3 3.6 %collective-permute-start.8 = (f32[8,128]{1,0:T(8,128)S(1)}, f32[8,128]{1,0:T(8,128)S(1)}, u32[]{:S(2)}, u32[]{:S(2)}) collective-permute-start(f32[8,128]{1,0:T(8,128)S(1)} %add.15.count), channel_id=1, source_target_pairs={{0,8},{8,0},{16,24},{24,16},{32,40},{40,32},{48,56},{56,48},{1,9},... | collective-permute-start | bytes 12296 | tf_op jit(solution)/shard_map/ppermute | solution.py:312
  68.0 2.9 %collective-permute-start.9 = (bf16[16,256,128]{2,1,0:T(8,128)(2,1)S(1)}, bf16[16,256,128]{2,1,0:T(8,128)(2,1)S(1)}, u32[]{:S(2)}, u32[]{:S(2)}) collective-permute-start(bf16[16,256,128]{2,1,0:T(8,128)(2,1)S(1)} %get-tuple-element.34), channel_id=1, source_target_pairs={{0,1},{1,0},{2,3},{3,2},{4,5},{5,4},{6,7},{7,6},{8,9},{9,8},{10,11... | collective-permute-start | bytes 3145736 | tf_op jit(solution)/shard_map/ppermute | solution.py:337
  72.6 27.6 %all-to-all-start.2 = ((bf16[16,256,128]{2,1,0:T(8,128)(2,1)}), bf16[16,256,128]{2,1,0:T(8,128)(2,1)S(1)}, u32[]{:S(2)}, u32[]{:S(2)}) async-start(bf16[16,256,128]{2,1,0:T(8,128)(2,1)} %shard_map.73), calls=%async_computation.2 | async-start | bytes 2097152 | tf_op jit(solution)/shard_map/all_to_all | solution.py:52
  77.6 9.5 %collective-permute-start.10 = (bf16[520,256]{1,0:T(8,128)(2,1)S(1)}, bf16[520,256]{1,0:T(8,128)(2,1)S(1)}, u32[]{:S(2)}, u32[]{:S(2)}) collective-permute-start(bf16[520,256]{1,0:T(8,128)(2,1)S(1)} %get-tuple-element.35), channel_id=1, source_target_pairs={{0,0},{1,33},{2,10},{3,43},{4,60},{5,29},{6,22},{7,55},{8,8},{9,41... | collective-permute-start | bytes 798728 | tf_op jit(solution)/shard_map/ppermute | solution.py:344
  87.1 6.9 %collective-permute-start.11 = (bf16[264,256]{1,0:T(8,128)(2,1)S(1)}, bf16[264,256]{1,0:T(8,128)(2,1)S(1)}, u32[]{:S(2)}, u32[]{:S(2)}) collective-permute-start(bf16[264,256]{1,0:T(8,128)(2,1)S(1)} %slice.8), channel_id=1, source_target_pairs={{0,1},{1,0},{2,3},{3,2},{4,5},{5,4},{6,7},{7,6},{8,9},{9,8},{10,11... | collective-permute-start | bytes 405512 | tf_op jit(solution)/shard_map/ppermute | solution.py:349
  94.0 4.3 %collective-permute-start.12 = (bf16[72,256]{1,0:T(8,128)(2,1)S(1)}, bf16[72,256]{1,0:T(8,128)(2,1)S(1)}, u32[]{:S(2)}, u32[]{:S(2)}) collective-permute-start(bf16[72,256]{1,0:T(8,128)(2,1)S(1)} %get-tuple-element.37), channel_id=1, source_target_pairs={{0,2},{2,4},{4,6},{6,0},{1,3},{3,5},{5,7},{7,1},{8,10},{10,12},{12... | collective-permute-start | bytes 110600 | tf_op jit(solution)/shard_map/ppermute | solution.py:353
  94.7 5.5 %collective-permute-start.13 = (bf16[72,256]{1,0:T(8,128)(2,1)S(1)}, bf16[72,256]{1,0:T(8,128)(2,1)S(1)}, u32[]{:S(2)}, u32[]{:S(2)}) collective-permute-start(bf16[72,256]{1,0:T(8,128)(2,1)S(1)} %get-tuple-element.38), channel_id=1, source_target_pairs={{0,4},{2,6},{4,0},{6,2},{1,5},{3,7},{5,1},{7,3},{8,12},{10,14},{12... | collective-permute-start | bytes 110600 | tf_op jit(solution)/shard_map/ppermute | solution.py:353
  94.7 5.5 %collective-permute-start.14 = (bf16[72,256]{1,0:T(8,128)(2,1)S(1)}, bf16[72,256]{1,0:T(8,128)(2,1)S(1)}, u32[]{:S(2)}, u32[]{:S(2)}) collective-permute-start(bf16[72,256]{1,0:T(8,128)(2,1)S(1)} %get-tuple-element.39), channel_id=1, source_target_pairs={{0,6},{2,0},{4,2},{6,4},{1,7},{3,1},{5,3},{7,5},{8,14},{10,8},{12,... | collective-permute-start | bytes 110600 | tf_op jit(solution)/shard_map/ppermute | solution.py:353

commit v9 on v7

--- a/solution.py
+++ b/solution.py
@@ -10,7 +10,7 @@
 
 
 NCOH = 16
-PLANE = ("y", "x")
+PLANE = ("x", "y")
 COLUMN = ("z", "x", "c")
 ALL = ("y", "z", "x", "c")
 SHIFT = (0, 4, 1, 5, 7, 3, 2, 6)
@@ -169,7 +169,8 @@
         rest += stats[k, both:]
     lse = top + jnp.log(total)
     lse_out[...] = lse
-    per_cohort = scale / row_to_column(rest[1:2])
+    counts = row_to_column(rest[1:2])
+    per_cohort = jnp.where(counts > 0, scale / jnp.maximum(counts, F32(1)), F32(0))
     weight_out[...] = jnp.broadcast_to(per_cohort, weight_out.shape)
     weights = jnp.zeros((both, LANES), F32)
     cohorts = jnp.concatenate([coh_near[...], coh_far[...]], axis=0)
@@ -250,14 +251,34 @@
     write_digits(out, nx * height, loss[...])
 
 
-def users_near_kernel(kept, bank, far_part, user_part):
+def users_near_kernel(kept, bank, far_part, user_part, parts, sems):
     bank_t = bank[...].T
+    copies_out = []
     for step in range(kept.shape[0]):
         part = jnp.dot(bank_t, kept[step], preferred_element_type=F32)
         for s in range(STEP):
             mine = part[:, s * LANES : (s + 1) * LANES]
             at = step * STEP + s
-            user_part[at] = (mine + far_part[at].astype(F32)).astype(BF16)
+            parts[at] = (mine + far_part[at].astype(F32)).astype(BF16)
+        cut = pl.ds(step * STEP, STEP)
+        copies_out.append(pltpu.make_async_copy(parts.at[cut], user_part.at[cut], sems.at[step]))
+        copies_out[-1].start()
+    for copy in copies_out:
+        copy.wait()
+
+
+def users_near(kept, bank, far_part):
+    shape = bf16(*far_part.shape)
+    steps = kept.shape[0]
+    return pl.pallas_call(
+        users_near_kernel,
+        in_specs=[VMEM] * 3,
+        out_specs=pl.BlockSpec(memory_space=pltpu.HBM),
+        out_shape=shape,
+        scratch_shapes=[pltpu.VMEM(shape.shape, BF16), pltpu.SemaphoreType.DMA((steps,))],
+        compiler_params=pltpu.CompilerParams(vmem_limit_bytes=24 << 20),
+        name="users_near",
+    )(kept, bank, far_part)
 
 
 def halve_kernel(mine, theirs, *pieces):
@@ -341,7 +362,7 @@
         scratch=[pltpu.VMEM(bank.shape, F32)],
     )
     bank_part = lax.ppermute(bank_part, COLUMN, [(b, a) for a, b in fetch])
-    user_part = call(users_near_kernel, bf16(plane, width, rows), *(kept, item_block, far_part))
+    user_part = users_near(kept, item_block, far_part)
     user_part = exchange(user_part, PLANE)
     half = bank.shape[0] // nc
     height = half // nx

time: 104 us -> 104 us (level)
    pallas_call x9 -> x8, Pallas kernels: 11.8 us -> 10.1 us  [call(): pl.pallas_call(kernel, in_specs=[VMEM] * len(operands), out_specs=jax.tre...]
    pallas_call x0 -> x1, Pallas kernels: none -> 1.48 us  [users_near(): pl.pallas_call(users_near_kernel, in_specs=[VMEM] * 3, out_specs=pl.Block...]
where the time goes in v9:
time: 104 us; the launch traced here: 102 us
  blocking collectives  35.1 us (34%)
  starting transfers between devices  32 us (31%)
  waiting for transfers between devices  22.8 us (22%)
  Pallas kernels  11.6 us (11%)
    all_to_all x2, blocking collectives, exchange(): return lax.all_to_all(value, axis, split_axis=0, concat_axis=0, tiled=True)  35.1 us
    ppermute x4, waiting for transfers between devices, step(): other_count = lax.ppermute(count, axis, ways)  10.8 us
    pallas_call x8, Pallas kernels, call(): pl.pallas_call(kernel, in_specs=[VMEM] * len(operands), out_specs=jax.tre...  10.1 us
    ppermute x1, starting transfers between devices, step(): item_block = lax.ppermute(bank, COLUMN, fetch)  7.75 us
    ppermute x1, waiting for transfers between devices, step(): bank_part = lax.ppermute(bank_part, COLUMN, [(b, a) for a, b in fetch])  6.59 us
    all_to_all x1, starting transfers between devices, exchange(): return lax.all_to_all(value, axis, split_axis=0, concat_axis=0, tiled=True)  5.49 us
    ppermute x1, starting transfers between devices, step(): theirs = lax.ppermute(bank_part[:half + 8], 'c', cross)  5.23 us
    ppermute x3, starting transfers between devices, step(): lax.ppermute(pieces[r], 'x', [(k, (k + r) % nx) for k in range(nx)])  4.18 us
  transfers between devices with their start and end apart: 15, of which 7 were waited for; matrix products, arithmetic and copies ran while one was open for 0% of the time, Pallas kernels for 5%

profile of v9, /device:TPU:2, one launch (start us, length us, event | category | flops | bytes accessed | tf_op | source)
XLA Modules:
  0.0 102.3 jit_solution(12256924755515161275)
XLA Ops:
  0.6 2.0 %shard_map.67 = (bf16[16,136,256]{2,1,0:T(8,128)(2,1)}, f32[8,128]{1,0:T(8,128)}) custom-call(bf16[128,256]{1,0:T(8,128)(2,1)} %users.1, s32[1,128]{1,0:T(1,128)} %bitcast.4, s32[1,128]{1,0:T(1,128)} %bitcast.5), custom_call_target="tpu_custom_call" | custom-call | tf_op jit(solution)/shard_map/pallas_call | solution.py:26
  2.6 24.2 %all_to_all.15.packed = bf16[16,136,256]{2,1,0:T(8,128)(2,1)S(1)} all-to-all(bf16[16,136,256]{2,1,0:T(8,128)(2,1)} %get-tuple-element.23), channel_id=1, replica_groups=mesh['y'=4,'z'=8,'x'=4,'c'=2] {'x','y'}, dimensions={0} | all-to-all | bytes 2228224 | tf_op jit(solution)/shard_map/all_to_all | solution.py:52
  26.8 7.8 %collective-permute-start = (bf16[512,256]{1,0:T(8,128)(2,1)S(1)}, bf16[512,256]{1,0:T(8,128)(2,1)S(1)}, u32[]{:S(2)}, u32[]{:S(2)}) collective-permute-start(bf16[512,256]{1,0:T(8,128)(2,1)S(1)} %copy-done.1), channel_id=1, source_target_pairs={{0,0},{33,1},{10,2},{43,3},{60,4},{29,5},{22,6},{55,7},{8,8},{41,9... | collective-permute-start | bytes 786440 | tf_op jit(solution)/shard_map/ppermute | solution.py:327
  34.5 1.5 %collective-permute-start.4 = (f32[8,128]{1,0:T(8,128)S(1)}, f32[8,128]{1,0:T(8,128)S(1)}, u32[]{:S(2)}, u32[]{:S(2)}) collective-permute-start(f32[8,128]{1,0:T(8,128)S(1)} %copy-done), channel_id=1, source_target_pairs={{0,32},{8,40},{16,48},{24,56},{32,0},{40,8},{48,16},{56,24},{1,33}... | collective-permute-start | bytes 12296 | tf_op jit(solution)/shard_map/ppermute | solution.py:330
  36.1 6.4 %collective-permute-done.4 = f32[8,128]{1,0:T(8,128)S(1)} collective-permute-done((f32[8,128]{1,0:T(8,128)S(1)}, f32[8,128]{1,0:T(8,128)S(1)}, u32[]{:S(2)}, u32[]{:S(2)}) %collective-permute-start.4) | collective-permute-done | bytes 4128 | tf_op jit(solution)/shard_map/ppermute | solution.py:330
  42.4 0.9 collective-permute-start.5
  43.3 1.7 %shard_map.68 = (f32[24,128]{1,0:T(8,128)S(1)}, f32[16,128]{1,0:T(8,128)S(1)}) custom-call(bf16[16,136,256]{2,1,0:T(8,128)(2,1)S(1)} %all_to_all.15.packed, bf16[512,256]{1,0:T(8,128)(2,1)S(1)} %collective-permute-done.bank), custom_call_target="tpu_custom_call" | custom-call | tf_op jit(solution)/shard_map/pallas_call | solution.py:26
  45.1 3.2 %collective-permute-start.2 = (f32[24,128]{1,0:T(8,128)S(1)}, f32[24,128]{1,0:T(8,128)S(1)}, u32[]{:S(2)}, u32[]{:S(2)}) collective-permute-start(f32[24,128]{1,0:T(8,128)S(1)} %get-tuple-element.24.near), channel_id=1, source_target_pairs={{0,1},{1,0},{2,3},{3,2},{4,5},{5,4},{6,7},{7,6},{8,9},{9,8},{10,11... | collective-permute-start | bytes 36872 | tf_op jit(solution)/shard_map/ppermute | solution.py:336
  48.3 1.7 %shard_map.69 = (f32[24,128]{1,0:T(8,128)S(1)}, f32[16,128]{1,0:T(8,128)S(1)}) custom-call(bf16[16,136,256]{2,1,0:T(8,128)(2,1)S(1)} %collective-permute-done.1.packed, bf16[512,256]{1,0:T(8,128)(2,1)S(1)} %collective-permute-done.bank), custom_call_target="tpu_custom_call" | custom-call | tf_op jit(solution)/shard_map/pallas_call | solution.py:26
  51.4 3.6 %collective-permute-done.7.other_count = f32[8,128]{1,0:T(8,128)S(1)} collective-permute-done((f32[8,128]{1,0:T(8,128)S(1)}, f32[8,128]{1,0:T(8,128)S(1)}, u32[]{:S(2)}, u32[]{:S(2)}) %collective-permute-start.7) | collective-permute-done | bytes 4128 | tf_op jit(solution)/shard_map/ppermute | solution.py:330
  55.1 11.0 %all_to_all.16.stats = f32[16,40,128]{2,1,0:T(8,128)S(1)} all-to-all(f32[16,40,128]{2,1,0:T(8,128)S(1)} %shard_map.70), channel_id=1, replica_groups=mesh['y'=4,'z'=8,'x'=4,'c'=2] {'x','y'}, dimensions={0} | all-to-all | bytes 655360 | tf_op jit(solution)/shard_map/all_to_all | solution.py:52
  66.0 2.2 %shard_map.71 = (bf16[16,256,128]{2,1,0:T(8,128)(2,1)S(1)}, f32[512,256]{1,0:T(8,128)S(1)}, f32[32,128]{1,0:T(8,128)S(1)}, f32[16,128]{1,0:T(8,128)S(1)}, f32[8,128]{1,0:T(8,128)S(1)}) custom-call(bf16[16,136,256]{2,1,0:T(8,128)(2,1)S(1)} %collective-permute-done.1.packed, bf16[512,256]{1,0:T(8,128)(2,1)S(1)} %collective-permute-done.bank, ...), custom_call_target="tpu_custom_call" | custom-call | tf_op jit(solution)/shard_map/pallas_call | solution.py:26
  68.6 1.5 %shard_map.72 = (bf16[4,512,512]{2,1,0:T(8,128)(2,1)S(1)}, bf16[520,256]{1,0:T(8,128)(2,1)S(1)}) custom-call(bf16[16,136,256]{2,1,0:T(8,128)(2,1)S(1)} %all_to_all.15.packed, bf16[512,256]{1,0:T(8,128)(2,1)S(1)} %collective-permute-done.bank, f32[32,128]{1,0:T(8,128)S(1)} %get-tuple-element.29.lse, f32[16,128]{1,0:T(8,128)S(1)} %get-tuple-element.30.weight, ...), custom_call_target="tpu_custom_call" | custom-call | tf_op jit(solution)/shard_map/pallas_call | solution.py:26
  70.1 1.1 %collective-permute-done.8.far_part = bf16[16,256,128]{2,1,0:T(8,128)(2,1)S(1)} collective-permute-done((bf16[16,256,128]{2,1,0:T(8,128)(2,1)S(1)}, bf16[16,256,128]{2,1,0:T(8,128)(2,1)S(1)}, u32[]{:S(2)}, u32[]{:S(2)}) %collective-permute-start.8) | collective-permute-done | bytes 1048608 | tf_op jit(solution)/shard_map/ppermute | solution.py:357
  71.2 1.5 %users_near.1 = bf16[16,256,128]{2,1,0:T(8,128)(2,1)} custom-call(bf16[4,512,512]{2,1,0:T(8,128)(2,1)S(1)} %get-tuple-element.33.kept, bf16[512,256]{1,0:T(8,128)(2,1)S(1)} %collective-permute-done.bank, bf16[16,256,128]{2,1,0:T(8,128)(2,1)S(1)} %collective-permute-done.8.far_part), custom_call_target="tpu_custom_call" | custom-call | tf_op jit(solution)/shard_map/users_near/pallas_call | solution.py:273
  72.7 5.5 %all-to-all-start.2 = ((bf16[16,256,128]{2,1,0:T(8,128)(2,1)}), bf16[16,256,128]{2,1,0:T(8,128)(2,1)S(1)}, u32[]{:S(2)}, u32[]{:S(2)}) async-start(bf16[16,256,128]{2,1,0:T(8,128)(2,1)} %users_near.1), calls=%async_computation.2 | async-start | bytes 2097152 | tf_op jit(solution)/shard_map/all_to_all | solution.py:52
  78.2 2.9 %collective-permute-start.9 = (bf16[520,256]{1,0:T(8,128)(2,1)S(1)}, bf16[520,256]{1,0:T(8,128)(2,1)S(1)}, u32[]{:S(2)}, u32[]{:S(2)}) collective-permute-start(bf16[520,256]{1,0:T(8,128)(2,1)S(1)} %get-tuple-element.35), channel_id=1, source_target_pairs={{0,0},{1,33},{2,10},{3,43},{4,60},{5,29},{6,22},{7,55},{8,8},{9,41... | collective-permute-start | bytes 798728 | tf_op jit(solution)/shard_map/ppermute | solution.py:364
  81.1 6.6 %collective-permute-done.9.mine = bf16[520,256]{1,0:T(8,128)(2,1)S(1)} collective-permute-done((bf16[520,256]{1,0:T(8,128)(2,1)S(1)}, bf16[520,256]{1,0:T(8,128)(2,1)S(1)}, u32[]{:S(2)}, u32[]{:S(2)}) %collective-permute-start.9) | collective-permute-done | bytes 266272 | tf_op jit(solution)/shard_map/ppermute | solution.py:364
  87.7 5.2 %collective-permute-start.10 = (bf16[264,256]{1,0:T(8,128)(2,1)S(1)}, bf16[264,256]{1,0:T(8,128)(2,1)S(1)}, u32[]{:S(2)}, u32[]{:S(2)}) collective-permute-start(bf16[264,256]{1,0:T(8,128)(2,1)S(1)} %slice.8), channel_id=1, source_target_pairs={{0,1},{1,0},{2,3},{3,2},{4,5},{5,4},{6,7},{7,6},{8,9},{9,8},{10,11... | collective-permute-start | bytes 405512 | tf_op jit(solution)/shard_map/ppermute | solution.py:369
  92.9 1.0 collective-permute-done.10.theirs
  94.0 2.0 %collective-permute-start.11 = (bf16[72,256]{1,0:T(8,128)(2,1)S(1)}, bf16[72,256]{1,0:T(8,128)(2,1)S(1)}, u32[]{:S(2)}, u32[]{:S(2)}) collective-permute-start(bf16[72,256]{1,0:T(8,128)(2,1)S(1)} %get-tuple-element.37), channel_id=1, source_target_pairs={{0,2},{2,4},{4,6},{6,0},{1,3},{3,5},{5,7},{7,1},{8,10},{10,12},{12... | collective-permute-start | bytes 110600 | tf_op jit(solution)/shard_map/ppermute | solution.py:373
  96.0 2.2 %collective-permute-start.13 = (bf16[72,256]{1,0:T(8,128)(2,1)S(1)}, bf16[72,256]{1,0:T(8,128)(2,1)S(1)}, u32[]{:S(2)}, u32[]{:S(2)}) collective-permute-start(bf16[72,256]{1,0:T(8,128)(2,1)S(1)} %get-tuple-element.39), channel_id=1, source_target_pairs={{0,6},{2,0},{4,2},{6,4},{1,7},{3,1},{5,3},{7,5},{8,14},{10,8},{12,... | collective-permute-start | bytes 110600 | tf_op jit(solution)/shard_map/ppermute | solution.py:373
  98.2 3.3 %collective-permute-done.12.refs_2_ = bf16[72,256]{1,0:T(8,128)(2,1)S(1)} collective-permute-done((bf16[72,256]{1,0:T(8,128)(2,1)S(1)}, bf16[72,256]{1,0:T(8,128)(2,1)S(1)}, u32[]{:S(2)}, u32[]{:S(2)}) %collective-permute-start.12) | collective-permute-done | bytes 36896 | tf_op jit(solution)/shard_map/ppermute | solution.py:373
  101.5 0.9 shard_map.74
  (25 shorter events, 1.8 us)
Async XLA Ops:
  2.6 24.2 %copy-start.1 = (bf16[512,256]{1,0:T(8,128)(2,1)S(1)}, bf16[512,256]{1,0:T(8,128)(2,1)}, u32[]{:S(2)}) copy-start(bf16[512,256]{1,0:T(8,128)(2,1)} %param.5) | copy-start | bytes 786436
  2.6 31.9 %copy-start = (f32[8,128]{1,0:T(8,128)S(1)}, f32[8,128]{1,0:T(8,128)}, u32[]{:S(2)}) copy-start(f32[8,128]{1,0:T(8,128)} %get-tuple-element.26) | copy-start | bytes 12292
  26.8 21.5 %collective-permute-start.1 = (bf16[16,136,256]{2,1,0:T(8,128)(2,1)S(1)}, bf16[16,136,256]{2,1,0:T(8,128)(2,1)S(1)}, u32[]{:S(2)}, u32[]{:S(2)}) collective-permute-start(bf16[16,136,256]{2,1,0:T(8,128)(2,1)S(1)} %all_to_all.15.packed), channel_id=1, source_target_pairs={{0,1},{1,0},{2,3},{3,2},{4,5},{5,4},{6,7},{7,6},{8,9},{9,8},{10,11... | collective-permute-start | bytes 3342344 | tf_op jit(solution)/shard_map/ppermute | solution.py:333
  26.8 16.5 %collective-permute-start = (bf16[512,256]{1,0:T(8,128)(2,1)S(1)}, bf16[512,256]{1,0:T(8,128)(2,1)S(1)}, u32[]{:S(2)}, u32[]{:S(2)}) collective-permute-start(bf16[512,256]{1,0:T(8,128)(2,1)S(1)} %copy-done.1), channel_id=1, source_target_pairs={{0,0},{33,1},{10,2},{43,3},{60,4},{29,5},{22,6},{55,7},{8,8},{41,9... | collective-permute-start | bytes 786440 | tf_op jit(solution)/shard_map/ppermute | solution.py:327
  34.5 7.9 %collective-permute-start.4 = (f32[8,128]{1,0:T(8,128)S(1)}, f32[8,128]{1,0:T(8,128)S(1)}, u32[]{:S(2)}, u32[]{:S(2)}) collective-permute-start(f32[8,128]{1,0:T(8,128)S(1)} %copy-done), channel_id=1, source_target_pairs={{0,32},{8,40},{16,48},{24,56},{32,0},{40,8},{48,16},{56,24},{1,33}... | collective-permute-start | bytes 12296 | tf_op jit(solution)/shard_map/ppermute | solution.py:330
  42.4 7.7 %collective-permute-start.5 = (f32[8,128]{1,0:T(8,128)S(1)}, f32[8,128]{1,0:T(8,128)S(1)}, u32[]{:S(2)}, u32[]{:S(2)}) collective-permute-start(f32[8,128]{1,0:T(8,128)S(1)} %add.9), channel_id=1, source_target_pairs={{0,16},{8,24},{16,0},{24,8},{32,48},{40,56},{48,32},{56,40},{1,17}... | collective-permute-start | bytes 12296 | tf_op jit(solution)/shard_map/ppermute | solution.py:330
  45.1 10.0 %collective-permute-start.2 = (f32[24,128]{1,0:T(8,128)S(1)}, f32[24,128]{1,0:T(8,128)S(1)}, u32[]{:S(2)}, u32[]{:S(2)}) collective-permute-start(f32[24,128]{1,0:T(8,128)S(1)} %get-tuple-element.24.near), channel_id=1, source_target_pairs={{0,1},{1,0},{2,3},{3,2},{4,5},{5,4},{6,7},{7,6},{8,9},{9,8},{10,11... | collective-permute-start | bytes 36872 | tf_op jit(solution)/shard_map/ppermute | solution.py:336
  50.0 5.0 %collective-permute-start.3 = (f32[24,128]{1,0:T(8,128)S(1)}, f32[24,128]{1,0:T(8,128)S(1)}, u32[]{:S(2)}, u32[]{:S(2)}) collective-permute-start(f32[24,128]{1,0:T(8,128)S(1)} %get-tuple-element.25.far), channel_id=1, source_target_pairs={{0,1},{1,0},{2,3},{3,2},{4,5},{5,4},{6,7},{7,6},{8,9},{9,8},{10,11... | collective-permute-start | bytes 36872 | tf_op jit(solution)/shard_map/ppermute | solution.py:338
  50.1 1.3 %collective-permute-start.6 = (f32[8,128]{1,0:T(8,128)S(1)}, f32[8,128]{1,0:T(8,128)S(1)}, u32[]{:S(2)}, u32[]{:S(2)}) collective-permute-start(f32[8,128]{1,0:T(8,128)S(1)} %add.10), channel_id=1, source_target_pairs={{0,1},{1,0},{2,3},{3,2},{4,5},{5,4},{6,7},{7,6},{8,9},{9,8},{10,11... | collective-permute-start | bytes 12296 | tf_op jit(solution)/shard_map/ppermute | solution.py:330
  51.4 3.6 %collective-permute-start.7 = (f32[8,128]{1,0:T(8,128)S(1)}, f32[8,128]{1,0:T(8,128)S(1)}, u32[]{:S(2)}, u32[]{:S(2)}) collective-permute-start(f32[8,128]{1,0:T(8,128)S(1)} %add.11.count), channel_id=1, source_target_pairs={{0,8},{8,0},{16,24},{24,16},{32,40},{40,32},{48,56},{56,48},{1,9},... | collective-permute-start | bytes 12296 | tf_op jit(solution)/shard_map/ppermute | solution.py:330
  68.3 2.9 %collective-permute-start.8 = (bf16[16,256,128]{2,1,0:T(8,128)(2,1)S(1)}, bf16[16,256,128]{2,1,0:T(8,128)(2,1)S(1)}, u32[]{:S(2)}, u32[]{:S(2)}) collective-permute-start(bf16[16,256,128]{2,1,0:T(8,128)(2,1)S(1)} %get-tuple-element.34), channel_id=1, source_target_pairs={{0,1},{1,0},{2,3},{3,2},{4,5},{5,4},{6,7},{7,6},{8,9},{9,8},{10,11... | collective-permute-start | bytes 3145736 | tf_op jit(solution)/shard_map/ppermute | solution.py:357
  72.7 28.8 %all-to-all-start.2 = ((bf16[16,256,128]{2,1,0:T(8,128)(2,1)}), bf16[16,256,128]{2,1,0:T(8,128)(2,1)S(1)}, u32[]{:S(2)}, u32[]{:S(2)}) async-start(bf16[16,256,128]{2,1,0:T(8,128)(2,1)} %users_near.1), calls=%async_computation.2 | async-start | bytes 2097152 | tf_op jit(solution)/shard_map/all_to_all | solution.py:52
  78.2 9.5 %collective-permute-start.9 = (bf16[520,256]{1,0:T(8,128)(2,1)S(1)}, bf16[520,256]{1,0:T(8,128)(2,1)S(1)}, u32[]{:S(2)}, u32[]{:S(2)}) collective-permute-start(bf16[520,256]{1,0:T(8,128)(2,1)S(1)} %get-tuple-element.35), channel_id=1, source_target_pairs={{0,0},{1,33},{2,10},{3,43},{4,60},{5,29},{6,22},{7,55},{8,8},{9,41... | collective-permute-start | bytes 798728 | tf_op jit(solution)/shard_map/ppermute | solution.py:364
  87.7 6.2 %collective-permute-start.10 = (bf16[264,256]{1,0:T(8,128)(2,1)S(1)}, bf16[264,256]{1,0:T(8,128)(2,1)S(1)}, u32[]{:S(2)}, u32[]{:S(2)}) collective-permute-start(bf16[264,256]{1,0:T(8,128)(2,1)S(1)} %slice.8), channel_id=1, source_target_pairs={{0,1},{1,0},{2,3},{3,2},{4,5},{5,4},{6,7},{7,6},{8,9},{9,8},{10,11... | collective-permute-start | bytes 405512 | tf_op jit(solution)/shard_map/ppermute | solution.py:369
  94.0 4.2 %collective-permute-start.11 = (bf16[72,256]{1,0:T(8,128)(2,1)S(1)}, bf16[72,256]{1,0:T(8,128)(2,1)S(1)}, u32[]{:S(2)}, u32[]{:S(2)}) collective-permute-start(bf16[72,256]{1,0:T(8,128)(2,1)S(1)} %get-tuple-element.37), channel_id=1, source_target_pairs={{0,2},{2,4},{4,6},{6,0},{1,3},{3,5},{5,7},{7,1},{8,10},{10,12},{12... | collective-permute-start | bytes 110600 | tf_op jit(solution)/shard_map/ppermute | solution.py:373
  96.0 5.5 %collective-permute-start.12 = (bf16[72,256]{1,0:T(8,128)(2,1)S(1)}, bf16[72,256]{1,0:T(8,128)(2,1)S(1)}, u32[]{:S(2)}, u32[]{:S(2)}) collective-permute-start(bf16[72,256]{1,0:T(8,128)(2,1)S(1)} %get-tuple-element.38), channel_id=1, source_target_pairs={{0,4},{2,6},{4,0},{6,2},{1,5},{3,7},{5,1},{7,3},{8,12},{10,14},{12... | collective-permute-start | bytes 110600 | tf_op jit(solution)/shard_map/ppermute | solution.py:373
  96.0 5.5 %collective-permute-start.13 = (bf16[72,256]{1,0:T(8,128)(2,1)S(1)}, bf16[72,256]{1,0:T(8,128)(2,1)S(1)}, u32[]{:S(2)}, u32[]{:S(2)}) collective-permute-start(bf16[72,256]{1,0:T(8,128)(2,1)S(1)} %get-tuple-element.39), channel_id=1, source_target_pairs={{0,6},{2,0},{4,2},{6,4},{1,7},{3,1},{5,3},{7,5},{8,14},{10,8},{12,... | collective-permute-start | bytes 110600 | tf_op jit(solution)/shard_map/ppermute | solution.py:373
